TPU v7x, 32 devices: a whole 2x2x4 slice. The times are simulated.
32 devices in a mesh: parts: 2 (over x), row: 8 (over z, y), col: 2 (over core).
Axes of the slice: x: 2, y: 2, z: 4, core: 2. Of those that a mesh axis runs over, the one named last changes fastest.
Arguments:
- tokens: bfloat16 [64, 512, 512], P(('parts', 'row'), 'col'), parts along dimension 0, may hold values from -6 to 6
- expand_weight: bfloat16 [512, 2048], replicated, may hold values from -0.25 to 0.25
- depth_kernel: float32 [3, 3, 2048], replicated, may hold values from -2 to 2
- project_weight: bfloat16 [2048, 512], replicated, may hold values from -0.125 to 0.125
- norm_gain: float32 [512], replicated, may hold values from 0.25 to 1.75
- attend_weight: bfloat16 [512, 1536], replicated, may hold values from -3 to 3
- output_weight: bfloat16 [512, 512], replicated, may hold values from -0.25 to 0.25
Outputs:
- section_out: bfloat16 [64, 512, 512], P(('parts', 'row'), 'col'), parts along dimension 0
There are 2 independent parts, one for each index of `parts`. A program takes and returns all parts, laid end to end along the dimension named above; an argument that names none is the same for every part. Nothing has to cross between parts.
All inputs are finite; a program needn't handle non-finite values.
Results may differ from a plain program's by a relative error of at most 0.012.
Values may be sent and summed in bfloat16 or wider, within the bound.
No kernel may reach another device: no remote copies, remote signals or barrier semaphores. Data moves between devices by JAX's collectives and lax.ppermute only.
A program may use at most 128 MiB of HBM per device.

v0:
```python
import math

import jax
import jax.numpy as jnp
from jax import lax
from jax.sharding import PartitionSpec as P

HEADS = 16
HEAD_DIM = 32
GRID = 16


def extended(cells, sides, width):
    for axis, dim in sides:
        count = lax.axis_size(axis)
        ends = count - 1
        head = lax.slice_in_dim(cells, 0, width, axis=dim)
        tail = lax.slice_in_dim(cells, cells.shape[dim] - width, cells.shape[dim], axis=dim)
        cells = jnp.concatenate(
            [
                lax.ppermute(tail, axis, [(i, (i + 1) % count) for i in range(ends)]),
                cells,
                lax.ppermute(head, axis, [((i + 1) % count, i) for i in range(ends)]),
            ],
            axis=dim,
        )
    return cells


def gelu_tanh(values):
    return jax.nn.gelu(values, approximate=True)


def expand_tile(inputs, expand_weight):
    shape = inputs.shape
    product = jnp.dot(
        inputs.reshape(-1, shape[2]), expand_weight, preferred_element_type=jnp.float32
    )
    return gelu_tanh(product).astype(jnp.bfloat16).reshape(shape[0], shape[1], -1)


def layer_norm(values, gain):
    values = values.astype(jnp.float32)
    center = jnp.mean(values, axis=-1, keepdims=True)
    spread = jnp.mean((values - center) ** 2, axis=-1, keepdims=True)
    return ((values - center) * lax.rsqrt(spread + 1e-05) * gain).astype(jnp.bfloat16)


def attend_groups(groups, attend_weight, output_weight):
    count, members, channels = groups.shape
    projected = jnp.dot(
        groups.reshape(count * members, channels), attend_weight, preferred_element_type=jnp.float32
    )
    projected = projected.astype(jnp.bfloat16).reshape(count, members, 3, HEADS, HEAD_DIM)
    query_heads = projected[:, :, 0]
    key_heads = projected[:, :, 1]
    value_heads = projected[:, :, 2]
    scores = jnp.einsum(
        "nqhd,nkhd->nhqk", query_heads, key_heads, preferred_element_type=jnp.float32
    ) / math.sqrt(HEAD_DIM)
    soft = jax.nn.softmax(scores, axis=-1).astype(jnp.bfloat16)
    heads_out = jnp.einsum("nhqk,nkhd->nqhd", soft, value_heads, preferred_element_type=jnp.float32)
    heads_out = heads_out.astype(jnp.bfloat16).reshape(count * members, channels)
    result = jnp.dot(heads_out, output_weight, preferred_element_type=jnp.float32).astype(
        jnp.bfloat16
    )
    return result.reshape(count, members, channels)


def local(
    tokens, expand_weight, depth_kernel, project_weight, norm_gain, attend_weight, output_weight
):
    tile_rows, tile_cols, channels = tokens.shape
    padded_in = extended(tokens, (("row", 0), ("col", 1)), 1)
    expanded = expand_tile(padded_in, expand_weight)
    total = jnp.zeros((tile_rows, tile_cols, expanded.shape[2]), jnp.float32)
    for shift_row in range(3):
        for shift_col in range(3):
            total = (
                total
                + expanded[
                    shift_row : shift_row + tile_rows, shift_col : shift_col + tile_cols
                ].astype(jnp.float32)
                * depth_kernel[shift_row, shift_col]
            )
    depth = gelu_tanh(total).astype(jnp.bfloat16)
    branch = jnp.dot(
        depth.reshape(tile_rows * tile_cols, -1), project_weight, preferred_element_type=jnp.float32
    )
    mbconv = (tokens.astype(jnp.float32) + branch.reshape(tile_rows, tile_cols, channels)).astype(
        jnp.bfloat16
    )
    normed = layer_norm(mbconv, norm_gain)
    row_count = lax.axis_size("row")
    col_count = lax.axis_size("col")
    devices = row_count * col_count
    stride_rows = tile_rows * row_count // GRID
    stride_cols = tile_cols * col_count // GRID
    col_blocks = tile_cols // stride_cols
    if row_count % GRID == 0:
        spread_count = stride_rows // tile_rows
        per_dest = tile_rows * stride_cols // devices
        ordered = normed.reshape(tile_rows, col_blocks, stride_cols, channels).transpose(0, 2, 1, 3)
        ordered = ordered.reshape(devices, per_dest, col_blocks, channels)
    else:
        spread_count = 1
        row_blocks = tile_rows // stride_rows
        ordered = normed.reshape(
            row_blocks, stride_rows, col_blocks, stride_cols, channels
        ).transpose(1, 3, 0, 2, 4)
        ordered = ordered.reshape(devices, -1, row_blocks * col_blocks, channels)
    piece = lax.all_to_all(ordered, ("row", "col"), split_axis=0, concat_axis=0, tiled=True)
    items = piece.shape[1]
    per_source = piece.shape[2]
    grouped = piece.reshape(
        row_count // spread_count, spread_count, col_count, items, per_source, channels
    )
    grouped = grouped.transpose(3, 1, 0, 2, 4, 5).reshape(items * spread_count, -1, channels)
    result = attend_groups(grouped, attend_weight, output_weight)
    result = result.reshape(
        items, spread_count, row_count // spread_count, col_count, per_source, channels
    )
    returned = lax.all_to_all(
        result.transpose(2, 1, 3, 0, 4, 5).reshape(devices, items, per_source, channels),
        ("row", "col"),
        split_axis=0,
        concat_axis=0,
        tiled=True,
    )
    if row_count % GRID == 0:
        attention = returned.reshape(tile_rows, stride_cols, col_blocks, channels).transpose(
            0, 2, 1, 3
        )
    else:
        row_blocks = tile_rows // stride_rows
        attention = returned.reshape(
            stride_rows, stride_cols, row_blocks, col_blocks, channels
        ).transpose(2, 0, 3, 1, 4)
    attention = attention.reshape(tile_rows, tile_cols, channels)
    return (mbconv.astype(jnp.float32) + attention.astype(jnp.float32)).astype(jnp.bfloat16)


def solution(mesh):
    placed = (P(("parts", "row"), "col", None), P(), P(), P(), P(), P(), P())
    return jax.shard_map(
        local,
        mesh=mesh,
        in_specs=placed,
        out_specs=P(("parts", "row"), "col", None),
        check_vma=False,
    )
```

profile of v0, /device:TPU:0, one launch (start us, length us, event | category | flops | bytes accessed | tf_op | source)
XLA Modules:
  0.0 168.5 jit_solution(11963751496534343237)
XLA Ops:
  0.0 1.2 fusion.47
  1.2 4.9 %collective-permute-start = (bf16[1,256,512]{2,1,0:T(8,128)(2,1)S(1)}, bf16[1,256,512]{2,1,0:T(8,128)(2,1)S(1)}, u32[]{:S(2)}, u32[]{:S(2)}) collective-permute-start(bf16[1,256,512]{2,1,0:T(8,128)(2,1)S(1)} %get-tuple-element.11), channel_id=1, source_target_pairs={{0,2},{2,4},{4,6},{6,8},{8,10},{10,12},{12,14},{1,3},{3,5},{5,7},{... | collective-permute-start | bytes 786440 | tf_op jit(solution)/shard_map/ppermute | solution.py:21
  6.1 1.3 collective-permute-start.1
  7.4 9.8 %collective-permute-done = bf16[1,256,512]{2,1,0:T(8,128)(2,1)S(1)} collective-permute-done((bf16[1,256,512]{2,1,0:T(8,128)(2,1)S(1)}, bf16[1,256,512]{2,1,0:T(8,128)(2,1)S(1)}, u32[]{:S(2)}, u32[]{:S(2)}) %collective-permute-start) | collective-permute-done | bytes 262176 | tf_op jit(solution)/shard_map/ppermute | solution.py:21
  17.3 1.3 constant_dynamic-update-slice_fusion.1
  18.7 1.3 collective-permute-start.2
  20.0 1.3 collective-permute-start.3
  21.3 1.1 fusion.48
  23.1 1.6 pad_maximum_fusion
  24.6 2.7 %reshape.49 = bf16[1548,512]{1,0:T(8,128)(2,1)} reshape(bf16[6,258,512]{2,1,0:T(8,128)(2,1)} %pad_maximum_fusion) | data formatting | bytes 3170304 | tf_op jit(solution)/shard_map/reshape | solution.py:37
  27.3 8.9 %fusion.11 = bf16[1548,2048]{1,0:T(8,128)(2,1)} fusion(bf16[1548,512]{1,0:T(8,128)(2,1)} %reshape.49, bf16[512,2048]{1,0:T(8,128)(2,1)S(1)} %copy-done), kind=kOutput, calls=%fused_computation.13 | convolution fusion | flops 3274924032 | bytes 10022912 | tf_op jit(solution)/shard_map/dot_general | solution.py:36
  36.3 8.8 %reshape.50 = bf16[6,258,2048]{2,1,0:T(8,128)(2,1)} reshape(bf16[1548,2048]{1,0:T(8,128)(2,1)} %fusion.11) | data formatting | bytes 12681216 | tf_op jit(solution)/shard_map/reshape | solution.py:39
  45.0 26.2 %convert_reduce_fusion = (f32[4,256]{1,0:T(4,128)S(1)}, bf16[4,256,512]{2,1,0:T(8,128)(2,1)S(1)}) fusion(bf16[2048,512]{1,0:T(8,128)(2,1)} %param.10, bf16[6,258,2048]{2,1,0:T(8,128)(2,1)} %reshape.50, f32[2048]{0:T(1024)S(1)} %bitcast.90, f32[2048]{0:T(1024)S(1)} %bitcast.91, f32[2048]{0:T(1024)S(1)} %bitcast.84, f32[2048]{0:T(1024)S(1)} %bitcast.85, ...), kind=kOutput, calls=%fused_computation.30 | convolution fusion | flops 2223504384 | bytes 42020864 | tf_op jit(solution)/shard_map/dot_general | solution.py:87
  73.3 30.6 %all_to_all.10 = bf16[16,4,16,512]{3,2,1,0:T(8,128)(2,1)S(1)} all-to-all(bf16[16,4,16,512]{3,2,1,0:T(8,128)(2,1)S(1)} %bitcast.76), channel_id=1, replica_groups=mesh['parts'=2,'row'=8,'col'=2] {'row','col'}, dimensions={0} | all-to-all | bytes 2097152 | tf_op jit(solution)/shard_map/all_to_all | solution.py:112
  104.0 1.8 %convolution_convert_fusion = bf16[1024,1536]{1,0:T(8,128)(2,1)S(1)} fusion(bf16[1024,512]{1,0:T(8,128)(2,1)S(1)} %bitcast.80, bf16[512,1536]{1,0:T(8,128)(2,1)S(1)} %copy-done.7), kind=kOutput, calls=%fused_computation.27 | convolution fusion | flops 1612185600 | bytes 5767168 | tf_op jit(solution)/shard_map/dot_general | solution.py:51
  105.8 2.9 %copy.14 = bf16[1024,1536]{0,1:T(8,128)(2,1)} copy(bf16[1024,1536]{1,0:T(8,128)(2,1)S(1)} %convolution_convert_fusion) | data formatting | bytes 6291456 | tf_op jit(solution)/shard_map/convert_element_type | solution.py:54
  108.7 4.8 %reshape.54 = bf16[4,256,3,16,32]{1,0,4,3,2:T(4,128)(2,1)S(1)} reshape(bf16[1024,1536]{0,1:T(8,128)(2,1)} %copy.14) | data formatting | bytes 6291456 | tf_op jit(solution)/shard_map/reshape | solution.py:54
  113.5 2.6 %fusion.45 = (bf16[4,256,1,16,32]{1,0,4,3,2:T(4,128)(2,1)}, bf16[4,256,1,16,32]{1,0,4,3,2:T(4,128)(2,1)}, bf16[4,256,1,16,32]{1,0,4,3,2:T(4,128)(2,1)}) fusion(bf16[4,256,3,16,32]{1,0,4,3,2:T(4,128)(2,1)S(1)} %reshape.54), kind=kLoop, calls=%fused_computation.58 | loop fusion | bytes 6291456 | tf_op jit(solution)/shard_map/slice | solution.py:57
  116.1 10.4 %fusion.49 = (f32[4,16,256]{2,1,0:T(8,128)S(1)}, f32[4,16,256,256]{2,3,1,0:T(8,128)}) fusion(bf16[4,256,1,16,32]{1,0,4,3,2:T(4,128)(2,1)} %get-tuple-element.6, bf16[4,256,1,16,32]{1,0,4,3,2:T(4,128)(2,1)} %get-tuple-element.7), kind=kOutput, calls=%fused_computation.62 | convolution fusion | flops 281018624 | bytes 18939904 | tf_op jit(solution)/shard_map/sub | solution.py:61
  126.5 7.3 %fusion.38 = bf16[4,256,16,32]{1,3,2,0:T(8,128)(2,1)S(1)} fusion(f32[4,16,256,256]{2,3,1,0:T(8,128)} %get-tuple-element.24, f32[4,16,256]{2,1,0:T(8,128)S(1)} %get-tuple-element.23, bf16[4,256,1,16,32]{1,0,4,3,2:T(4,128)(2,1)S(1)} %copy-done.5), kind=kOutput, calls=%fused_computation.43 | convolution fusion | flops 277348352 | bytes 18939904 | tf_op jit(solution)/shard_map/nhqk,nkhd->nqhd/dot_general | solution.py:62
  133.8 0.9 copy.19
  135.8 29.8 %all_to_all.11 = bf16[16,4,16,512]{3,2,1,0:T(8,128)(2,1)S(1)} all-to-all(bf16[16,4,16,512]{3,2,1,0:T(8,128)(2,1)S(1)} %bitcast.79), channel_id=1, replica_groups=mesh['parts'=2,'row'=8,'col'=2] {'row','col'}, dimensions={0} | all-to-all | bytes 2097152 | tf_op jit(solution)/shard_map/all_to_all | solution.py:123
  165.9 1.2 copy.21
  167.1 1.3 fusion.31
  (34 shorter events, 4.2 us)
Async XLA Ops:
  0.0 27.3 %copy-start = (bf16[512,2048]{1,0:T(8,128)(2,1)S(1)}, bf16[512,2048]{1,0:T(8,128)(2,1)}, u32[]{:S(2)}) copy-start(bf16[512,2048]{1,0:T(8,128)(2,1)} %param.8) | copy-start | bytes 6291460
  1.2 16.1 %collective-permute-start = (bf16[1,256,512]{2,1,0:T(8,128)(2,1)S(1)}, bf16[1,256,512]{2,1,0:T(8,128)(2,1)S(1)}, u32[]{:S(2)}, u32[]{:S(2)}) collective-permute-start(bf16[1,256,512]{2,1,0:T(8,128)(2,1)S(1)} %get-tuple-element.11), channel_id=1, source_target_pairs={{0,2},{2,4},{4,6},{6,8},{8,10},{10,12},{12,14},{1,3},{3,5},{5,7},{... | collective-permute-start | bytes 786440 | tf_op jit(solution)/shard_map/ppermute | solution.py:21
  6.1 12.5 %collective-permute-start.1 = (bf16[1,256,512]{2,1,0:T(8,128)(2,1)S(1)}, bf16[1,256,512]{2,1,0:T(8,128)(2,1)S(1)}, u32[]{:S(2)}, u32[]{:S(2)}) collective-permute-start(bf16[1,256,512]{2,1,0:T(8,128)(2,1)S(1)} %get-tuple-element.10), channel_id=1, source_target_pairs={{2,0},{4,2},{6,4},{8,6},{10,8},{12,10},{14,12},{3,1},{5,3},{7,5},{... | collective-permute-start | bytes 786440 | tf_op jit(solution)/shard_map/ppermute | solution.py:23
  18.7 3.7 %collective-permute-start.2 = (bf16[6,1,512]{2,1,0:T(2,128)(2,1)S(1)}, bf16[6,1,512]{2,1,0:T(2,128)(2,1)S(1)}, u32[]{:S(2)}, u32[]{:S(2)}) collective-permute-start(bf16[6,1,512]{2,1,0:T(2,128)(2,1)S(1)} %get-tuple-element.8), channel_id=1, source_target_pairs={{0,1},{2,3},{4,5},{6,7},{8,9},{10,11},{12,13},{14,15},{16,17},{18,... | collective-permute-start | bytes 18440 | tf_op jit(solution)/shard_map/ppermute | solution.py:21
  20.0 3.1 %collective-permute-start.3 = (bf16[6,1,512]{2,1,0:T(2,128)(2,1)S(1)}, bf16[6,1,512]{2,1,0:T(2,128)(2,1)S(1)}, u32[]{:S(2)}, u32[]{:S(2)}) collective-permute-start(bf16[6,1,512]{2,1,0:T(2,128)(2,1)S(1)} %get-tuple-element.9), channel_id=1, source_target_pairs={{1,0},{3,2},{5,4},{7,6},{9,8},{11,10},{13,12},{15,14},{17,16},{19,... | collective-permute-start | bytes 18440 | tf_op jit(solution)/shard_map/ppermute | solution.py:23
  36.3 8.8 %copy-start.4 = (bf16[4,256,512]{2,1,0:T(8,128)(2,1)S(1)}, bf16[4,256,512]{2,1,0:T(8,128)(2,1)}, u32[]{:S(2)}) copy-start(bf16[4,256,512]{2,1,0:T(8,128)(2,1)} %param.7) | copy-start | bytes 3145732
  45.0 27.2 %copy-start.6 = (f32[512]{0:T(512)S(1)}, f32[512]{0:T(512)}, u32[]{:S(2)}) copy-start(f32[512]{0:T(512)} %param.11) | copy-start | bytes 6148
  71.3 1.0 copy-start.2
  71.3 32.7 %copy-start.7 = (bf16[512,1536]{1,0:T(8,128)(2,1)S(1)}, bf16[512,1536]{1,0:T(8,128)(2,1)}, u32[]{:S(2)}) copy-start(bf16[512,1536]{1,0:T(8,128)(2,1)} %param.12) | copy-start | bytes 4718596
  116.1 10.4 %copy-start.5 = (bf16[4,256,1,16,32]{1,0,4,3,2:T(4,128)(2,1)S(1)}, bf16[4,256,1,16,32]{1,0,4,3,2:T(4,128)(2,1)}, u32[]{:S(2)}) copy-start(bf16[4,256,1,16,32]{1,0,4,3,2:T(4,128)(2,1)} %get-tuple-element.5) | copy-start | bytes 3145732
  126.5 8.5 %copy-start.8 = (bf16[512,512]{1,0:T(8,128)(2,1)S(1)}, bf16[512,512]{1,0:T(8,128)(2,1)}, u32[]{:S(2)}) copy-start(bf16[512,512]{1,0:T(8,128)(2,1)} %param.13) | copy-start | bytes 1572868
  135.7 31.4 %copy-start.3 = (bf16[4,256,512]{2,1,0:T(8,128)(2,1)S(1)}, bf16[4,256,512]{2,1,0:T(8,128)(2,1)}, u32[]{:S(2)}) copy-start(bf16[4,256,512]{2,1,0:T(8,128)(2,1)} %copy-done.2) | copy-start | bytes 3145732
  135.8 32.7 %copy-start.1 = (bf16[512,2048]{1,0:T(8,128)(2,1)S(1)}, bf16[512,2048]{1,0:T(8,128)(2,1)}, u32[]{:S(2)}) copy-start(bf16[512,2048]{1,0:T(8,128)(2,1)} %param.8) | copy-start | bytes 6291460
where the time goes:
time: 169 us; the launch traced here: 168 us
  blocking collectives  60.4 us (36%)
  matrix products  55.4 us (33%)
  local copies, waits for them, and re-layouts  28.9 us (17%)
  waiting for transfers between devices  10.6 us (6%)
  starting transfers between devices  8.79 us (5%)
  other arithmetic  4.13 us (2%)
    all_to_all x1, blocking collectives, local(): lax.all_to_all(ordered, ('row', 'col'), split_axis=0, concat_axis=0, tile...  30.6 us
    all_to_all x1, blocking collectives, local(): lax.all_to_all(result.transpose(2, 1, 3, 0, 4, 5).reshape(devices, items,...  29.8 us
    dot_general x1, matrix products, local(): jnp.dot(depth.reshape(tile_rows * tile_cols, -1), project_weight, preferr...  26.2 us
    sub x1, matrix products, attend_groups(): soft = jax.nn.softmax(scores, axis=-1).astype(jnp.bfloat16)  10.4 us
    ppermute x2, waiting for transfers between devices, extended(): lax.ppermute(tail, axis, [(i, (i + 1) % count) for i in range(ends)])  9.85 us
    dot_general x1, matrix products, expand_tile(): jnp.dot(inputs.reshape(-1, shape[2]), expand_weight, preferred_element_ty...  8.95 us
    reshape x1, local copies, waits for them, and re-layouts, expand_tile(): gelu_tanh(product).astype(jnp.bfloat16).reshape(shape[0], shape[1], -1)  8.79 us
    dot_general x1, matrix products, attend_groups(): jnp.einsum('nhqk,nkhd->nqhd', soft, value_heads, preferred_element_type=j...  7.34 us
  transfers between devices with their start and end apart: 4, of which 2 were waited for; matrix products, arithmetic and copies ran while one was open for 1% of the time, Pallas kernels for 0%

commit v1 on v0

--- a/solution.py
+++ b/solution.py
@@ -1,13 +1,20 @@
+import functools
 import math
 
 import jax
 import jax.numpy as jnp
 from jax import lax
+from jax.experimental import pallas as pl
+from jax.experimental.pallas import tpu as pltpu
 from jax.sharding import PartitionSpec as P
 
 HEADS = 16
 HEAD_DIM = 32
 GRID = 16
+CHUNKS = 2
+SUBLANES = 8
+LANES = 128
+LOG2E = 1.4426950408889634
 
 
 def extended(cells, sides, width):
@@ -31,6 +38,12 @@
     return jax.nn.gelu(values, approximate=True)
 
 
+def gelu_fast(v):
+    inner = v * (0.7978845608028654 + (0.7978845608028654 * 0.044715) * (v * v))
+    half = 0.5 * v
+    return half + half * jnp.tanh(inner)
+
+
 def expand_tile(inputs, expand_weight):
     shape = inputs.shape
     product = jnp.dot(
@@ -67,9 +80,366 @@
     return result.reshape(count, members, channels)
 
 
+def mbconv_kernel(
+    col_ref, x_ref, up_ref, down_ref, side_ref, side_up_ref, side_down_ref,
+    expand_ref, taps_ref, project_ref, gain_ref,
+    normed_ref, mbconv_ref,
+    ordered, expanded, depth, acc,
+    *, chunk, span, stride_cols, stride_rows,
+):
+    step = pl.program_id(0)
+    rows, cols, channels = x_ref.shape
+    blocks = cols // stride_cols
+    wide = span + 2
+    size = wide * blocks
+    hidden = expand_ref.shape[1]
+    row_blocks = rows // stride_rows
+    first = chunk * span == 0
+    last = (chunk + 1) * span == stride_cols
+
+    @pl.when(step == 0)
+    def _():
+        at = lax.broadcasted_iota(jnp.int32, (size, cols), 0)
+        want = (at % blocks) * stride_cols + at // blocks + (chunk * span - 1)
+        select = (lax.broadcasted_iota(jnp.int32, (size, cols), 1) == want).astype(jnp.bfloat16)
+        position = lax.broadcasted_iota(jnp.int32, (size, channels), 0)
+        is_left = col_ref[0] == 0
+        for row in range(rows + 2):
+            if row == 0:
+                source, edge = up_ref[0], side_up_ref[...]
+            elif row == rows + 1:
+                source, edge = down_ref[0], side_down_ref[...]
+            else:
+                source, edge = x_ref[row - 1], side_ref[row - 1 : row, :]
+            picked = jnp.dot(select, source, preferred_element_type=jnp.float32)
+            edge = edge.astype(jnp.float32)
+            zero = jnp.zeros_like(edge)
+            if first:
+                picked = jnp.where(position == 0, jnp.where(is_left, zero, edge), picked)
+            if last:
+                picked = jnp.where(position == size - 1, jnp.where(is_left, edge, zero), picked)
+            ordered[row] = picked.astype(jnp.bfloat16)
+
+    for row in range(rows + 2):
+        product = jnp.dot(ordered[row], expand_ref[...], preferred_element_type=jnp.float32)
+        expanded[row] = gelu_fast(product).reshape(wide, blocks, hidden)
+
+    for lane in range(0, hidden, LANES):
+        taps = [
+            [taps_ref[3 * dr + dc : 3 * dr + dc + 1, lane : lane + LANES] for dc in range(3)]
+            for dr in range(3)
+        ]
+        for b in range(span):
+            for hm in range(stride_rows):
+                parts = []
+                for rb in range(row_blocks):
+                    row = rb * stride_rows + hm
+                    total = None
+                    for dr in range(3):
+                        for dc in range(3):
+                            term = expanded[row + dr, b + dc, :, lane : lane + LANES] * taps[dr][dc]
+                            total = term if total is None else total + term
+                    parts.append(gelu_fast(total))
+                place = (hm * span + b) * row_blocks * blocks
+                depth[place : place + row_blocks * blocks, lane : lane + LANES] = jnp.concatenate(
+                    parts, axis=0
+                ).astype(jnp.bfloat16)
+
+    branch = jnp.dot(depth[...], project_ref[...], preferred_element_type=jnp.float32)
+
+    @pl.when(step == 0)
+    def _():
+        acc[...] = branch
+
+    @pl.when(step > 0)
+    def _():
+        acc[...] = acc[...] + branch
+
+    @pl.when(step == pl.num_programs(0) - 1)
+    def _():
+        gain = gain_ref[...]
+        members = row_blocks * blocks
+        for hm in range(stride_rows):
+            for b in range(span):
+                pieces = []
+                for rb in range(row_blocks):
+                    begin = (b + 1) * blocks
+                    low = begin - begin % 16
+                    pair = ordered[rb * stride_rows + hm + 1, low : low + 16, :].astype(jnp.float32)
+                    pieces.append(pair[begin - low : begin - low + blocks])
+                place = (hm * span + b) * members
+                mixed = jnp.concatenate(pieces, axis=0) + acc[place : place + members, :]
+                mixed = mixed.astype(jnp.bfloat16)
+                mbconv_ref[place : place + members, :] = mixed
+                mixed = mixed.astype(jnp.float32)
+                center = jnp.mean(mixed, axis=-1, keepdims=True)
+                moved = mixed - center
+                spread = jnp.mean(moved * moved, axis=-1, keepdims=True)
+                normed_ref[place : place + members, :] = (
+                    moved * lax.rsqrt(spread + 1e-05) * gain
+                ).astype(jnp.bfloat16)
+
+
+def mbconv_chunk(chunk, span, stride_rows, stride_cols, col, tokens, halos, weights):
+    rows, cols, channels = tokens.shape
+    expand_weight, taps, project_weight, gain = weights
+    hidden = expand_weight.shape[1]
+    block = 256 if hidden % 256 == 0 else hidden
+    blocks = cols // stride_cols
+    count = rows * span * blocks
+    size = (span + 2) * blocks
+
+    def whole(array):
+        return pl.BlockSpec(array.shape, lambda i, c: (0,) * array.ndim)
+
+    grid_spec = pltpu.PrefetchScalarGridSpec(
+        num_scalar_prefetch=1,
+        grid=(hidden // block,),
+        in_specs=[whole(tokens)]
+        + [whole(h) for h in halos]
+        + [
+            pl.BlockSpec((channels, block), lambda i, c: (0, i)),
+            pl.BlockSpec((taps.shape[0], block), lambda i, c: (0, i)),
+            pl.BlockSpec((block, channels), lambda i, c: (i, 0)),
+            whole(gain),
+        ],
+        out_specs=[pl.BlockSpec((count, channels), lambda i, c: (0, 0))] * 2,
+        scratch_shapes=[
+            pltpu.VMEM((rows + 2, size, channels), jnp.bfloat16),
+            pltpu.VMEM((rows + 2, span + 2, blocks, block), jnp.float32),
+            pltpu.VMEM((count, block), jnp.bfloat16),
+            pltpu.VMEM((count, channels), jnp.float32),
+        ],
+    )
+    return pl.pallas_call(
+        functools.partial(
+            mbconv_kernel, chunk=chunk, span=span, stride_cols=stride_cols, stride_rows=stride_rows
+        ),
+        grid_spec=grid_spec,
+        out_shape=[jax.ShapeDtypeStruct((count, channels), jnp.bfloat16)] * 2,
+        compiler_params=pltpu.CompilerParams(dimension_semantics=("arbitrary",)),
+        cost_estimate=pl.CostEstimate(
+            flops=4 * count * channels * hidden * 2, bytes_accessed=8 << 20, transcendentals=0
+        ),
+        name=f"mbconv_{chunk}",
+    )(col, tokens, *halos, expand_weight, taps, project_weight, gain)
+
+
+def attend_kernel(x_ref, attend_ref, output_ref, out_ref):
+    sources, per, channels = x_ref.shape
+    members = sources * per
+    x = x_ref[...].reshape(members, channels)
+    scale = LOG2E / math.sqrt(HEAD_DIM)
+    fold = LANES // HEAD_DIM
+    lane = lax.broadcasted_iota(jnp.int32, (members, LANES), 1) // HEAD_DIM
+    ones = jnp.ones((members, LANES), jnp.bfloat16)
+    tiles = []
+    for tile in range(channels // LANES):
+        begin = tile * LANES
+        query = jnp.dot(
+            x, attend_ref[:, begin : begin + LANES], preferred_element_type=jnp.float32
+        )
+        query = (query * scale).astype(jnp.bfloat16)
+        key = jnp.dot(
+            x,
+            attend_ref[:, channels + begin : channels + begin + LANES],
+            preferred_element_type=jnp.float32,
+        ).astype(jnp.bfloat16)
+        value = jnp.dot(
+            x,
+            attend_ref[:, 2 * channels + begin : 2 * channels + begin + LANES],
+            preferred_element_type=jnp.float32,
+        ).astype(jnp.bfloat16)
+        upper = None
+        for head in range(fold):
+            inside = lane == head
+            key_head = jnp.where(inside, key, jnp.zeros_like(key))
+            value_head = jnp.where(inside, value, jnp.zeros_like(value))
+            scores = lax.dot_general(
+                query, key_head, (((1,), (1,)), ((), ())), preferred_element_type=jnp.float32
+            )
+            top = jnp.max(scores, axis=-1, keepdims=True)
+            weight = jnp.exp2(scores - top).astype(jnp.bfloat16)
+            mixed = jnp.dot(
+                weight,
+                jnp.concatenate([value_head, ones], axis=1),
+                preferred_element_type=jnp.float32,
+            )
+            if upper is None:
+                upper, lower = mixed[:, :LANES], mixed[:, LANES:]
+            else:
+                upper = upper + mixed[:, :LANES]
+                lower = jnp.where(inside, mixed[:, LANES:], lower)
+        tiles.append((upper / lower).astype(jnp.bfloat16))
+    heads_out = jnp.concatenate(tiles, axis=1)
+    result = jnp.dot(heads_out, output_ref[...], preferred_element_type=jnp.float32)
+    out_ref[...] = result.astype(jnp.bfloat16).reshape(sources, per, channels)
+
+
+def attend_chunk(chunk, piece, per, attend_weight, output_weight):
+    sources, length, channels = piece.shape
+    items = length // per
+    members = sources * per
+    spec = pl.BlockSpec((sources, per, channels), lambda i: (0, i, 0))
+    return pl.pallas_call(
+        attend_kernel,
+        grid=(items,),
+        in_specs=[
+            spec,
+            pl.BlockSpec(attend_weight.shape, lambda i: (0, 0)),
+            pl.BlockSpec(output_weight.shape, lambda i: (0, 0)),
+        ],
+        out_specs=spec,
+        out_shape=jax.ShapeDtypeStruct(piece.shape, jnp.bfloat16),
+        compiler_params=pltpu.CompilerParams(dimension_semantics=("arbitrary",)),
+        cost_estimate=pl.CostEstimate(
+            flops=items * members * channels * (8 * channels + 8 * members),
+            bytes_accessed=4 << 20,
+            transcendentals=0,
+        ),
+        name=f"attend_{chunk}",
+    )(piece, attend_weight, output_weight)
+
+
+def finish_kernel(*refs, span, stride_rows, row_blocks, blocks):
+    back_ref, mbconv_ref, out_ref = refs[0], refs[1], refs[-1]
+    channels = back_ref.shape[-1]
+    length = span * row_blocks * blocks
+    total = back_ref[...].reshape(-1, channels).astype(jnp.float32) + mbconv_ref[...].astype(
+        jnp.float32
+    )
+    total = total.astype(jnp.bfloat16)
+    at = lax.broadcasted_iota(jnp.int32, (length, length), 0)
+    b = at % span
+    a = (at // span) % blocks
+    rb = at // (span * blocks)
+    select = lax.broadcasted_iota(jnp.int32, (length, length), 1) == (b * row_blocks + rb) * blocks + a
+    select = select.astype(jnp.bfloat16)
+    for hm in range(stride_rows):
+        placed = jnp.dot(
+            select, total[hm * length : (hm + 1) * length], preferred_element_type=jnp.float32
+        ).astype(jnp.bfloat16)
+        for rb_at in range(row_blocks):
+            out_ref[rb_at * stride_rows + hm] = placed[
+                rb_at * blocks * span : (rb_at + 1) * blocks * span
+            ].reshape(blocks, span, channels)
+
+
+def finish_chunk(chunk, back, mbconv, previous, shape, span, stride_rows, stride_cols):
+    rows, cols, channels = shape
+    blocks = cols // stride_cols
+    row_blocks = rows // stride_rows
+    operands = [back, mbconv] + ([] if previous is None else [previous])
+    specs = [
+        pl.BlockSpec(back.shape, lambda i: (0, 0, 0)),
+        pl.BlockSpec(mbconv.shape, lambda i: (0, 0)),
+    ] + ([] if previous is None else [pl.BlockSpec(memory_space=pl.ANY)])
+    return pl.pallas_call(
+        functools.partial(
+            finish_kernel, span=span, stride_rows=stride_rows, row_blocks=row_blocks, blocks=blocks
+        ),
+        grid=(1,),
+        in_specs=specs,
+        out_specs=pl.BlockSpec((rows, blocks, span, channels), lambda i: (0, 0, chunk, 0)),
+        out_shape=jax.ShapeDtypeStruct((rows, blocks, stride_cols, channels), jnp.bfloat16),
+        input_output_aliases={} if previous is None else {2: 0},
+        cost_estimate=pl.CostEstimate(
+            flops=2 * rows * span * blocks * channels * span * row_blocks * blocks,
+            bytes_accessed=2 << 20,
+            transcendentals=0,
+        ),
+        name=f"finish_{chunk}",
+    )(*operands)
+
+
+def chunked(
+    tokens, expand_weight, depth_kernel, project_weight, norm_gain, attend_weight, output_weight
+):
+    rows, cols, channels = tokens.shape
+    row_count = lax.axis_size("row")
+    col_count = lax.axis_size("col")
+    devices = row_count * col_count
+    stride_rows = rows * row_count // GRID
+    stride_cols = cols * col_count // GRID
+    blocks = cols // stride_cols
+    row_blocks = rows // stride_rows
+    span = stride_cols // CHUNKS
+    per = row_blocks * blocks
+    both = ("row", "col")
+
+    col = lax.axis_index("col")
+    edge = jnp.where(col == 0, tokens[:, cols - 1], tokens[:, 0])
+    ups = [(r, r + 1) for r in range(row_count - 1)]
+    downs = [(r + 1, r) for r in range(row_count - 1)]
+    across = lambda pairs: [
+        (f * col_count + c, t * col_count + 1 - c) for f, t in pairs for c in range(col_count)
+    ]
+    up = lax.ppermute(tokens[rows - 1 :], "row", ups)
+    down = lax.ppermute(tokens[:1], "row", downs)
+    side = lax.ppermute(edge, "col", [(0, 1), (1, 0)])
+    side_up = lax.ppermute(edge[rows - 1 :], both, across(ups))
+    side_down = lax.ppermute(edge[:1], both, across(downs))
+    halos = (up, down, side, side_up, side_down)
+    weights = (
+        expand_weight,
+        depth_kernel.reshape(9, -1),
+        project_weight,
+        norm_gain.reshape(1, -1),
+    )
+    col_scalar = col.astype(jnp.int32).reshape(1)
+
+    pieces, keeps = [], []
+    for chunk in range(CHUNKS):
+        normed, mbconv = mbconv_chunk(
+            chunk, span, stride_rows, stride_cols, col_scalar, tokens, halos, weights
+        )
+        keeps.append(mbconv)
+        pieces.append(
+            lax.all_to_all(
+                normed.reshape(devices, -1, channels), both, split_axis=0, concat_axis=0, tiled=True
+            )
+        )
+    backs = []
+    for chunk in range(CHUNKS):
+        result = attend_chunk(chunk, pieces[chunk], per, attend_weight, output_weight)
+        backs.append(lax.all_to_all(result, both, split_axis=0, concat_axis=0, tiled=True))
+    out = None
+    for chunk in range(CHUNKS):
+        out = finish_chunk(
+            chunk, backs[chunk], keeps[chunk], out, tokens.shape, span, stride_rows, stride_cols
+        )
+    return out.reshape(rows, cols, channels)
+
+
+def fits(tokens_shape, row_count, col_count):
+    rows, cols, channels = tokens_shape
+    stride_rows = rows * row_count // GRID
+    stride_cols = cols * col_count // GRID
+    groups = stride_rows * stride_cols
+    return (
+        col_count == 2
+        and rows % stride_rows == 0
+        and cols % stride_cols == 0
+        and cols // stride_cols == SUBLANES
+        and rows // stride_rows == 2
+        and groups % (CHUNKS * row_count * col_count) == 0
+        and channels % LANES == 0
+    )
+
+
 def local(
     tokens, expand_weight, depth_kernel, project_weight, norm_gain, attend_weight, output_weight
 ):
+    if fits(tokens.shape, lax.axis_size("row"), lax.axis_size("col")):
+        return chunked(
+            tokens,
+            expand_weight,
+            depth_kernel,
+            project_weight,
+            norm_gain,
+            attend_weight,
+            output_weight,
+        )
     tile_rows, tile_cols, channels = tokens.shape
     padded_in = extended(tokens, (("row", 0), ("col", 1)), 1)
     expanded = expand_tile(padded_in, expand_weight)

time: 169 us -> 114 us (0.67)
  blocking collectives: 60.4 us -> 0 us
  matrix products: 55.4 us -> 0 us
  Pallas kernels: 0 us -> 49.6 us
  starting transfers between devices: 8.79 us -> 33.7 us
  local copies, waits for them, and re-layouts: 28.9 us -> 5.03 us
  waiting for transfers between devices: 10.6 us -> 24.3 us
  other arithmetic: 4.13 us -> 0.01 us
    all_to_all x2 -> x0, blocking collectives: 60.4 us -> none  [the longest x1 30.6 us: local(): lax.all_to_all(ordered, ('row', 'col'), split_axis=0, concat_axis=0, tile...]
    pallas_call x0 -> x6, Pallas kernels: none -> 49.6 us  [the longest x2 27.2 us: mbconv_chunk(): pl.pallas_call(functools.partial(mbconv_kernel, chunk=chunk, span=span, s...]
    dot_general x5 -> x0, matrix products: 45.1 us -> none  [the longest x1 26.2 us: local(): jnp.dot(depth.reshape(tile_rows * tile_cols, -1), project_weight, preferr...]
    all_to_all x0 -> x4, waiting for transfers between devices: none -> 23.4 us  [the longest x2 17.3 us: chunked(): lax.all_to_all(result, both, split_axis=0, concat_axis=0, tiled=True)]
    all_to_all x0 -> x4, starting transfers between devices: none -> 19.9 us  [the longest x2 11.6 us: chunked(): lax.all_to_all(normed.reshape(devices, -1, channels), both, split_axis=0,...]
    reshape x5 -> x1, local copies, waits for them, and re-layouts: 16.9 us -> 1.58 us  [chunked(): depth_kernel.reshape(9, -1)]
    sub x1 -> x0, matrix products: 10.4 us -> none  [attend_groups(): soft = jax.nn.softmax(scores, axis=-1).astype(jnp.bfloat16)]
    ppermute x4 -> x5, waiting for transfers between devices: 10.6 us -> 0.9 us  [the longest x1 0.88 us: chunked(): side_up = lax.ppermute(edge[rows - 1:], both, across(ups))]
  transfers between devices with their start and end apart: 4 -> 9, of which waited for: 2 -> 5; matrix products, arithmetic and copies ran while one was open for 1% -> 2% of each run, Pallas kernels for 0% -> 30%
where the time goes in v1:
time: 114 us; the launch traced here: 113 us
  Pallas kernels  49.6 us (44%)
  starting transfers between devices  33.7 us (30%)
  waiting for transfers between devices  24.3 us (21%)
  local copies, waits for them, and re-layouts  5.03 us (4%)
    pallas_call x2, Pallas kernels, mbconv_chunk(): pl.pallas_call(functools.partial(mbconv_kernel, chunk=chunk, span=span, s...  27.2 us
    pallas_call x2, Pallas kernels, attend_chunk(): pl.pallas_call(attend_kernel, grid=(items,), in_specs=[spec, pl.BlockSpec...  17.7 us
    all_to_all x2, waiting for transfers between devices, chunked(): lax.all_to_all(result, both, split_axis=0, concat_axis=0, tiled=True)  17.3 us
    all_to_all x2, starting transfers between devices, chunked(): lax.all_to_all(normed.reshape(devices, -1, channels), both, split_axis=0,...  11.6 us
    all_to_all x2, starting transfers between devices, chunked(): lax.all_to_all(result, both, split_axis=0, concat_axis=0, tiled=True)  8.33 us
    all_to_all x2, waiting for transfers between devices, chunked(): lax.all_to_all(normed.reshape(devices, -1, channels), both, split_axis=0,...  6.07 us
    ppermute x1, starting transfers between devices, chunked(): up = lax.ppermute(tokens[rows - 1:], 'row', ups)  5.54 us
    ppermute x1, starting transfers between devices, chunked(): side_up = lax.ppermute(edge[rows - 1:], both, across(ups))  5.51 us
  transfers between devices with their start and end apart: 9, of which 5 were waited for; matrix products, arithmetic and copies ran while one was open for 2% of the time, Pallas kernels for 30%

profile of v1, /device:TPU:0, one launch (start us, length us, event | category | flops | bytes accessed | tf_op | source)
XLA Modules:
  0.0 112.8 jit_solution(17629820132279861811)
XLA Ops:
  0.0 1.1 fusion.1
  1.1 1.3 %collective-permute-start.1 = (bf16[1,256,512]{2,1,0:T(8,128)(2,1)S(1)}, bf16[1,256,512]{2,1,0:T(8,128)(2,1)S(1)}, u32[]{:S(2)}, u32[]{:S(2)}) collective-permute-start(bf16[1,256,512]{2,1,0:T(8,128)(2,1)S(1)} %get-tuple-element.15), channel_id=1, source_target_pairs={{2,0},{4,2},{6,4},{8,6},{10,8},{12,10},{14,12},{3,1},{5,3},{7,5},{... | collective-permute-start | bytes 786440 | tf_op jit(solution)/shard_map/ppermute | solution.py:378
  2.4 5.5 %collective-permute-start = (bf16[1,256,512]{2,1,0:T(8,128)(2,1)S(1)}, bf16[1,256,512]{2,1,0:T(8,128)(2,1)S(1)}, u32[]{:S(2)}, u32[]{:S(2)}) collective-permute-start(bf16[1,256,512]{2,1,0:T(8,128)(2,1)S(1)} %get-tuple-element.16), channel_id=1, source_target_pairs={{0,2},{2,4},{4,6},{6,8},{8,10},{10,12},{12,14},{1,3},{3,5},{5,7},{... | collective-permute-start | bytes 786440 | tf_op jit(solution)/shard_map/ppermute | solution.py:377
  7.9 0.8 fusion
  8.8 1.3 %collective-permute-start.4 = (bf16[1,512]{1,0:T(2,128)(2,1)S(1)}, bf16[1,512]{1,0:T(2,128)(2,1)S(1)}, u32[]{:S(2)}, u32[]{:S(2)}) collective-permute-start(bf16[1,512]{1,0:T(2,128)(2,1)S(1)} %get-tuple-element.17), channel_id=1, source_target_pairs={{2,1},{3,0},{4,3},{5,2},{6,5},{7,4},{8,7},{9,6},{10,9},{11,8},{12,... | collective-permute-start | bytes 3080 | tf_op jit(solution)/shard_map/ppermute | solution.py:381
  10.1 5.5 %collective-permute-start.3 = (bf16[1,512]{1,0:T(2,128)(2,1)S(1)}, bf16[1,512]{1,0:T(2,128)(2,1)S(1)}, u32[]{:S(2)}, u32[]{:S(2)}) collective-permute-start(bf16[1,512]{1,0:T(2,128)(2,1)S(1)} %get-tuple-element.18), channel_id=1, source_target_pairs={{0,3},{1,2},{2,5},{3,4},{4,7},{5,6},{6,9},{7,8},{8,11},{9,10},{10,... | collective-permute-start | bytes 3080 | tf_op jit(solution)/shard_map/ppermute | solution.py:380
  15.7 1.6 %reshape.23.taps_ref = f32[9,2048]{1,0:T(8,128)} reshape(f32[3,3,2048]{2,1,0:T(4,128)} %param.9) | data formatting | bytes 147456 | tf_op jit(solution)/shard_map/reshape | solution.py:385
  17.3 0.9 collective-permute-done.3.side_up_ref
  18.2 0.5 copy-done.8
  18.9 13.6 %mbconv_0.1 = (bf16[512,512]{1,0:T(8,128)(2,1)}, bf16[512,512]{1,0:T(8,128)(2,1)}) custom-call(s32[1]{0:T(128)} %bitcast.col_ref, bf16[4,256,512]{2,1,0:T(8,128)(2,1)} %x_ref.3, bf16[1,256,512]{2,1,0:T(8,128)(2,1)} %copy-done.5, bf16[1,256,512]{2,1,0:T(8,128)(2,1)} %copy-done.4, bf16[4,512]{1,0:T(4,128)(2,1)} %copy-done.6, bf16[1,512]{1,0:T(2,128)(2,1)} %copy-done.8, ...), custom_call_target="tpu_custom_call" | custom-call | flops 4294967296 | bytes 8388608 | tf_op jit(solution)/shard_map/mbconv_0/pallas_call | solution.py:214
  32.5 6.3 %all-to-all-start.2 = ((bf16[16,32,512]{2,1,0:T(8,128)(2,1)}), bf16[16,32,512]{2,1,0:T(8,128)(2,1)S(1)}, u32[]{:S(2)}, u32[]{:S(2)}) async-start(bf16[16,32,512]{2,1,0:T(8,128)(2,1)} %bitcast.11), calls=%async_computation.2 | async-start | bytes 1048576 | tf_op jit(solution)/shard_map/all_to_all | solution.py:398
  38.8 13.6 %mbconv_1.1 = (bf16[512,512]{1,0:T(8,128)(2,1)}, bf16[512,512]{1,0:T(8,128)(2,1)}) custom-call(s32[1]{0:T(128)} %bitcast.col_ref, bf16[4,256,512]{2,1,0:T(8,128)(2,1)} %x_ref.3, bf16[1,256,512]{2,1,0:T(8,128)(2,1)} %copy-done.5, bf16[1,256,512]{2,1,0:T(8,128)(2,1)} %copy-done.4, bf16[4,512]{1,0:T(4,128)(2,1)} %copy-done.6, bf16[1,512]{1,0:T(2,128)(2,1)} %copy-done.8, ...), custom_call_target="tpu_custom_call" | custom-call | flops 4294967296 | bytes 8388608 | tf_op jit(solution)/shard_map/mbconv_1/pallas_call | solution.py:214
  52.5 0.7 all-to-all-done.2.x_ref
  53.1 5.3 %all-to-all-start = ((bf16[16,32,512]{2,1,0:T(8,128)(2,1)}), bf16[16,32,512]{2,1,0:T(8,128)(2,1)S(1)}, u32[]{:S(2)}, u32[]{:S(2)}) async-start(bf16[16,32,512]{2,1,0:T(8,128)(2,1)} %bitcast.10), calls=%async_computation | async-start | bytes 1048576 | tf_op jit(solution)/shard_map/all_to_all | solution.py:398
  58.5 8.8 %attend_0.1 = bf16[16,32,512]{2,1,0:T(8,128)(2,1)} custom-call(bf16[16,32,512]{2,1,0:T(8,128)(2,1)} %copy-done.2, bf16[512,1536]{1,0:T(8,128)(2,1)} %attend_ref.3, bf16[512,512]{1,0:T(8,128)(2,1)} %output_ref.3), custom_call_target="tpu_custom_call" | custom-call | flops 1610612736 | bytes 4194304 | tf_op jit(solution)/shard_map/attend_0/pallas_call | solution.py:284
  67.3 5.4 %all-to-all-done.x_ref = bf16[16,32,512]{2,1,0:T(8,128)(2,1)S(1)} async-done(((bf16[16,32,512]{2,1,0:T(8,128)(2,1)}), bf16[16,32,512]{2,1,0:T(8,128)(2,1)S(1)}, u32[]{:S(2)}, u32[]{:S(2)}) %all-to-all-start) | async-done | bytes 524320 | tf_op jit(solution)/shard_map/all_to_all | solution.py:398
  72.7 4.2 %all-to-all-start.3 = ((bf16[16,32,512]{2,1,0:T(8,128)(2,1)}), bf16[16,32,512]{2,1,0:T(8,128)(2,1)S(1)}, u32[]{:S(2)}, u32[]{:S(2)}) async-start(bf16[16,32,512]{2,1,0:T(8,128)(2,1)} %attend_0.1), calls=%async_computation.3 | async-start | bytes 1048576 | tf_op jit(solution)/shard_map/all_to_all | solution.py:405
  76.9 8.8 %attend_1.1 = bf16[16,32,512]{2,1,0:T(8,128)(2,1)} custom-call(bf16[16,32,512]{2,1,0:T(8,128)(2,1)} %copy-done.3, bf16[512,1536]{1,0:T(8,128)(2,1)} %attend_ref.3, bf16[512,512]{1,0:T(8,128)(2,1)} %output_ref.3), custom_call_target="tpu_custom_call" | custom-call | flops 1610612736 | bytes 4194304 | tf_op jit(solution)/shard_map/attend_1/pallas_call | solution.py:284
  85.7 5.4 %all-to-all-done.3.refs_0_ = bf16[16,32,512]{2,1,0:T(8,128)(2,1)S(1)} async-done(((bf16[16,32,512]{2,1,0:T(8,128)(2,1)}), bf16[16,32,512]{2,1,0:T(8,128)(2,1)S(1)}, u32[]{:S(2)}, u32[]{:S(2)}) %all-to-all-start.3) | async-done | bytes 524320 | tf_op jit(solution)/shard_map/all_to_all | solution.py:405
  91.2 4.2 %all-to-all-start.1 = ((bf16[16,32,512]{2,1,0:T(8,128)(2,1)}), bf16[16,32,512]{2,1,0:T(8,128)(2,1)S(1)}, u32[]{:S(2)}, u32[]{:S(2)}) async-start(bf16[16,32,512]{2,1,0:T(8,128)(2,1)} %attend_1.1), calls=%async_computation.1 | async-start | bytes 1048576 | tf_op jit(solution)/shard_map/all_to_all | solution.py:405
  95.4 2.4 %finish_0.1.refs_2_ = bf16[4,8,32,512]{3,2,1,0:T(8,128)(2,1)} custom-call(bf16[16,32,512]{2,1,0:T(8,128)(2,1)} %copy-done, bf16[512,512]{1,0:T(8,128)(2,1)} %get-tuple-element.12.refs_1_), custom_call_target="tpu_custom_call" | custom-call | flops 134217728 | bytes 2097152 | tf_op jit(solution)/shard_map/finish_0/pallas_call | solution.py:337
  97.7 11.9 %all-to-all-done.1.refs_0_ = bf16[16,32,512]{2,1,0:T(8,128)(2,1)S(1)} async-done(((bf16[16,32,512]{2,1,0:T(8,128)(2,1)}), bf16[16,32,512]{2,1,0:T(8,128)(2,1)S(1)}, u32[]{:S(2)}, u32[]{:S(2)}) %all-to-all-start.1) | async-done | bytes 524320 | tf_op jit(solution)/shard_map/all_to_all | solution.py:405
  109.6 0.8 copy-done.1
  110.4 2.4 %finish_1.1 = bf16[4,8,32,512]{3,2,1,0:T(8,128)(2,1)} custom-call(bf16[16,32,512]{2,1,0:T(8,128)(2,1)} %copy-done.1, bf16[512,512]{1,0:T(8,128)(2,1)} %get-tuple-element.10.refs_1_, bf16[4,8,32,512]{3,2,1,0:T(8,128)(2,1)} %finish_0.1.refs_2_), custom_call_target="tpu_custom_call", output_to_operand_aliasing={{}: (2, {})} | custom-call | flops 134217728 | bytes 2097152 | tf_op jit(solution)/shard_map/finish_1/pallas_call | solution.py:337
  (23 shorter events, 0.3 us)
Async XLA Ops:
  1.1 17.1 %collective-permute-start.1 = (bf16[1,256,512]{2,1,0:T(8,128)(2,1)S(1)}, bf16[1,256,512]{2,1,0:T(8,128)(2,1)S(1)}, u32[]{:S(2)}, u32[]{:S(2)}) collective-permute-start(bf16[1,256,512]{2,1,0:T(8,128)(2,1)S(1)} %get-tuple-element.15), channel_id=1, source_target_pairs={{2,0},{4,2},{6,4},{8,6},{10,8},{12,10},{14,12},{3,1},{5,3},{7,5},{... | collective-permute-start | bytes 786440 | tf_op jit(solution)/shard_map/ppermute | solution.py:378
  2.4 15.8 %collective-permute-start = (bf16[1,256,512]{2,1,0:T(8,128)(2,1)S(1)}, bf16[1,256,512]{2,1,0:T(8,128)(2,1)S(1)}, u32[]{:S(2)}, u32[]{:S(2)}) collective-permute-start(bf16[1,256,512]{2,1,0:T(8,128)(2,1)S(1)} %get-tuple-element.16), channel_id=1, source_target_pairs={{0,2},{2,4},{4,6},{6,8},{8,10},{10,12},{12,14},{1,3},{3,5},{5,7},{... | collective-permute-start | bytes 786440 | tf_op jit(solution)/shard_map/ppermute | solution.py:377
  8.7 9.4 %collective-permute-start.2 = (bf16[4,512]{1,0:T(4,128)(2,1)S(1)}, bf16[4,512]{1,0:T(4,128)(2,1)S(1)}, u32[]{:S(2)}, u32[]{:S(2)}) collective-permute-start(bf16[4,512]{1,0:T(4,128)(2,1)S(1)} %bitcast.12), channel_id=1, source_target_pairs={{0,1},{1,0},{2,3},{3,2},{4,5},{5,4},{6,7},{7,6},{8,9},{9,8},{10,11... | collective-permute-start | bytes 12296 | tf_op jit(solution)/shard_map/ppermute | solution.py:379
  8.8 8.4 %collective-permute-start.4 = (bf16[1,512]{1,0:T(2,128)(2,1)S(1)}, bf16[1,512]{1,0:T(2,128)(2,1)S(1)}, u32[]{:S(2)}, u32[]{:S(2)}) collective-permute-start(bf16[1,512]{1,0:T(2,128)(2,1)S(1)} %get-tuple-element.17), channel_id=1, source_target_pairs={{2,1},{3,0},{4,3},{5,2},{6,5},{7,4},{8,7},{9,6},{10,9},{11,8},{12,... | collective-permute-start | bytes 3080 | tf_op jit(solution)/shard_map/ppermute | solution.py:381
  10.1 8.0 %collective-permute-start.3 = (bf16[1,512]{1,0:T(2,128)(2,1)S(1)}, bf16[1,512]{1,0:T(2,128)(2,1)S(1)}, u32[]{:S(2)}, u32[]{:S(2)}) collective-permute-start(bf16[1,512]{1,0:T(2,128)(2,1)S(1)} %get-tuple-element.18), channel_id=1, source_target_pairs={{0,3},{1,2},{2,5},{3,4},{4,7},{5,6},{6,9},{7,8},{8,11},{9,10},{10,... | collective-permute-start | bytes 3080 | tf_op jit(solution)/shard_map/ppermute | solution.py:380
  17.2 0.9 copy-start.7
  18.1 0.6 copy-start.8
  18.1 0.6 copy-start.6
  18.1 0.7 copy-start.4
  18.2 0.8 copy-start.5
  32.5 20.6 %all-to-all-start.2 = ((bf16[16,32,512]{2,1,0:T(8,128)(2,1)}), bf16[16,32,512]{2,1,0:T(8,128)(2,1)S(1)}, u32[]{:S(2)}, u32[]{:S(2)}) async-start(bf16[16,32,512]{2,1,0:T(8,128)(2,1)} %bitcast.11), calls=%async_computation.2 | async-start | bytes 1048576 | tf_op jit(solution)/shard_map/all_to_all | solution.py:398
  53.1 5.4 %copy-start.2 = (bf16[16,32,512]{2,1,0:T(8,128)(2,1)}, bf16[16,32,512]{2,1,0:T(8,128)(2,1)S(1)}, u32[]{:S(2)}) copy-start(bf16[16,32,512]{2,1,0:T(8,128)(2,1)S(1)} %all-to-all-done.2.x_ref) | copy-start | bytes 1572868
  53.1 19.6 %all-to-all-start = ((bf16[16,32,512]{2,1,0:T(8,128)(2,1)}), bf16[16,32,512]{2,1,0:T(8,128)(2,1)S(1)}, u32[]{:S(2)}, u32[]{:S(2)}) async-start(bf16[16,32,512]{2,1,0:T(8,128)(2,1)} %bitcast.10), calls=%async_computation | async-start | bytes 1048576 | tf_op jit(solution)/shard_map/all_to_all | solution.py:398
  72.7 4.2 %copy-start.3 = (bf16[16,32,512]{2,1,0:T(8,128)(2,1)}, bf16[16,32,512]{2,1,0:T(8,128)(2,1)S(1)}, u32[]{:S(2)}) copy-start(bf16[16,32,512]{2,1,0:T(8,128)(2,1)S(1)} %all-to-all-done.x_ref) | copy-start | bytes 1572868
  72.7 18.4 %all-to-all-start.3 = ((bf16[16,32,512]{2,1,0:T(8,128)(2,1)}), bf16[16,32,512]{2,1,0:T(8,128)(2,1)S(1)}, u32[]{:S(2)}, u32[]{:S(2)}) async-start(bf16[16,32,512]{2,1,0:T(8,128)(2,1)} %attend_0.1), calls=%async_computation.3 | async-start | bytes 1048576 | tf_op jit(solution)/shard_map/all_to_all | solution.py:405
  91.2 4.2 %copy-start = (bf16[16,32,512]{2,1,0:T(8,128)(2,1)}, bf16[16,32,512]{2,1,0:T(8,128)(2,1)S(1)}, u32[]{:S(2)}) copy-start(bf16[16,32,512]{2,1,0:T(8,128)(2,1)S(1)} %all-to-all-done.3.refs_0_) | copy-start | bytes 1572868
  91.2 18.4 %all-to-all-start.1 = ((bf16[16,32,512]{2,1,0:T(8,128)(2,1)}), bf16[16,32,512]{2,1,0:T(8,128)(2,1)S(1)}, u32[]{:S(2)}, u32[]{:S(2)}) async-start(bf16[16,32,512]{2,1,0:T(8,128)(2,1)} %attend_1.1), calls=%async_computation.1 | async-start | bytes 1048576 | tf_op jit(solution)/shard_map/all_to_all | solution.py:405
  109.6 0.8 copy-start.1

commit v2 on v1

--- a/solution.py
+++ b/solution.py
@@ -15,6 +15,11 @@
 SUBLANES = 8
 LANES = 128
 LOG2E = 1.4426950408889634
+BLOCK = 256
+GELU_ONE = math.sqrt(2 / math.pi)
+GELU_THREE = 0.044715 * GELU_ONE
+TAP_SCALE = 0.5 * math.sqrt(GELU_THREE)
+BRANCH_SCALE = 0.5 / math.sqrt(GELU_THREE)
 
 
 def extended(cells, sides, width):
@@ -38,10 +43,12 @@
     return jax.nn.gelu(values, approximate=True)
 
 
-def gelu_fast(v):
-    inner = v * (0.7978845608028654 + (0.7978845608028654 * 0.044715) * (v * v))
-    half = 0.5 * v
-    return half + half * jnp.tanh(inner)
+def gelu_twice(v):
+    return v + v * jnp.tanh(v * (GELU_ONE + GELU_THREE * (v * v)))
+
+
+def gelu_scaled(w):
+    return w + w * jnp.tanh(w * (GELU_ONE / math.sqrt(GELU_THREE) + w * w))
 
 
 def expand_tile(inputs, expand_weight):
@@ -80,95 +87,186 @@
     return result.reshape(count, members, channels)
 
 
-def mbconv_kernel(
-    col_ref, x_ref, up_ref, down_ref, side_ref, side_up_ref, side_down_ref,
-    expand_ref, taps_ref, project_ref, gain_ref,
-    normed_ref, mbconv_ref,
-    ordered, expanded, depth, acc,
-    *, chunk, span, stride_cols, stride_rows,
+def expand_kernel(
+    col_ref, x_ref, side_ref, expand_ref, ordered_ref, *rest, stride_cols, span, chunks
 ):
+    expanded_refs = rest
     step = pl.program_id(0)
     rows, cols, channels = x_ref.shape
     blocks = cols // stride_cols
+    size = (stride_cols + 2) * blocks
+    part = (span + 2) * blocks
+
+    @pl.when(step == 0)
+    def _():
+        for row in range(rows):
+            ordered_ref[row] = arrange(
+                x_ref[row], side_ref[row : row + 1, :], col_ref[0] == 0, -1, size, stride_cols, blocks,
+                True, True,
+            )
+
+    for half in range(2):
+        for row in range(rows):
+            product = jnp.dot(
+                ordered_ref[row],
+                expand_ref[:, half * BLOCK : (half + 1) * BLOCK],
+                preferred_element_type=jnp.float32,
+            )
+            value = gelu_twice(product).astype(jnp.bfloat16)
+            for chunk in range(chunks):
+                begin = chunk * span * blocks
+                expanded_refs[chunk][half, row] = value[begin : begin + part]
+
+
+def arrange(source, edge, is_left, start, size, stride_cols, blocks, first, last):
+    cols, channels = source.shape
+    at = lax.broadcasted_iota(jnp.int32, (size, cols), 0)
+    want = (at % blocks) * stride_cols + at // blocks + start
+    select = (lax.broadcasted_iota(jnp.int32, (size, cols), 1) == want).astype(jnp.bfloat16)
+    picked = jnp.dot(select, source, preferred_element_type=jnp.float32)
+    position = lax.broadcasted_iota(jnp.int32, (size, channels), 0)
+    edge = edge.astype(jnp.float32)
+    zero = jnp.zeros_like(edge)
+    if first:
+        picked = jnp.where(position == 0, jnp.where(is_left, zero, edge), picked)
+    if last:
+        picked = jnp.where(position == size - 1, jnp.where(is_left, edge, zero), picked)
+    return picked.astype(jnp.bfloat16)
+
+
+def expand_rows(col, tokens, side, expand_weight, stride_cols, span):
+    rows, cols, channels = tokens.shape
+    hidden = expand_weight.shape[1]
+    blocks = cols // stride_cols
+    size = (stride_cols + 2) * blocks
+    part = (span + 2) * blocks
+    steps = hidden // BLOCK
+    return pl.pallas_call(
+        functools.partial(expand_kernel, stride_cols=stride_cols, span=span, chunks=CHUNKS),
+        grid_spec=pltpu.PrefetchScalarGridSpec(
+            num_scalar_prefetch=1,
+            grid=(steps // 2,),
+            in_specs=[
+                pl.BlockSpec(tokens.shape, lambda i, c: (0, 0, 0)),
+                pl.BlockSpec(side.shape, lambda i, c: (0, 0)),
+                pl.BlockSpec((channels, 2 * BLOCK), lambda i, c: (0, i)),
+            ],
+            out_specs=[pl.BlockSpec((rows, size, channels), lambda i, c: (0, 0, 0))]
+            + [pl.BlockSpec((2, rows, part, BLOCK), lambda i, c: (i, 0, 0, 0))] * CHUNKS,
+        ),
+        out_shape=[jax.ShapeDtypeStruct((rows, size, channels), jnp.bfloat16)]
+        + [jax.ShapeDtypeStruct((steps, rows, part, BLOCK), jnp.bfloat16)] * CHUNKS,
+        compiler_params=pltpu.CompilerParams(dimension_semantics=("arbitrary",)),
+        cost_estimate=pl.CostEstimate(
+            flops=2 * rows * size * channels * hidden, bytes_accessed=8 << 20, transcendentals=0
+        ),
+        name="expand",
+    )(col, tokens, side, expand_weight)
+
+
+def mbconv_kernel(
+    col_ref, up_ref, down_ref, side_up_ref, side_down_ref, ordered_ref, own_ref,
+    expand_ref, taps_ref, project_old_ref, project_new_ref, project_last_ref, gain_ref,
+    normed_ref, mbconv_ref,
+    halo, edge_rows, depth_a, depth_b, acc,
+    *, chunk, span, stride_cols, stride_rows, rows,
+):
+    step = pl.program_id(0)
+    channels = up_ref.shape[2]
+    blocks = up_ref.shape[1] // stride_cols
     wide = span + 2
     size = wide * blocks
-    hidden = expand_ref.shape[1]
     row_blocks = rows // stride_rows
-    first = chunk * span == 0
-    last = (chunk + 1) * span == stride_cols
+    members = row_blocks * blocks
 
     @pl.when(step == 0)
     def _():
-        at = lax.broadcasted_iota(jnp.int32, (size, cols), 0)
-        want = (at % blocks) * stride_cols + at // blocks + (chunk * span - 1)
-        select = (lax.broadcasted_iota(jnp.int32, (size, cols), 1) == want).astype(jnp.bfloat16)
-        position = lax.broadcasted_iota(jnp.int32, (size, channels), 0)
-        is_left = col_ref[0] == 0
-        for row in range(rows + 2):
-            if row == 0:
-                source, edge = up_ref[0], side_up_ref[...]
-            elif row == rows + 1:
-                source, edge = down_ref[0], side_down_ref[...]
-            else:
-                source, edge = x_ref[row - 1], side_ref[row - 1 : row, :]
-            picked = jnp.dot(select, source, preferred_element_type=jnp.float32)
-            edge = edge.astype(jnp.float32)
-            zero = jnp.zeros_like(edge)
-            if first:
-                picked = jnp.where(position == 0, jnp.where(is_left, zero, edge), picked)
-            if last:
-                picked = jnp.where(position == size - 1, jnp.where(is_left, edge, zero), picked)
-            ordered[row] = picked.astype(jnp.bfloat16)
-
-    for row in range(rows + 2):
-        product = jnp.dot(ordered[row], expand_ref[...], preferred_element_type=jnp.float32)
-        expanded[row] = gelu_fast(product).reshape(wide, blocks, hidden)
-
-    for lane in range(0, hidden, LANES):
-        taps = [
-            [taps_ref[3 * dr + dc : 3 * dr + dc + 1, lane : lane + LANES] for dc in range(3)]
-            for dr in range(3)
-        ]
-        for b in range(span):
-            for hm in range(stride_rows):
-                parts = []
-                for rb in range(row_blocks):
-                    row = rb * stride_rows + hm
-                    total = None
-                    for dr in range(3):
-                        for dc in range(3):
-                            term = expanded[row + dr, b + dc, :, lane : lane + LANES] * taps[dr][dc]
-                            total = term if total is None else total + term
-                    parts.append(gelu_fast(total))
-                place = (hm * span + b) * row_blocks * blocks
-                depth[place : place + row_blocks * blocks, lane : lane + LANES] = jnp.concatenate(
-                    parts, axis=0
-                ).astype(jnp.bfloat16)
-
-    branch = jnp.dot(depth[...], project_ref[...], preferred_element_type=jnp.float32)
-
-    @pl.when(step == 0)
-    def _():
-        acc[...] = branch
-
-    @pl.when(step > 0)
-    def _():
-        acc[...] = acc[...] + branch
+        for side, (source_ref, edge_ref) in enumerate(
+            ((up_ref, side_up_ref), (down_ref, side_down_ref))
+        ):
+            halo[side] = arrange(
+                source_ref[0], edge_ref[...], col_ref[0] == 0, chunk * span - 1, size, stride_cols,
+                blocks, chunk * span == 0, (chunk + 1) * span == stride_cols,
+            )
+        depth_b[...] = jnp.zeros_like(depth_b)
+        acc[...] = jnp.zeros_like(acc)
+
+    for half, depth in ((0, depth_a), (1, depth_b)):
+        lanes = slice(half * BLOCK, (half + 1) * BLOCK)
+        for side in range(2):
+            product = jnp.dot(halo[side], expand_ref[:, lanes], preferred_element_type=jnp.float32)
+            edge_rows[half, side] = gelu_twice(product).reshape(wide, blocks, BLOCK)
+        if half == 0:
+            acc[...] = acc[...] + jnp.dot(
+                depth_b[...], project_old_ref[...], preferred_element_type=jnp.float32
+            )
+        for lane in range(0, BLOCK, LANES):
+            taps = [
+                [
+                    taps_ref[dr, dc : dc + 1, half * BLOCK + lane : half * BLOCK + lane + LANES]
+                    * TAP_SCALE
+                    for dc in range(3)
+                ]
+                for dr in range(3)
+            ]
+            for pair in range(0, span, 2):
+                source = []
+                for row in range(rows + 2):
+                    if row == 0 or row == rows + 1:
+                        source.append(
+                            [
+                                edge_rows[half, min(row, 1), pair + k, :, lane : lane + LANES]
+                                for k in range(4)
+                            ]
+                        )
+                    else:
+                        source.append(
+                            [
+                                own_ref[
+                                    half, row - 1, (pair + k) * blocks : (pair + k + 2) * blocks,
+                                    lane : lane + LANES,
+                                ].astype(jnp.float32)[j * blocks : (j + 1) * blocks]
+                                for k in (0, 2)
+                                for j in (0, 1)
+                            ]
+                        )
+                for b in (0, 1):
+                    for hm in range(stride_rows):
+                        parts = []
+                        for rb in range(row_blocks):
+                            row = rb * stride_rows + hm
+                            total = None
+                            for dr in range(3):
+                                for dc in range(3):
+                                    term = source[row + dr][b + dc] * taps[dr][dc]
+                                    total = term if total is None else total + term
+                            parts.append(gelu_scaled(total))
+                        place = (hm * span + pair + b) * members
+                        depth[place : place + members, lane : lane + LANES] = jnp.concatenate(
+                            parts, axis=0
+                        ).astype(jnp.bfloat16)
+        if half == 0:
+            acc[...] = acc[...] + jnp.dot(
+                depth_a[...], project_new_ref[...], preferred_element_type=jnp.float32
+            )
 
     @pl.when(step == pl.num_programs(0) - 1)
     def _():
         gain = gain_ref[...]
-        members = row_blocks * blocks
+        acc[...] = acc[...] + jnp.dot(
+            depth_b[...], project_last_ref[...], preferred_element_type=jnp.float32
+        )
         for hm in range(stride_rows):
             for b in range(span):
                 pieces = []
                 for rb in range(row_blocks):
-                    begin = (b + 1) * blocks
+                    begin = (chunk * span + b + 1) * blocks
                     low = begin - begin % 16
-                    pair = ordered[rb * stride_rows + hm + 1, low : low + 16, :].astype(jnp.float32)
+                    pair = ordered_ref[rb * stride_rows + hm, low : low + 16, :].astype(jnp.float32)
                     pieces.append(pair[begin - low : begin - low + blocks])
                 place = (hm * span + b) * members
-                mixed = jnp.concatenate(pieces, axis=0) + acc[place : place + members, :]
+                branch = acc[place : place + members, :]
+                mixed = jnp.concatenate(pieces, axis=0) + branch * BRANCH_SCALE
                 mixed = mixed.astype(jnp.bfloat16)
                 mbconv_ref[place : place + members, :] = mixed
                 mixed = mixed.astype(jnp.float32)
@@ -180,49 +278,58 @@
                 ).astype(jnp.bfloat16)
 
 
-def mbconv_chunk(chunk, span, stride_rows, stride_cols, col, tokens, halos, weights):
-    rows, cols, channels = tokens.shape
+def mbconv_chunk(chunk, span, stride_rows, stride_cols, col, halos, ordered, own, weights):
+    rows = own.shape[1]
+    cols, channels = halos[0].shape[1:]
     expand_weight, taps, project_weight, gain = weights
     hidden = expand_weight.shape[1]
-    block = 256 if hidden % 256 == 0 else hidden
     blocks = cols // stride_cols
     count = rows * span * blocks
     size = (span + 2) * blocks
+    last = hidden // BLOCK - 1
 
     def whole(array):
         return pl.BlockSpec(array.shape, lambda i, c: (0,) * array.ndim)
 
     grid_spec = pltpu.PrefetchScalarGridSpec(
         num_scalar_prefetch=1,
-        grid=(hidden // block,),
-        in_specs=[whole(tokens)]
-        + [whole(h) for h in halos]
+        grid=(hidden // (2 * BLOCK),),
+        in_specs=[whole(h) for h in halos]
         + [
-            pl.BlockSpec((channels, block), lambda i, c: (0, i)),
-            pl.BlockSpec((taps.shape[0], block), lambda i, c: (0, i)),
-            pl.BlockSpec((block, channels), lambda i, c: (i, 0)),
+            whole(ordered),
+            pl.BlockSpec((2, rows, size, BLOCK), lambda i, c: (i, 0, 0, 0)),
+            pl.BlockSpec((channels, 2 * BLOCK), lambda i, c: (0, i)),
+            pl.BlockSpec((3, 3, 2 * BLOCK), lambda i, c: (0, 0, i)),
+            pl.BlockSpec((BLOCK, channels), lambda i, c: (jnp.maximum(2 * i - 1, 0), 0)),
+            pl.BlockSpec((BLOCK, channels), lambda i, c: (2 * i, 0)),
+            pl.BlockSpec((BLOCK, channels), lambda i, c: (last, 0)),
             whole(gain),
         ],
         out_specs=[pl.BlockSpec((count, channels), lambda i, c: (0, 0))] * 2,
         scratch_shapes=[
-            pltpu.VMEM((rows + 2, size, channels), jnp.bfloat16),
-            pltpu.VMEM((rows + 2, span + 2, blocks, block), jnp.float32),
-            pltpu.VMEM((count, block), jnp.bfloat16),
+            pltpu.VMEM((2, size, channels), jnp.bfloat16),
+            pltpu.VMEM((2, 2, span + 2, blocks, BLOCK), jnp.float32),
+            pltpu.VMEM((count, BLOCK), jnp.bfloat16),
+            pltpu.VMEM((count, BLOCK), jnp.bfloat16),
             pltpu.VMEM((count, channels), jnp.float32),
         ],
     )
     return pl.pallas_call(
         functools.partial(
-            mbconv_kernel, chunk=chunk, span=span, stride_cols=stride_cols, stride_rows=stride_rows
+            mbconv_kernel, chunk=chunk, span=span, stride_cols=stride_cols, stride_rows=stride_rows,
+            rows=rows,
         ),
         grid_spec=grid_spec,
         out_shape=[jax.ShapeDtypeStruct((count, channels), jnp.bfloat16)] * 2,
         compiler_params=pltpu.CompilerParams(dimension_semantics=("arbitrary",)),
         cost_estimate=pl.CostEstimate(
-            flops=4 * count * channels * hidden * 2, bytes_accessed=8 << 20, transcendentals=0
+            flops=4 * count * channels * hidden, bytes_accessed=8 << 20, transcendentals=0
         ),
         name=f"mbconv_{chunk}",
-    )(col, tokens, *halos, expand_weight, taps, project_weight, gain)
+    )(
+        col, *halos, ordered, own, expand_weight, taps, project_weight, project_weight,
+        project_weight, gain,
+    )
 
 
 def attend_kernel(x_ref, attend_ref, output_ref, out_ref):
@@ -234,22 +341,21 @@
     lane = lax.broadcasted_iota(jnp.int32, (members, LANES), 1) // HEAD_DIM
     ones = jnp.ones((members, LANES), jnp.bfloat16)
     tiles = []
+    projected = [
+        jnp.dot(
+            x, attend_ref[:, begin : begin + BLOCK], preferred_element_type=jnp.float32
+        )
+        for begin in range(0, 3 * channels, BLOCK)
+    ]
+
+    def cut(begin):
+        return projected[begin // BLOCK][:, begin % BLOCK : begin % BLOCK + LANES]
+
     for tile in range(channels // LANES):
         begin = tile * LANES
-        query = jnp.dot(
-            x, attend_ref[:, begin : begin + LANES], preferred_element_type=jnp.float32
-        )
-        query = (query * scale).astype(jnp.bfloat16)
-        key = jnp.dot(
-            x,
-            attend_ref[:, channels + begin : channels + begin + LANES],
-            preferred_element_type=jnp.float32,
-        ).astype(jnp.bfloat16)
-        value = jnp.dot(
-            x,
-            attend_ref[:, 2 * channels + begin : 2 * channels + begin + LANES],
-            preferred_element_type=jnp.float32,
-        ).astype(jnp.bfloat16)
+        query = (cut(begin) * scale).astype(jnp.bfloat16)
+        key = cut(channels + begin).astype(jnp.bfloat16)
+        value = cut(2 * channels + begin).astype(jnp.bfloat16)
         upper = None
         for head in range(fold):
             inside = lane == head
@@ -374,24 +480,20 @@
     across = lambda pairs: [
         (f * col_count + c, t * col_count + 1 - c) for f, t in pairs for c in range(col_count)
     ]
-    up = lax.ppermute(tokens[rows - 1 :], "row", ups)
-    down = lax.ppermute(tokens[:1], "row", downs)
     side = lax.ppermute(edge, "col", [(0, 1), (1, 0)])
     side_up = lax.ppermute(edge[rows - 1 :], both, across(ups))
     side_down = lax.ppermute(edge[:1], both, across(downs))
-    halos = (up, down, side, side_up, side_down)
-    weights = (
-        expand_weight,
-        depth_kernel.reshape(9, -1),
-        project_weight,
-        norm_gain.reshape(1, -1),
-    )
+    up = lax.ppermute(tokens[rows - 1 :], "row", ups)
+    down = lax.ppermute(tokens[:1], "row", downs)
+    halos = (up, down, side_up, side_down)
+    weights = (expand_weight, depth_kernel, project_weight, norm_gain.reshape(1, -1))
     col_scalar = col.astype(jnp.int32).reshape(1)
+    ordered, *own = expand_rows(col_scalar, tokens, side, expand_weight, stride_cols, span)
 
     pieces, keeps = [], []
     for chunk in range(CHUNKS):
         normed, mbconv = mbconv_chunk(
-            chunk, span, stride_rows, stride_cols, col_scalar, tokens, halos, weights
+            chunk, span, stride_rows, stride_cols, col_scalar, halos, ordered, own[chunk], weights
         )
         keeps.append(mbconv)
         pieces.append(
@@ -411,7 +513,7 @@
     return out.reshape(rows, cols, channels)
 
 
-def fits(tokens_shape, row_count, col_count):
+def fits(tokens_shape, hidden, row_count, col_count):
     rows, cols, channels = tokens_shape
     stride_rows = rows * row_count // GRID
     stride_cols = cols * col_count // GRID
@@ -423,14 +525,16 @@
         and cols // stride_cols == SUBLANES
         and rows // stride_rows == 2
         and groups % (CHUNKS * row_count * col_count) == 0
-        and channels % LANES == 0
+        and channels % BLOCK == 0
+        and hidden % (2 * BLOCK) == 0
+        and stride_cols // CHUNKS % 2 == 0
     )
 
 
 def local(
     tokens, expand_weight, depth_kernel, project_weight, norm_gain, attend_weight, output_weight
 ):
-    if fits(tokens.shape, lax.axis_size("row"), lax.axis_size("col")):
+    if fits(tokens.shape, expand_weight.shape[1], lax.axis_size("row"), lax.axis_size("col")):
         return chunked(
             tokens,
             expand_weight,

time: 114 us -> 114 us (level)
  waiting for transfers between devices: 24.3 us -> 31.9 us
  Pallas kernels: 49.6 us -> 44.3 us
  starting transfers between devices: 33.7 us -> 32.2 us
    pallas_call x2, Pallas kernels: 27.2 us -> 20 us  [mbconv_chunk(): pl.pallas_call(functools.partial(mbconv_kernel, chunk=chunk, span=span, s...]
    pallas_call x0 -> x1, Pallas kernels: none -> 6.77 us  [expand_rows(): pl.pallas_call(functools.partial(expand_kernel, stride_cols=stride_cols,...]
    all_to_all x2, waiting for transfers between devices: 6.07 us -> 12.1 us  [chunked(): lax.all_to_all(normed.reshape(devices, -1, channels), both, split_axis=0,...]
    pallas_call x2, Pallas kernels: 17.7 us -> 12.8 us  [attend_chunk(): pl.pallas_call(attend_kernel, grid=(items,), in_specs=[spec, pl.BlockSpec...]
    all_to_all x2, waiting for transfers between devices: 17.3 us -> 19.7 us  [chunked(): lax.all_to_all(result, both, split_axis=0, concat_axis=0, tiled=True)]
    reshape x1 -> x0, local copies, waits for them, and re-layouts: 1.58 us -> none  [chunked(): depth_kernel.reshape(9, -1)]
  transfers between devices with their start and end apart: 9 -> 9, of which waited for: 5 -> 4; matrix products, arithmetic and copies ran while one was open for 2% -> 1% of each run, Pallas kernels for 30% -> 28%
where the time goes in v2:
time: 114 us; the launch traced here: 113 us
  Pallas kernels  44.3 us (39%)
  starting transfers between devices  32.2 us (28%)
  waiting for transfers between devices  31.9 us (28%)
  local copies, waits for them, and re-layouts  4.04 us (4%)
    pallas_call x2, Pallas kernels, mbconv_chunk(): pl.pallas_call(functools.partial(mbconv_kernel, chunk=chunk, span=span, s...  20 us
    all_to_all x2, waiting for transfers between devices, chunked(): lax.all_to_all(result, both, split_axis=0, concat_axis=0, tiled=True)  19.7 us
    pallas_call x2, Pallas kernels, attend_chunk(): pl.pallas_call(attend_kernel, grid=(items,), in_specs=[spec, pl.BlockSpec...  12.8 us
    all_to_all x2, waiting for transfers between devices, chunked(): lax.all_to_all(normed.reshape(devices, -1, channels), both, split_axis=0,...  12.1 us
    all_to_all x2, starting transfers between devices, chunked(): lax.all_to_all(normed.reshape(devices, -1, channels), both, split_axis=0,...  10.7 us
    all_to_all x2, starting transfers between devices, chunked(): lax.all_to_all(result, both, split_axis=0, concat_axis=0, tiled=True)  8.33 us
    pallas_call x1, Pallas kernels, expand_rows(): pl.pallas_call(functools.partial(expand_kernel, stride_cols=stride_cols,...  6.77 us
    ppermute x1, starting transfers between devices, chunked(): up = lax.ppermute(tokens[rows - 1:], 'row', ups)  5.07 us
  transfers between devices with their start and end apart: 9, of which 4 were waited for; matrix products, arithmetic and copies ran while one was open for 1% of the time, Pallas kernels for 28%

profile of v2, /device:TPU:0, one launch (start us, length us, event | category | flops | bytes accessed | tf_op | source)
XLA Modules:
  0.0 112.6 jit_solution(17226507781158921897)
XLA Ops:
  0.0 0.8 fusion
  0.8 0.6 collective-permute-start.4
  1.4 1.1 fusion.1
  2.4 1.3 %collective-permute-start.1 = (bf16[1,256,512]{2,1,0:T(8,128)(2,1)S(1)}, bf16[1,256,512]{2,1,0:T(8,128)(2,1)S(1)}, u32[]{:S(2)}, u32[]{:S(2)}) collective-permute-start(bf16[1,256,512]{2,1,0:T(8,128)(2,1)S(1)} %get-tuple-element.21), channel_id=1, source_target_pairs={{2,0},{4,2},{6,4},{8,6},{10,8},{12,10},{14,12},{3,1},{5,3},{7,5},{... | collective-permute-start | bytes 786440 | tf_op jit(solution)/shard_map/ppermute | solution.py:487
  3.7 5.1 %collective-permute-start = (bf16[1,256,512]{2,1,0:T(8,128)(2,1)S(1)}, bf16[1,256,512]{2,1,0:T(8,128)(2,1)S(1)}, u32[]{:S(2)}, u32[]{:S(2)}) collective-permute-start(bf16[1,256,512]{2,1,0:T(8,128)(2,1)S(1)} %get-tuple-element.22), channel_id=1, source_target_pairs={{0,2},{2,4},{4,6},{6,8},{8,10},{10,12},{12,14},{1,3},{3,5},{5,7},{... | collective-permute-start | bytes 786440 | tf_op jit(solution)/shard_map/ppermute | solution.py:486
  8.8 1.3 %collective-permute-start.3 = (bf16[1,512]{1,0:T(2,128)(2,1)S(1)}, bf16[1,512]{1,0:T(2,128)(2,1)S(1)}, u32[]{:S(2)}, u32[]{:S(2)}) collective-permute-start(bf16[1,512]{1,0:T(2,128)(2,1)S(1)} %get-tuple-element.23), channel_id=1, source_target_pairs={{2,1},{3,0},{4,3},{5,2},{6,5},{7,4},{8,7},{9,6},{10,9},{11,8},{12,... | collective-permute-start | bytes 3080 | tf_op jit(solution)/shard_map/ppermute | solution.py:485
  10.1 5.0 %collective-permute-start.2 = (bf16[1,512]{1,0:T(2,128)(2,1)S(1)}, bf16[1,512]{1,0:T(2,128)(2,1)S(1)}, u32[]{:S(2)}, u32[]{:S(2)}) collective-permute-start(bf16[1,512]{1,0:T(2,128)(2,1)S(1)} %get-tuple-element.24), channel_id=1, source_target_pairs={{0,3},{1,2},{2,5},{3,4},{4,7},{5,6},{6,9},{7,8},{8,11},{9,10},{10,... | collective-permute-start | bytes 3080 | tf_op jit(solution)/shard_map/ppermute | solution.py:484
  15.1 0.6 copy-done.8
  15.7 6.8 %expand.1 = (bf16[4,272,512]{2,1,0:T(8,128)(2,1)}, bf16[8,4,144,256]{3,2,1,0:T(8,128)(2,1)}, bf16[8,4,144,256]{3,2,1,0:T(8,128)(2,1)}) custom-call(s32[1]{0:T(128)} %bitcast.col_ref, bf16[4,256,512]{2,1,0:T(8,128)(2,1)} %x_ref.1, bf16[4,512]{1,0:T(4,128)(2,1)} %copy-done.8, bf16[512,2048]{1,0:T(8,128)(2,1)} %expand_ref.5), custom_call_target="tpu_custom_call" | custom-call | flops 2281701376 | bytes 8388608 | tf_op jit(solution)/shard_map/expand/pallas_call | solution.py:144
  23.3 10.0 %mbconv_0.1 = (bf16[512,512]{1,0:T(8,128)(2,1)}, bf16[512,512]{1,0:T(8,128)(2,1)}) custom-call(s32[1]{0:T(128)} %bitcast.col_ref, bf16[1,256,512]{2,1,0:T(8,128)(2,1)} %copy-done.3, bf16[1,256,512]{2,1,0:T(8,128)(2,1)} %copy-done.2, bf16[1,512]{1,0:T(2,128)(2,1)} %copy-done.7, bf16[1,512]{1,0:T(2,128)(2,1)} %copy-done.6, ...), custom_call_target="tpu_custom_call" | custom-call | flops 2147483648 | bytes 8388608 | tf_op jit(solution)/shard_map/mbconv_0/pallas_call | solution.py:317
  33.3 6.5 %all-to-all-start.2 = ((bf16[16,32,512]{2,1,0:T(8,128)(2,1)}), bf16[16,32,512]{2,1,0:T(8,128)(2,1)S(1)}, u32[]{:S(2)}, u32[]{:S(2)}) async-start(bf16[16,32,512]{2,1,0:T(8,128)(2,1)} %bitcast.11), calls=%async_computation.2 | async-start | bytes 1048576 | tf_op jit(solution)/shard_map/all_to_all | solution.py:500
  39.8 10.0 %mbconv_1.1 = (bf16[512,512]{1,0:T(8,128)(2,1)}, bf16[512,512]{1,0:T(8,128)(2,1)}) custom-call(s32[1]{0:T(128)} %bitcast.col_ref, bf16[1,256,512]{2,1,0:T(8,128)(2,1)} %copy-done.3, bf16[1,256,512]{2,1,0:T(8,128)(2,1)} %copy-done.2, bf16[1,512]{1,0:T(2,128)(2,1)} %copy-done.7, bf16[1,512]{1,0:T(2,128)(2,1)} %copy-done.6, ...), custom_call_target="tpu_custom_call" | custom-call | flops 2147483648 | bytes 8388608 | tf_op jit(solution)/shard_map/mbconv_1/pallas_call | solution.py:317
  49.8 4.3 %all-to-all-done.2.x_ref = bf16[16,32,512]{2,1,0:T(8,128)(2,1)S(1)} async-done(((bf16[16,32,512]{2,1,0:T(8,128)(2,1)}), bf16[16,32,512]{2,1,0:T(8,128)(2,1)S(1)}, u32[]{:S(2)}, u32[]{:S(2)}) %all-to-all-start.2) | async-done | bytes 524320 | tf_op jit(solution)/shard_map/all_to_all | solution.py:500
  54.1 4.2 %all-to-all-start = ((bf16[16,32,512]{2,1,0:T(8,128)(2,1)}), bf16[16,32,512]{2,1,0:T(8,128)(2,1)S(1)}, u32[]{:S(2)}, u32[]{:S(2)}) async-start(bf16[16,32,512]{2,1,0:T(8,128)(2,1)} %bitcast.10), calls=%async_computation | async-start | bytes 1048576 | tf_op jit(solution)/shard_map/all_to_all | solution.py:500
  58.3 6.4 %attend_0.1 = bf16[16,32,512]{2,1,0:T(8,128)(2,1)} custom-call(bf16[16,32,512]{2,1,0:T(8,128)(2,1)} %copy-done.4, bf16[512,1536]{1,0:T(8,128)(2,1)} %attend_ref.3, bf16[512,512]{1,0:T(8,128)(2,1)} %output_ref.3), custom_call_target="tpu_custom_call" | custom-call | flops 1610612736 | bytes 4194304 | tf_op jit(solution)/shard_map/attend_0/pallas_call | solution.py:390
  64.7 7.9 %all-to-all-done.x_ref = bf16[16,32,512]{2,1,0:T(8,128)(2,1)S(1)} async-done(((bf16[16,32,512]{2,1,0:T(8,128)(2,1)}), bf16[16,32,512]{2,1,0:T(8,128)(2,1)S(1)}, u32[]{:S(2)}, u32[]{:S(2)}) %all-to-all-start) | async-done | bytes 524320 | tf_op jit(solution)/shard_map/all_to_all | solution.py:500
  72.5 4.2 %all-to-all-start.3 = ((bf16[16,32,512]{2,1,0:T(8,128)(2,1)}), bf16[16,32,512]{2,1,0:T(8,128)(2,1)S(1)}, u32[]{:S(2)}, u32[]{:S(2)}) async-start(bf16[16,32,512]{2,1,0:T(8,128)(2,1)} %attend_0.1), calls=%async_computation.3 | async-start | bytes 1048576 | tf_op jit(solution)/shard_map/all_to_all | solution.py:507
  76.7 6.4 %attend_1.1 = bf16[16,32,512]{2,1,0:T(8,128)(2,1)} custom-call(bf16[16,32,512]{2,1,0:T(8,128)(2,1)} %copy-done.5, bf16[512,1536]{1,0:T(8,128)(2,1)} %attend_ref.3, bf16[512,512]{1,0:T(8,128)(2,1)} %output_ref.3), custom_call_target="tpu_custom_call" | custom-call | flops 1610612736 | bytes 4194304 | tf_op jit(solution)/shard_map/attend_1/pallas_call | solution.py:390
  83.1 7.8 %all-to-all-done.3.refs_0_ = bf16[16,32,512]{2,1,0:T(8,128)(2,1)S(1)} async-done(((bf16[16,32,512]{2,1,0:T(8,128)(2,1)}), bf16[16,32,512]{2,1,0:T(8,128)(2,1)S(1)}, u32[]{:S(2)}, u32[]{:S(2)}) %all-to-all-start.3) | async-done | bytes 524320 | tf_op jit(solution)/shard_map/all_to_all | solution.py:507
  91.0 4.2 %all-to-all-start.1 = ((bf16[16,32,512]{2,1,0:T(8,128)(2,1)}), bf16[16,32,512]{2,1,0:T(8,128)(2,1)S(1)}, u32[]{:S(2)}, u32[]{:S(2)}) async-start(bf16[16,32,512]{2,1,0:T(8,128)(2,1)} %attend_1.1), calls=%async_computation.1 | async-start | bytes 1048576 | tf_op jit(solution)/shard_map/all_to_all | solution.py:507
  95.2 2.4 %finish_0.1.refs_2_ = bf16[4,8,32,512]{3,2,1,0:T(8,128)(2,1)} custom-call(bf16[16,32,512]{2,1,0:T(8,128)(2,1)} %copy-done, bf16[512,512]{1,0:T(8,128)(2,1)} %get-tuple-element.18.refs_1_), custom_call_target="tpu_custom_call" | custom-call | flops 134217728 | bytes 2097152 | tf_op jit(solution)/shard_map/finish_0/pallas_call | solution.py:443
  97.6 11.9 %all-to-all-done.1.refs_0_ = bf16[16,32,512]{2,1,0:T(8,128)(2,1)S(1)} async-done(((bf16[16,32,512]{2,1,0:T(8,128)(2,1)}), bf16[16,32,512]{2,1,0:T(8,128)(2,1)S(1)}, u32[]{:S(2)}, u32[]{:S(2)}) %all-to-all-start.1) | async-done | bytes 524320 | tf_op jit(solution)/shard_map/all_to_all | solution.py:507
  109.4 0.8 copy-done.1
  110.3 2.4 %finish_1.1 = bf16[4,8,32,512]{3,2,1,0:T(8,128)(2,1)} custom-call(bf16[16,32,512]{2,1,0:T(8,128)(2,1)} %copy-done.1, bf16[512,512]{1,0:T(8,128)(2,1)} %get-tuple-element.15.refs_1_, bf16[4,8,32,512]{3,2,1,0:T(8,128)(2,1)} %finish_0.1.refs_2_), custom_call_target="tpu_custom_call", output_to_operand_aliasing={{}: (2, {})} | custom-call | flops 134217728 | bytes 2097152 | tf_op jit(solution)/shard_map/finish_1/pallas_call | solution.py:443
  (23 shorter events, 0.8 us)
Async XLA Ops:
  0.8 14.3 %collective-permute-start.4 = (bf16[4,512]{1,0:T(4,128)(2,1)S(1)}, bf16[4,512]{1,0:T(4,128)(2,1)S(1)}, u32[]{:S(2)}, u32[]{:S(2)}) collective-permute-start(bf16[4,512]{1,0:T(4,128)(2,1)S(1)} %bitcast.12), channel_id=1, source_target_pairs={{0,1},{1,0},{2,3},{3,2},{4,5},{5,4},{6,7},{7,6},{8,9},{9,8},{10,11... | collective-permute-start | bytes 12296 | tf_op jit(solution)/shard_map/ppermute | solution.py:483
  2.4 20.1 %collective-permute-start.1 = (bf16[1,256,512]{2,1,0:T(8,128)(2,1)S(1)}, bf16[1,256,512]{2,1,0:T(8,128)(2,1)S(1)}, u32[]{:S(2)}, u32[]{:S(2)}) collective-permute-start(bf16[1,256,512]{2,1,0:T(8,128)(2,1)S(1)} %get-tuple-element.21), channel_id=1, source_target_pairs={{2,0},{4,2},{6,4},{8,6},{10,8},{12,10},{14,12},{3,1},{5,3},{7,5},{... | collective-permute-start | bytes 786440 | tf_op jit(solution)/shard_map/ppermute | solution.py:487
  3.7 18.8 %collective-permute-start = (bf16[1,256,512]{2,1,0:T(8,128)(2,1)S(1)}, bf16[1,256,512]{2,1,0:T(8,128)(2,1)S(1)}, u32[]{:S(2)}, u32[]{:S(2)}) collective-permute-start(bf16[1,256,512]{2,1,0:T(8,128)(2,1)S(1)} %get-tuple-element.22), channel_id=1, source_target_pairs={{0,2},{2,4},{4,6},{6,8},{8,10},{10,12},{12,14},{1,3},{3,5},{5,7},{... | collective-permute-start | bytes 786440 | tf_op jit(solution)/shard_map/ppermute | solution.py:486
  8.8 13.7 %collective-permute-start.3 = (bf16[1,512]{1,0:T(2,128)(2,1)S(1)}, bf16[1,512]{1,0:T(2,128)(2,1)S(1)}, u32[]{:S(2)}, u32[]{:S(2)}) collective-permute-start(bf16[1,512]{1,0:T(2,128)(2,1)S(1)} %get-tuple-element.23), channel_id=1, source_target_pairs={{2,1},{3,0},{4,3},{5,2},{6,5},{7,4},{8,7},{9,6},{10,9},{11,8},{12,... | collective-permute-start | bytes 3080 | tf_op jit(solution)/shard_map/ppermute | solution.py:485
  10.1 12.4 %collective-permute-start.2 = (bf16[1,512]{1,0:T(2,128)(2,1)S(1)}, bf16[1,512]{1,0:T(2,128)(2,1)S(1)}, u32[]{:S(2)}, u32[]{:S(2)}) collective-permute-start(bf16[1,512]{1,0:T(2,128)(2,1)S(1)} %get-tuple-element.24), channel_id=1, source_target_pairs={{0,3},{1,2},{2,5},{3,4},{4,7},{5,6},{6,9},{7,8},{8,11},{9,10},{10,... | collective-permute-start | bytes 3080 | tf_op jit(solution)/shard_map/ppermute | solution.py:484
  15.1 0.6 copy-start.8
  22.5 0.6 copy-start.6
  22.5 0.6 copy-start.7
  22.5 0.7 copy-start.2
  22.5 0.8 copy-start.3
  33.3 20.8 %all-to-all-start.2 = ((bf16[16,32,512]{2,1,0:T(8,128)(2,1)}), bf16[16,32,512]{2,1,0:T(8,128)(2,1)S(1)}, u32[]{:S(2)}, u32[]{:S(2)}) async-start(bf16[16,32,512]{2,1,0:T(8,128)(2,1)} %bitcast.11), calls=%async_computation.2 | async-start | bytes 1048576 | tf_op jit(solution)/shard_map/all_to_all | solution.py:500
  54.1 4.2 %copy-start.4 = (bf16[16,32,512]{2,1,0:T(8,128)(2,1)}, bf16[16,32,512]{2,1,0:T(8,128)(2,1)S(1)}, u32[]{:S(2)}) copy-start(bf16[16,32,512]{2,1,0:T(8,128)(2,1)S(1)} %all-to-all-done.2.x_ref) | copy-start | bytes 1572868
  54.1 18.4 %all-to-all-start = ((bf16[16,32,512]{2,1,0:T(8,128)(2,1)}), bf16[16,32,512]{2,1,0:T(8,128)(2,1)S(1)}, u32[]{:S(2)}, u32[]{:S(2)}) async-start(bf16[16,32,512]{2,1,0:T(8,128)(2,1)} %bitcast.10), calls=%async_computation | async-start | bytes 1048576 | tf_op jit(solution)/shard_map/all_to_all | solution.py:500
  72.5 4.2 %copy-start.5 = (bf16[16,32,512]{2,1,0:T(8,128)(2,1)}, bf16[16,32,512]{2,1,0:T(8,128)(2,1)S(1)}, u32[]{:S(2)}) copy-start(bf16[16,32,512]{2,1,0:T(8,128)(2,1)S(1)} %all-to-all-done.x_ref) | copy-start | bytes 1572868
  72.5 18.4 %all-to-all-start.3 = ((bf16[16,32,512]{2,1,0:T(8,128)(2,1)}), bf16[16,32,512]{2,1,0:T(8,128)(2,1)S(1)}, u32[]{:S(2)}, u32[]{:S(2)}) async-start(bf16[16,32,512]{2,1,0:T(8,128)(2,1)} %attend_0.1), calls=%async_computation.3 | async-start | bytes 1048576 | tf_op jit(solution)/shard_map/all_to_all | solution.py:507
  91.0 4.2 %copy-start = (bf16[16,32,512]{2,1,0:T(8,128)(2,1)}, bf16[16,32,512]{2,1,0:T(8,128)(2,1)S(1)}, u32[]{:S(2)}) copy-start(bf16[16,32,512]{2,1,0:T(8,128)(2,1)S(1)} %all-to-all-done.3.refs_0_) | copy-start | bytes 1572868
  91.0 18.4 %all-to-all-start.1 = ((bf16[16,32,512]{2,1,0:T(8,128)(2,1)}), bf16[16,32,512]{2,1,0:T(8,128)(2,1)S(1)}, u32[]{:S(2)}, u32[]{:S(2)}) async-start(bf16[16,32,512]{2,1,0:T(8,128)(2,1)} %attend_1.1), calls=%async_computation.1 | async-start | bytes 1048576 | tf_op jit(solution)/shard_map/all_to_all | solution.py:507
  109.4 0.8 copy-start.1

commit v3 on v0

--- a/solution.py
+++ b/solution.py
@@ -1,13 +1,27 @@
+import functools
 import math
 
 import jax
 import jax.numpy as jnp
 from jax import lax
+from jax.experimental import pallas as pl
+from jax.experimental.pallas import tpu as pltpu
 from jax.sharding import PartitionSpec as P
+
 
 HEADS = 16
 HEAD_DIM = 32
 GRID = 16
+HALVES = 2
+SUBLANES = 8
+LANES = 128
+LOG2E = 1.4426950408889634
+BLOCK = 256
+GELU_ONE = math.sqrt(2 / math.pi)
+GELU_THREE = 0.044715 * GELU_ONE
+CUBE_ROOT = GELU_THREE ** (1 / 3)
+TAP_SCALE = 0.5 * CUBE_ROOT
+BRANCH_SCALE = 0.5 / CUBE_ROOT
 
 
 def extended(cells, sides, width):
@@ -31,6 +45,14 @@
     return jax.nn.gelu(values, approximate=True)
 
 
+def gelu_twice(v):
+    return v + v * jnp.tanh(v * (GELU_ONE + GELU_THREE * (v * v)))
+
+
+def gelu_scaled(w):
+    return w + w * jnp.tanh(w * (GELU_ONE / CUBE_ROOT + w * w))
+
+
 def expand_tile(inputs, expand_weight):
     shape = inputs.shape
     product = jnp.dot(
@@ -67,9 +89,475 @@
     return result.reshape(count, members, channels)
 
 
+def arrange_kernel(place_ref, *refs, stride_cols, share):
+    count = len(refs) // 3
+    cols, _ = refs[0].shape[1:]
+    size = refs[-1].shape[1]
+    col = place_ref[0]
+    at = lax.broadcasted_iota(jnp.int32, (size, cols), 0)
+    want = (at % GRID) * stride_cols + at // GRID + (col * share - 1)
+    index = lax.broadcasted_iota(jnp.int32, (size, cols), 1)
+    select_own = (index + col * cols == want).astype(jnp.bfloat16)
+    select_other = (index + (1 - col) * cols == want).astype(jnp.bfloat16)
+    for own_ref, other_ref, ordered_ref in zip(refs[:count], refs[count : 2 * count], refs[2 * count :]):
+        for row in range(own_ref.shape[0]):
+            picked = jnp.dot(select_own, own_ref[row], preferred_element_type=jnp.float32) + jnp.dot(
+                select_other, other_ref[row], preferred_element_type=jnp.float32
+            )
+            ordered_ref[row] = picked.astype(jnp.bfloat16)
+
+
+VMEM = pl.BlockSpec(memory_space=pltpu.VMEM)
+SMEM = pl.BlockSpec(memory_space=pltpu.SMEM)
+MIB = 1 << 20
+
+
+def call(kernel, place, operands, shapes, flops, limit, scratch=(), **options):
+    return pl.pallas_call(
+        kernel,
+        in_specs=[SMEM] + [VMEM] * len(operands),
+        out_specs=[VMEM] * len(shapes),
+        out_shape=[jax.ShapeDtypeStruct(shape, jnp.bfloat16) for shape in shapes],
+        scratch_shapes=list(scratch),
+        compiler_params=pltpu.CompilerParams(vmem_limit_bytes=limit),
+        cost_estimate=pl.CostEstimate(flops=flops, bytes_accessed=1 << 20, transcendentals=0),
+    )(place, *operands)
+
+
+def arrange(place, owns, others, stride_cols, share):
+    cols, channels = owns[0].shape[1:]
+    size = (share + 2) * GRID
+    return call(
+        functools.partial(arrange_kernel, stride_cols=stride_cols, share=share),
+        place,
+        [*owns, *others],
+        [(own.shape[0], size, channels) for own in owns],
+        sum(4 * own.shape[0] * size * cols * channels for own in owns),
+        8 * MIB,
+    )
+
+
+def expand_kernel(place_ref, ordered_ref, expand_ref, expanded_ref):
+    rows = ordered_ref.shape[0]
+    hidden = expand_ref.shape[1]
+
+    def step(index, carry):
+        for half in range(2):
+            lanes = pl.ds(pl.multiple_of(index * 2 * BLOCK + half * BLOCK, BLOCK), BLOCK)
+            for row in range(rows):
+                product = jnp.dot(
+                    ordered_ref[row], expand_ref[:, lanes], preferred_element_type=jnp.float32
+                )
+                expanded_ref[2 * index + half, row] = gelu_twice(product).astype(jnp.bfloat16)
+        return carry
+
+    lax.fori_loop(0, hidden // (2 * BLOCK), step, 0)
+
+
+def expand_rows(place, ordered, expand_weight):
+    rows, size, channels = ordered.shape
+    hidden = expand_weight.shape[1]
+    return call(
+        expand_kernel,
+        place,
+        [ordered, expand_weight],
+        [(hidden // BLOCK, rows, size, BLOCK)],
+        2 * rows * size * channels * hidden,
+        8 * MIB,
+    )[0]
+
+
+def mbconv_kernel(
+    place_ref, up_ref, down_ref, ordered_ref, own_ref,
+    expand_ref, taps_ref, project_ref, gain_ref,
+    mbconv_ref, *rest,
+    far, span, stride_rows,
+):
+    *normed_refs, edge_rows, depth_a, depth_b, acc = rest
+    hidden = expand_ref.shape[1]
+    rows = ordered_ref.shape[0]
+    row_blocks = rows // stride_rows
+    owners = len(normed_refs)
+    spot_half = place_ref[1] // owners
+    half_at = 1 - spot_half if far else spot_half
+    begin = pl.multiple_of(half_at * (span * GRID), GRID)
+    part = (span + 2) * GRID
+
+    depth_b[...] = jnp.zeros_like(depth_b)
+    acc[...] = jnp.zeros_like(acc)
+
+    def step(index, carry):
+        for half, depth in ((0, depth_a), (1, depth_b)):
+            block = 2 * index + half
+            for side, ref in enumerate((up_ref, down_ref)):
+                product = jnp.dot(
+                    ref[0, pl.ds(begin, part), :],
+                    expand_ref[:, pl.ds(block * BLOCK, BLOCK)],
+                    preferred_element_type=jnp.float32,
+                )
+                edge_rows[half, side] = gelu_twice(product)
+            if half == 0:
+                acc[...] = acc[...] + jnp.dot(
+                    depth_b[...],
+                    project_ref[pl.ds(jnp.maximum(block - 1, 0) * BLOCK, BLOCK), :],
+                    preferred_element_type=jnp.float32,
+                )
+            for lane in range(0, BLOCK, LANES):
+                lanes = slice(lane, lane + LANES)
+                taps = [
+                    [
+                        taps_ref[dr, dc : dc + 1, pl.ds(block * BLOCK + lane, LANES)]
+                        * TAP_SCALE
+                        for dc in range(3)
+                    ]
+                    for dr in range(3)
+                ]
+                for pair in range(0, span, 2):
+                    parts = {}
+                    for low in range(0, GRID, SUBLANES):
+                        source = []
+                        for row in range(rows + 2):
+                            tiles = []
+                            for k in range(4):
+                                at = (pair + k) * GRID
+                                if row == 0 or row == rows + 1:
+                                    at += low
+                                    tiles.append(edge_rows[half, min(row, 1), at : at + SUBLANES, lanes])
+                                else:
+                                    tile = own_ref[block, row - 1, pl.ds(begin + at, GRID), lanes]
+                                    tiles.append(tile.astype(jnp.float32)[low : low + SUBLANES])
+                            source.append(tiles)
+                        for b in (0, 1):
+                            for row in range(rows):
+                                total = None
+                                for dr in range(3):
+                                    for dc in range(3):
+                                        term = source[row + dr][b + dc] * taps[dr][dc]
+                                        total = term if total is None else total + term
+                                parts.setdefault((row, b), []).append(gelu_scaled(total))
+                    for (row, b), tiles in parts.items():
+                        spot = ((row % stride_rows) * span + pair + b) * row_blocks + row // stride_rows
+                        depth[spot * GRID : (spot + 1) * GRID, lanes] = jnp.concatenate(
+                            tiles, axis=0
+                        ).astype(jnp.bfloat16)
+            if half == 0:
+                acc[...] = acc[...] + jnp.dot(
+                    depth_a[...],
+                    project_ref[pl.ds(block * BLOCK, BLOCK), :],
+                    preferred_element_type=jnp.float32,
+                )
+        return carry
+
+    lax.fori_loop(0, hidden // (2 * BLOCK), step, 0)
+
+    gain = gain_ref[...]
+    acc[...] = acc[...] + jnp.dot(
+        depth_b[...],
+        project_ref[hidden - BLOCK : hidden, :],
+        preferred_element_type=jnp.float32,
+    )
+    members = row_blocks * GRID
+    per_row = stride_rows * span // owners
+    for k, normed_ref in enumerate(normed_refs):
+        owner = (place_ref[1] % owners) ^ k
+        hm = owner // (owners // stride_rows)
+        first = (owner % (owners // stride_rows)) * per_row
+        for item in range(per_row):
+            for rb in range(row_blocks):
+                spot = pl.multiple_of((owner * per_row + item) * members + rb * GRID, GRID)
+                column = pl.multiple_of(begin + (first + item + 1) * GRID, GRID)
+                tokens = ordered_ref[rb * stride_rows + hm, pl.ds(column, GRID), :]
+                mixed = tokens.astype(jnp.float32) + acc[pl.ds(spot, GRID), :] * BRANCH_SCALE
+                mixed = mixed.astype(jnp.bfloat16)
+                mbconv_ref[pl.ds(spot, GRID), :] = mixed
+                mixed = mixed.astype(jnp.float32)
+                center = jnp.mean(mixed, axis=-1, keepdims=True)
+                moved = mixed - center
+                spread = jnp.mean(moved * moved, axis=-1, keepdims=True)
+                to = item * members + rb * GRID
+                normed_ref[to : to + GRID, :] = (
+                    moved * lax.rsqrt(spread + 1e-05) * gain
+                ).astype(jnp.bfloat16)
+
+
+def mbconv_half(far, span, stride_rows, owners, place, up, down, ordered, own, weights):
+    rows, _, channels = ordered.shape
+    hidden = weights[0].shape[1]
+    count = rows * span * GRID
+    part = (span + 2) * GRID
+    mbconv, *normed = call(
+        functools.partial(mbconv_kernel, far=far, span=span, stride_rows=stride_rows),
+        place,
+        [up, down, ordered, own, *weights],
+        [(count, channels)] + [(count // owners, channels)] * owners,
+        4 * count * channels * hidden,
+        8 * MIB,
+        [
+            pltpu.VMEM((2, 2, part, BLOCK), jnp.float32),
+            pltpu.VMEM((count, BLOCK), jnp.bfloat16),
+            pltpu.VMEM((count, BLOCK), jnp.bfloat16),
+            pltpu.VMEM((count, channels), jnp.float32),
+        ],
+    )
+    return mbconv, normed
+
+
+def attend_kernel(place_ref, *refs, per, far, count):
+    x_refs = refs[:count]
+    attend_ref, output_ref = refs[-2 - count - far], refs[-1 - count - far]
+    out_refs = refs[-count - far :][:count]
+    channels = x_refs[0].shape[1]
+    scale = LOG2E / math.sqrt(HEAD_DIM)
+    fold = LANES // HEAD_DIM
+    kv_ref = refs[-1] if far else refs[count]
+    members = kv_ref.shape[1]
+    key_lane = lax.broadcasted_iota(jnp.int32, (members, LANES), 1) // HEAD_DIM
+    query_lane = lax.broadcasted_iota(jnp.int32, (count * per, LANES), 1) // HEAD_DIM
+    ones = jnp.ones((members, LANES), jnp.bfloat16)
+
+    def step(item, carry):
+        spot = pl.ds(pl.multiple_of(item * per, per), per)
+        x = jnp.concatenate([ref[spot, :] for ref in x_refs], axis=0)
+        if far:
+            everything = jnp.concatenate(
+                [x] + [ref[spot, :] for ref in refs[count : -2 - count - far]], axis=0
+            )
+            for begin in range(0, 2 * channels, BLOCK):
+                kv_ref[item, :, begin : begin + BLOCK] = jnp.dot(
+                    everything,
+                    attend_ref[:, channels + begin : channels + begin + BLOCK],
+                    preferred_element_type=jnp.float32,
+                ).astype(jnp.bfloat16)
+        queries = [
+            jnp.dot(x, attend_ref[:, begin : begin + BLOCK], preferred_element_type=jnp.float32)
+            for begin in range(0, channels, BLOCK)
+        ]
+        tiles = []
+        for begin in range(0, channels, LANES):
+            query = queries[begin // BLOCK][:, begin % BLOCK : begin % BLOCK + LANES]
+            query = (query * scale).astype(jnp.bfloat16)
+            key = kv_ref[item, :, begin : begin + LANES]
+            value = kv_ref[item, :, channels + begin : channels + begin + LANES]
+            upper = None
+            for head in range(fold):
+                key_head = jnp.where(key_lane == head, key, jnp.zeros_like(key))
+                value_head = jnp.where(key_lane == head, value, jnp.zeros_like(value))
+                scores = lax.dot_general(
+                    query, key_head, (((1,), (1,)), ((), ())), preferred_element_type=jnp.float32
+                )
+                top = jnp.max(scores, axis=-1, keepdims=True)
+                weight = jnp.exp2(scores - top).astype(jnp.bfloat16)
+                mixed = jnp.dot(
+                    weight,
+                    jnp.concatenate([value_head, ones], axis=1),
+                    preferred_element_type=jnp.float32,
+                )
+                if upper is None:
+                    upper, lower = mixed[:, :LANES], mixed[:, LANES:]
+                else:
+                    upper = upper + mixed[:, :LANES]
+                    lower = jnp.where(query_lane == head, mixed[:, LANES:], lower)
+            tiles.append((upper / lower).astype(jnp.bfloat16))
+        heads_out = jnp.concatenate(tiles, axis=1)
+        result = jnp.dot(heads_out, output_ref[...], preferred_element_type=jnp.float32)
+        result = result.astype(jnp.bfloat16)
+        for index, ref in enumerate(out_refs):
+            ref[spot, :] = result[index * per : (index + 1) * per]
+        return carry
+
+    lax.fori_loop(0, x_refs[0].shape[0] // per, step, 0)
+
+
+def attend_half(place, pieces, others, far, per, attend_weight, output_weight):
+    size, channels = pieces[0].shape
+    items = size // per
+    members = 2 * len(pieces) * per
+    shapes = [p.shape for p in pieces]
+    if far:
+        shapes.append((items, members, 2 * channels))
+    return call(
+        functools.partial(attend_kernel, per=per, far=far, count=len(pieces)),
+        place,
+        [*pieces, *others, attend_weight, output_weight],
+        shapes,
+        items * members * channels * (4 * channels + 4 * members),
+        8 * MIB,
+    )
+
+
+def add_kernel(place_ref, mbconv_ref, *refs):
+    *back_refs, keep_ref, send_ref = refs
+    owners = len(back_refs)
+    channels = mbconv_ref.shape[1]
+    is_left = place_ref[0] == 0
+    for k, back_ref in enumerate(back_refs):
+        size = back_ref.shape[0]
+        base = ((place_ref[1] % owners) ^ k) * size
+        for at in range(0, size, 2 * GRID):
+            spot = pl.multiple_of(base + at, 2 * GRID)
+            total = (
+                back_ref[at : at + 2 * GRID, :].astype(jnp.float32)
+                + mbconv_ref[pl.ds(spot, 2 * GRID), :].astype(jnp.float32)
+            ).reshape(2, 2, SUBLANES, channels)
+            left = total[:, 0].reshape(GRID, channels)
+            right = total[:, 1].reshape(GRID, channels)
+            to = pl.ds(pl.multiple_of(spot // 2, GRID), GRID)
+            keep_ref[to, :] = jnp.where(is_left, left, right).astype(jnp.bfloat16)
+            send_ref[to, :] = jnp.where(is_left, right, left).astype(jnp.bfloat16)
+
+
+def add_half(place, mbconv, backs):
+    count, channels = mbconv.shape
+    return call(
+        add_kernel, place, [mbconv, *backs], [(count // 2, channels)] * 2,
+        count * channels * 64, 4 * MIB,
+    )
+
+
+def finish_kernel(place_ref, keep_ref, got_ref, *rest, far, owners, span, stride_rows):
+    spot_half = place_ref[1] // owners
+    half_at = 1 - spot_half if far else spot_half
+    out_ref, placed_ref, sems = rest[-3:]
+    count, channels = keep_ref.shape
+    length = count // stride_rows
+    row_blocks = length // (span * SUBLANES)
+    at = lax.broadcasted_iota(jnp.int32, (length, length), 0)
+    b = at % span
+    a = (at // span) % SUBLANES
+    rb = at // (span * SUBLANES)
+    source = (b * row_blocks + rb) * SUBLANES + a
+    select = lax.broadcasted_iota(jnp.int32, (length, length), 1) == source
+    select = select.astype(jnp.bfloat16)
+    copies = []
+    for hm in range(stride_rows):
+        for ref, which in ((keep_ref, place_ref[0]), (got_ref, 1 - place_ref[0])):
+            placed = jnp.dot(
+                select, ref[hm * length : (hm + 1) * length, :], preferred_element_type=jnp.float32
+            ).astype(jnp.bfloat16)
+            placed = placed.reshape(row_blocks, SUBLANES, span, channels)
+            for rb_at in range(row_blocks):
+                placed_ref[rb_at * stride_rows + hm, :, which] = placed[rb_at]
+        for rb_at in range(row_blocks):
+            row = rb_at * stride_rows + hm
+            copies.append(
+                pltpu.make_async_copy(
+                    placed_ref.at[row], out_ref.at[row, :, :, half_at], sems.at[row]
+                )
+            )
+            copies[-1].start()
+    for copy in copies:
+        copy.wait()
+
+
+def finish_half(place, keep, got, previous, far, owners, rows, stride_rows, span):
+    channels = keep.shape[1]
+    anywhere = pl.BlockSpec(memory_space=pl.ANY)
+    operands = [keep, got]
+    previous = [] if previous is None else [previous]
+    return pl.pallas_call(
+        functools.partial(
+            finish_kernel, far=far, owners=owners, span=span, stride_rows=stride_rows
+        ),
+        in_specs=[SMEM, VMEM, VMEM] + [anywhere] * len(previous),
+        out_specs=anywhere,
+        out_shape=jax.ShapeDtypeStruct((rows, SUBLANES, 2, HALVES, span, channels), jnp.bfloat16),
+        scratch_shapes=[
+            pltpu.VMEM((rows, SUBLANES, 2, span, channels), jnp.bfloat16),
+            pltpu.SemaphoreType.DMA((rows,)),
+        ],
+        input_output_aliases={3: 0} if previous else {},
+        compiler_params=pltpu.CompilerParams(vmem_limit_bytes=4 * MIB),
+        cost_estimate=pl.CostEstimate(
+            flops=2 * keep.shape[0] * channels * 256, bytes_accessed=2 << 20, transcendentals=0
+        ),
+    )(place, *operands, *previous)
+
+
+def fits(tokens_shape, hidden, row_count, col_count):
+    rows, cols, channels = tokens_shape
+    stride_rows = rows * row_count // GRID
+    stride_cols = cols * col_count // GRID
+    owners = row_count // HALVES
+    return (
+        col_count == 2
+        and row_count & (row_count - 1) == 0
+        and stride_rows > 0
+        and rows == 2 * stride_rows
+        and cols == SUBLANES * stride_cols
+        and stride_cols % (2 * col_count * HALVES) == 0
+        and owners % stride_rows == 0
+        and stride_cols // (col_count * HALVES) % (owners // stride_rows) == 0
+        and channels % BLOCK == 0
+        and hidden % (2 * BLOCK) == 0
+    )
+
+
+def chunked(
+    tokens, expand_weight, depth_kernel, project_weight, norm_gain, attend_weight, output_weight
+):
+    rows, cols, channels = tokens.shape
+    row_count = lax.axis_size("row")
+    col_count = lax.axis_size("col")
+    stride_rows = rows * row_count // GRID
+    stride_cols = cols * col_count // GRID
+    share = stride_cols // col_count
+    span = share // HALVES
+    owners = row_count // HALVES
+    per = rows // stride_rows * GRID
+    swap = [(0, 1), (1, 0)]
+    place = jnp.stack([lax.axis_index("col"), lax.axis_index("row")]).astype(jnp.int32)
+
+    up = lax.ppermute(tokens[rows - 1 :], "row", [(r, r + 1) for r in range(row_count - 1)])
+    down = lax.ppermute(tokens[:1], "row", [(r + 1, r) for r in range(row_count - 1)])
+    other = lax.ppermute(tokens, "col", swap)
+    (ordered,) = arrange(place, [tokens], [other], stride_cols, share)
+    own = expand_rows(place, ordered, expand_weight)
+    halos = [lax.ppermute(row, "col", swap) for row in (up, down)]
+    up, down = arrange(place, [up, down], halos, stride_cols, share)
+    weights = (expand_weight, depth_kernel, project_weight, norm_gain.reshape(1, -1))
+
+    def exchange(arrays, far):
+        return [
+            array
+            if k + far * owners == 0
+            else lax.ppermute(
+                array, "row", [(r, r ^ (k + far * owners)) for r in range(row_count)]
+            )
+            for k, array in enumerate(arrays)
+        ]
+
+    keeps, pieces = {}, {}
+    for far in (1, 0):
+        keeps[far], normed = mbconv_half(
+            far, span, stride_rows, owners, place, up, down, ordered, own, weights
+        )
+        pieces[far] = exchange(normed, far)
+    backs, others = {}, pieces[0]
+    for far in (1, 0):
+        result = attend_half(place, pieces[far], others, far, per, attend_weight, output_weight)
+        others = result[owners:]
+        backs[far] = exchange(result[:owners], far)
+    out = None
+    for far in (0, 1):
+        keep, send = add_half(place, keeps[far], backs[far])
+        got = lax.ppermute(send, "col", swap)
+        out = finish_half(place, keep, got, out, far, owners, rows, stride_rows, span)
+    return out.reshape(rows, cols, channels)
+
+
 def local(
     tokens, expand_weight, depth_kernel, project_weight, norm_gain, attend_weight, output_weight
 ):
+    if fits(tokens.shape, expand_weight.shape[1], lax.axis_size("row"), lax.axis_size("col")):
+        return chunked(
+            tokens,
+            expand_weight,
+            depth_kernel,
+            project_weight,
+            norm_gain,
+            attend_weight,
+            output_weight,
+        )
     tile_rows, tile_cols, channels = tokens.shape
     padded_in = extended(tokens, (("row", 0), ("col", 1)), 1)
     expanded = expand_tile(padded_in, expand_weight)
@@ -142,6 +630,7 @@
 
 def solution(mesh):
     placed = (P(("parts", "row"), "col", None), P(), P(), P(), P(), P(), P())
+
     return jax.shard_map(
         local,
         mesh=mesh,

time: 169 us -> 108 us (0.64)
  the two profiles are of different devices: /device:TPU:0 before, /device:TPU:9 now
where the time goes in v3:
time: 108 us
  waiting for transfers between devices  38.8 us (36%)
  Pallas kernels  38.4 us (36%)
  starting transfers between devices  29.3 us (27%)
  local copies, waits for them, and re-layouts  1.1 us (1%)
    pallas_call x9, Pallas kernels, call(): pl.pallas_call(kernel, in_specs=[SMEM] + [VMEM] * len(operands), out_spec...  35.2 us
    ppermute x14, waiting for transfers between devices, exchange(): lax.ppermute(array, 'row', [(r, r ^ k + far * owners) for r in range(row_...  28.2 us
    ppermute x14, starting transfers between devices, exchange(): lax.ppermute(array, 'row', [(r, r ^ k + far * owners) for r in range(row_...  16.1 us
    ppermute x1, waiting for transfers between devices, chunked(): lax.ppermute(tokens[rows - 1:], 'row', [(r, r + 1) for r in range(row_cou...  8.13 us
    ppermute x2, starting transfers between devices, chunked(): got = lax.ppermute(send, 'col', swap)  4.92 us
    pallas_call x2, Pallas kernels, finish_half(): pl.pallas_call(functools.partial(finish_kernel, far=far, owners=owners, s...  3.16 us
    ppermute x1, starting transfers between devices, chunked(): lax.ppermute(tokens[rows - 1:], 'row', [(r, r + 1) for r in range(row_cou...  3.15 us
    ppermute x1, starting transfers between devices, chunked(): lax.ppermute(tokens[:1], 'row', [(r + 1, r) for r in range(row_count - 1)])  3.03 us
  transfers between devices with their start and end apart: 21, of which 11 were waited for; matrix products, arithmetic and copies ran while one was open for 1% of the time, Pallas kernels for 11%

profile of v3, /device:TPU:9, one launch (start us, length us, event | category | flops | bytes accessed | tf_op | source)
XLA Modules:
  0.0 107.9 jit_solution(15308949946981557408)
XLA Ops:
  1.7 3.1 %collective-permute-start = (bf16[1,256,512]{2,1,0:T(8,128)(2,1)S(1)}, bf16[1,256,512]{2,1,0:T(8,128)(2,1)S(1)}, u32[]{:S(2)}, u32[]{:S(2)}) collective-permute-start(bf16[1,256,512]{2,1,0:T(8,128)(2,1)S(1)} %get-tuple-element.56), channel_id=1, source_target_pairs={{0,2},{2,4},{4,6},{6,8},{8,10},{10,12},{12,14},{1,3},{3,5},{5,7},{... | collective-permute-start | bytes 786440 | tf_op jit(solution)/shard_map/ppermute | solution.py:510
  4.9 3.0 %collective-permute-start.1 = (bf16[1,256,512]{2,1,0:T(8,128)(2,1)S(1)}, bf16[1,256,512]{2,1,0:T(8,128)(2,1)S(1)}, u32[]{:S(2)}, u32[]{:S(2)}) collective-permute-start(bf16[1,256,512]{2,1,0:T(8,128)(2,1)S(1)} %get-tuple-element.55), channel_id=1, source_target_pairs={{2,0},{4,2},{6,4},{8,6},{10,8},{12,10},{14,12},{3,1},{5,3},{7,5},{... | collective-permute-start | bytes 786440 | tf_op jit(solution)/shard_map/ppermute | solution.py:511
  7.9 8.1 %collective-permute-done.refs_0_ = bf16[1,256,512]{2,1,0:T(8,128)(2,1)S(1)} collective-permute-done((bf16[1,256,512]{2,1,0:T(8,128)(2,1)S(1)}, bf16[1,256,512]{2,1,0:T(8,128)(2,1)S(1)}, u32[]{:S(2)}, u32[]{:S(2)}) %collective-permute-start) | collective-permute-done | bytes 262176 | tf_op jit(solution)/shard_map/ppermute | solution.py:510
  17.0 1.4 %collective-permute-done.1.refs_1_ = bf16[1,256,512]{2,1,0:T(8,128)(2,1)S(1)} collective-permute-done((bf16[1,256,512]{2,1,0:T(8,128)(2,1)S(1)}, bf16[1,256,512]{2,1,0:T(8,128)(2,1)S(1)}, u32[]{:S(2)}, u32[]{:S(2)}) %collective-permute-start.1) | collective-permute-done | bytes 262176 | tf_op jit(solution)/shard_map/ppermute | solution.py:511
  22.4 4.4 %shard_map.75.own_ref = bf16[8,4,288,256]{3,2,1,0:T(8,128)(2,1)S(1)} custom-call(s32[2]{0:T(128)S(1)} %pad_add_fusion.place_ref, bf16[4,288,512]{2,1,0:T(8,128)(2,1)S(1)} %shard_map.74.ordered_ref, bf16[512,2048]{1,0:T(8,128)(2,1)S(1)} %copy-done), custom_call_target="tpu_custom_call" | custom-call | flops 2415919104 | bytes 1048576 | tf_op jit(solution)/shard_map/pallas_call | solution.py:116
  26.9 7.4 %shard_map.76 = (bf16[512,512]{1,0:T(8,128)(2,1)S(1)}, bf16[128,512]{1,0:T(8,128)(2,1)S(1)}, bf16[128,512]{1,0:T(8,128)(2,1)S(1)}, bf16[128,512]{1,0:T(8,128)(2,1)S(1)}, bf16[128,512]{1,0:T(8,128)(2,1)S(1)}) custom-call(s32[2]{0:T(128)S(1)} %pad_add_fusion.place_ref, bf16[1,288,512]{2,1,0:T(8,128)(2,1)S(1)} %get-tuple-element.30.up_ref, ...), custom_call_target="tpu_custom_call" | custom-call | flops 2147483648 | bytes 1048576 | tf_op jit(solution)/shard_map/pallas_call | solution.py:116
  34.4 2.4 %collective-permute-start.5 = (bf16[128,512]{1,0:T(8,128)(2,1)S(1)}, bf16[128,512]{1,0:T(8,128)(2,1)S(1)}, u32[]{:S(2)}, u32[]{:S(2)}) collective-permute-start(bf16[128,512]{1,0:T(8,128)(2,1)S(1)} %get-tuple-element.33), channel_id=1, source_target_pairs={{0,8},{2,10},{4,12},{6,14},{8,0},{10,2},{12,4},{14,6},{1,9},{3,11}... | collective-permute-start | bytes 393224 | tf_op jit(solution)/shard_map/ppermute | solution.py:523
  39.2 7.4 %shard_map.77 = (bf16[512,512]{1,0:T(8,128)(2,1)S(1)}, bf16[128,512]{1,0:T(8,128)(2,1)S(1)}, bf16[128,512]{1,0:T(8,128)(2,1)S(1)}, bf16[128,512]{1,0:T(8,128)(2,1)S(1)}, bf16[128,512]{1,0:T(8,128)(2,1)S(1)}) custom-call(s32[2]{0:T(128)S(1)} %pad_add_fusion.place_ref, bf16[1,288,512]{2,1,0:T(8,128)(2,1)S(1)} %get-tuple-element.30.up_ref, ...), custom_call_target="tpu_custom_call" | custom-call | flops 2147483648 | bytes 1048576 | tf_op jit(solution)/shard_map/pallas_call | solution.py:116
  47.4 3.7 %collective-permute-done.5.refs_0_ = bf16[128,512]{1,0:T(8,128)(2,1)S(1)} collective-permute-done((bf16[128,512]{1,0:T(8,128)(2,1)S(1)}, bf16[128,512]{1,0:T(8,128)(2,1)S(1)}, u32[]{:S(2)}, u32[]{:S(2)}) %collective-permute-start.5) | collective-permute-done | bytes 131104 | tf_op jit(solution)/shard_map/ppermute | solution.py:523
  51.7 2.2 %collective-permute-done.6.refs_1_ = bf16[128,512]{1,0:T(8,128)(2,1)S(1)} collective-permute-done((bf16[128,512]{1,0:T(8,128)(2,1)S(1)}, bf16[128,512]{1,0:T(8,128)(2,1)S(1)}, u32[]{:S(2)}, u32[]{:S(2)}) %collective-permute-start.6) | collective-permute-done | bytes 131104 | tf_op jit(solution)/shard_map/ppermute | solution.py:523
  53.9 1.5 %collective-permute-start.11 = (bf16[128,512]{1,0:T(8,128)(2,1)S(1)}, bf16[128,512]{1,0:T(8,128)(2,1)S(1)}, u32[]{:S(2)}, u32[]{:S(2)}) collective-permute-start(bf16[128,512]{1,0:T(8,128)(2,1)S(1)} %get-tuple-element.40), channel_id=1, source_target_pairs={{0,6},{2,4},{4,2},{6,0},{8,14},{10,12},{12,10},{14,8},{1,7},{3,5},... | collective-permute-start | bytes 393224 | tf_op jit(solution)/shard_map/ppermute | solution.py:523
  56.7 4.3 %collective-permute-done.8.refs_3_ = bf16[128,512]{1,0:T(8,128)(2,1)S(1)} collective-permute-done((bf16[128,512]{1,0:T(8,128)(2,1)S(1)}, bf16[128,512]{1,0:T(8,128)(2,1)S(1)}, u32[]{:S(2)}, u32[]{:S(2)}) %collective-permute-start.8) | collective-permute-done | bytes 131104 | tf_op jit(solution)/shard_map/ppermute | solution.py:523
  61.1 6.7 %shard_map.78 = (bf16[128,512]{1,0:T(8,128)(2,1)S(1)}, bf16[128,512]{1,0:T(8,128)(2,1)S(1)}, bf16[128,512]{1,0:T(8,128)(2,1)S(1)}, bf16[128,512]{1,0:T(8,128)(2,1)S(1)}, bf16[4,256,1024]{2,1,0:T(8,128)(2,1)S(1)}) custom-call(s32[2]{0:T(128)S(1)} %pad_add_fusion.place_ref, bf16[128,512]{1,0:T(8,128)(2,1)S(1)} %collective-permute-done.5.refs_0_, ...), custom_call_target="tpu_custom_call" | custom-call | flops 1610612736 | bytes 1048576 | tf_op jit(solution)/shard_map/pallas_call | solution.py:116
  67.8 5.5 %shard_map.80 = (bf16[128,512]{1,0:T(8,128)(2,1)S(1)}, bf16[128,512]{1,0:T(8,128)(2,1)S(1)}, bf16[128,512]{1,0:T(8,128)(2,1)S(1)}, bf16[128,512]{1,0:T(8,128)(2,1)S(1)}) custom-call(s32[2]{0:T(128)S(1)} %pad_add_fusion.place_ref, bf16[128,512]{1,0:T(8,128)(2,1)S(1)} %get-tuple-element.37.refs_4_.refs_0_, ...), custom_call_target="tpu_custom_call" | custom-call | flops 1610612736 | bytes 1048576 | tf_op jit(solution)/shard_map/pallas_call | solution.py:116
  73.7 2.3 %collective-permute-start.19 = (bf16[128,512]{1,0:T(8,128)(2,1)S(1)}, bf16[128,512]{1,0:T(8,128)(2,1)S(1)}, u32[]{:S(2)}, u32[]{:S(2)}) collective-permute-start(bf16[128,512]{1,0:T(8,128)(2,1)S(1)} %get-tuple-element.52), channel_id=1, source_target_pairs={{0,6},{2,4},{4,2},{6,0},{8,14},{10,12},{12,10},{14,8},{1,7},{3,5},... | collective-permute-start | bytes 393224 | tf_op jit(solution)/shard_map/ppermute | solution.py:523
  76.0 2.3 %collective-permute-start.12 = (bf16[128,512]{1,0:T(8,128)(2,1)S(1)}, bf16[128,512]{1,0:T(8,128)(2,1)S(1)}, u32[]{:S(2)}, u32[]{:S(2)}) collective-permute-start(bf16[128,512]{1,0:T(8,128)(2,1)S(1)} %get-tuple-element.41), channel_id=1, source_target_pairs={{0,8},{2,10},{4,12},{6,14},{8,0},{10,2},{12,4},{14,6},{1,9},{3,11}... | collective-permute-start | bytes 393224 | tf_op jit(solution)/shard_map/ppermute | solution.py:523
  79.2 2.6 %collective-permute-start.14 = (bf16[128,512]{1,0:T(8,128)(2,1)S(1)}, bf16[128,512]{1,0:T(8,128)(2,1)S(1)}, u32[]{:S(2)}, u32[]{:S(2)}) collective-permute-start(bf16[128,512]{1,0:T(8,128)(2,1)S(1)} %get-tuple-element.43), channel_id=1, source_target_pairs={{0,12},{2,14},{4,8},{6,10},{8,4},{10,6},{12,0},{14,2},{1,13},{3,15... | collective-permute-start | bytes 393224 | tf_op jit(solution)/shard_map/ppermute | solution.py:523
  82.9 3.4 %collective-permute-start.20 = (bf16[256,512]{1,0:T(8,128)(2,1)S(1)}, bf16[256,512]{1,0:T(8,128)(2,1)S(1)}, u32[]{:S(2)}, u32[]{:S(2)}) collective-permute-start(bf16[256,512]{1,0:T(8,128)(2,1)S(1)} %get-tuple-element.54), channel_id=1, source_target_pairs={{0,1},{1,0},{2,3},{3,2},{4,5},{5,4},{6,7},{7,6},{8,9},{9,8},{10,11... | collective-permute-start | bytes 786440 | tf_op jit(solution)/shard_map/ppermute | solution.py:543
  86.3 8.0 %collective-permute-done.13.refs_1_ = bf16[128,512]{1,0:T(8,128)(2,1)S(1)} collective-permute-done((bf16[128,512]{1,0:T(8,128)(2,1)S(1)}, bf16[128,512]{1,0:T(8,128)(2,1)S(1)}, u32[]{:S(2)}, u32[]{:S(2)}) %collective-permute-start.13) | collective-permute-done | bytes 131104 | tf_op jit(solution)/shard_map/ppermute | solution.py:523
  94.3 3.9 %collective-permute-done.14.refs_2_ = bf16[128,512]{1,0:T(8,128)(2,1)S(1)} collective-permute-done((bf16[128,512]{1,0:T(8,128)(2,1)S(1)}, bf16[128,512]{1,0:T(8,128)(2,1)S(1)}, u32[]{:S(2)}, u32[]{:S(2)}) %collective-permute-start.14) | collective-permute-done | bytes 131104 | tf_op jit(solution)/shard_map/ppermute | solution.py:523
  98.2 4.4 %collective-permute-done.15.refs_3_ = bf16[128,512]{1,0:T(8,128)(2,1)S(1)} collective-permute-done((bf16[128,512]{1,0:T(8,128)(2,1)S(1)}, bf16[128,512]{1,0:T(8,128)(2,1)S(1)}, u32[]{:S(2)}, u32[]{:S(2)}) %collective-permute-start.15) | collective-permute-done | bytes 131104 | tf_op jit(solution)/shard_map/ppermute | solution.py:523
  103.2 1.5 %collective-permute-start.16 = (bf16[256,512]{1,0:T(8,128)(2,1)S(1)}, bf16[256,512]{1,0:T(8,128)(2,1)S(1)}, u32[]{:S(2)}, u32[]{:S(2)}) collective-permute-start(bf16[256,512]{1,0:T(8,128)(2,1)S(1)} %get-tuple-element.46), channel_id=1, source_target_pairs={{0,1},{1,0},{2,3},{3,2},{4,5},{5,4},{6,7},{7,6},{8,9},{9,8},{10,11... | collective-permute-start | bytes 786440 | tf_op jit(solution)/shard_map/ppermute | solution.py:543
  104.7 1.6 %shard_map.82.rest_0_ = bf16[4,8,2,2,8,512]{5,4,3,2,1,0:T(8,128)(2,1)} custom-call(s32[2]{0:T(128)S(1)} %pad_add_fusion.place_ref, bf16[256,512]{1,0:T(8,128)(2,1)S(1)} %get-tuple-element.53.keep_ref, bf16[256,512]{1,0:T(8,128)(2,1)S(1)} %collective-permute-done.20.got_ref), custom_call_target="tpu_custom_call" | custom-call | flops 67108864 | bytes 2097152 | tf_op jit(solution)/shard_map/pallas_call | solution.py:457
  106.3 1.6 %shard_map.83 = bf16[4,8,2,2,8,512]{5,4,3,2,1,0:T(8,128)(2,1)} custom-call(s32[2]{0:T(128)S(1)} %pad_add_fusion.place_ref, bf16[256,512]{1,0:T(8,128)(2,1)S(1)} %get-tuple-element.45.keep_ref, bf16[256,512]{1,0:T(8,128)(2,1)S(1)} %collective-permute-done.16.got_ref, bf16[4,8,2,2,8,512]{5,4,3,2,1,0:T(8,128)(2,1)} %shard_map.82.rest_0_), custom_call_target="tpu_custom_call", output_to_operand_aliasing={{}: (3, {})} | custom-call | flops 67108864 | bytes 2097152 | tf_op jit(solution)/shard_map/pallas_call | solution.py:457
  (45 shorter events, 14.9 us)
Async XLA Ops:
  0.0 21.1 %copy-start.2 = (bf16[4,256,512]{2,1,0:T(8,128)(2,1)S(1)}, bf16[4,256,512]{2,1,0:T(8,128)(2,1)}, u32[]{:S(2)}) copy-start(bf16[4,256,512]{2,1,0:T(8,128)(2,1)} %refs_0_.1) | copy-start | bytes 3145732
  0.0 21.1 %collective-permute-start.4 = (bf16[4,256,512]{2,1,0:T(8,128)(2,1)}, bf16[4,256,512]{2,1,0:T(8,128)(2,1)S(1)}, u32[]{:S(2)}, u32[]{:S(2)}) collective-permute-start(bf16[4,256,512]{2,1,0:T(8,128)(2,1)} %refs_0_.1), channel_id=1, source_target_pairs={{0,1},{1,0},{2,3},{3,2},{4,5},{5,4},{6,7},{7,6},{8,9},{9,8},{10,11... | collective-permute-start | bytes 3145736 | tf_op jit(solution)/shard_map/ppermute | solution.py:512
  1.7 14.3 %collective-permute-start = (bf16[1,256,512]{2,1,0:T(8,128)(2,1)S(1)}, bf16[1,256,512]{2,1,0:T(8,128)(2,1)S(1)}, u32[]{:S(2)}, u32[]{:S(2)}) collective-permute-start(bf16[1,256,512]{2,1,0:T(8,128)(2,1)S(1)} %get-tuple-element.56), channel_id=1, source_target_pairs={{0,2},{2,4},{4,6},{6,8},{8,10},{10,12},{12,14},{1,3},{3,5},{5,7},{... | collective-permute-start | bytes 786440 | tf_op jit(solution)/shard_map/ppermute | solution.py:510
  4.9 13.5 %collective-permute-start.1 = (bf16[1,256,512]{2,1,0:T(8,128)(2,1)S(1)}, bf16[1,256,512]{2,1,0:T(8,128)(2,1)S(1)}, u32[]{:S(2)}, u32[]{:S(2)}) collective-permute-start(bf16[1,256,512]{2,1,0:T(8,128)(2,1)S(1)} %get-tuple-element.55), channel_id=1, source_target_pairs={{2,0},{4,2},{6,4},{8,6},{10,8},{12,10},{14,12},{3,1},{5,3},{7,5},{... | collective-permute-start | bytes 786440 | tf_op jit(solution)/shard_map/ppermute | solution.py:511
  16.1 2.9 %collective-permute-start.2 = (bf16[1,256,512]{2,1,0:T(8,128)(2,1)S(1)}, bf16[1,256,512]{2,1,0:T(8,128)(2,1)S(1)}, u32[]{:S(2)}, u32[]{:S(2)}) collective-permute-start(bf16[1,256,512]{2,1,0:T(8,128)(2,1)S(1)} %collective-permute-done.refs_0_), channel_id=1, source_target_pairs={{0,1},{1,0},{2,3},{3,2},{4,5},{5,4},{6,7},{7,6},{8,9},{9,8},{10,11... | collective-permute-start | bytes 786440 | tf_op jit(solution)/shard_map/ppermute | solution.py:515
  18.4 1.6 %collective-permute-start.3 = (bf16[1,256,512]{2,1,0:T(8,128)(2,1)S(1)}, bf16[1,256,512]{2,1,0:T(8,128)(2,1)S(1)}, u32[]{:S(2)}, u32[]{:S(2)}) collective-permute-start(bf16[1,256,512]{2,1,0:T(8,128)(2,1)S(1)} %collective-permute-done.1.refs_1_), channel_id=1, source_target_pairs={{0,1},{1,0},{2,3},{3,2},{4,5},{5,4},{6,7},{7,6},{8,9},{9,8},{10,11... | collective-permute-start | bytes 786440 | tf_op jit(solution)/shard_map/ppermute | solution.py:515
  34.4 16.7 %collective-permute-start.5 = (bf16[128,512]{1,0:T(8,128)(2,1)S(1)}, bf16[128,512]{1,0:T(8,128)(2,1)S(1)}, u32[]{:S(2)}, u32[]{:S(2)}) collective-permute-start(bf16[128,512]{1,0:T(8,128)(2,1)S(1)} %get-tuple-element.33), channel_id=1, source_target_pairs={{0,8},{2,10},{4,12},{6,14},{8,0},{10,2},{12,4},{14,6},{1,9},{3,11}... | collective-permute-start | bytes 393224 | tf_op jit(solution)/shard_map/ppermute | solution.py:523
  36.7 17.2 %collective-permute-start.6 = (bf16[128,512]{1,0:T(8,128)(2,1)S(1)}, bf16[128,512]{1,0:T(8,128)(2,1)S(1)}, u32[]{:S(2)}, u32[]{:S(2)}) collective-permute-start(bf16[128,512]{1,0:T(8,128)(2,1)S(1)} %get-tuple-element.34), channel_id=1, source_target_pairs={{0,10},{2,8},{4,14},{6,12},{8,2},{10,0},{12,6},{14,4},{1,11},{3,9}... | collective-permute-start | bytes 393224 | tf_op jit(solution)/shard_map/ppermute | solution.py:523
  37.2 19.5 %collective-permute-start.7 = (bf16[128,512]{1,0:T(8,128)(2,1)S(1)}, bf16[128,512]{1,0:T(8,128)(2,1)S(1)}, u32[]{:S(2)}, u32[]{:S(2)}) collective-permute-start(bf16[128,512]{1,0:T(8,128)(2,1)S(1)} %get-tuple-element.35), channel_id=1, source_target_pairs={{0,12},{2,14},{4,8},{6,10},{8,4},{10,6},{12,0},{14,2},{1,13},{3,15... | collective-permute-start | bytes 393224 | tf_op jit(solution)/shard_map/ppermute | solution.py:523
  38.5 22.6 %copy-start.5 = (bf16[512,1536]{1,0:T(8,128)(2,1)S(1)}, bf16[512,1536]{1,0:T(8,128)(2,1)}, u32[]{:S(2)}) copy-start(bf16[512,1536]{1,0:T(8,128)(2,1)} %refs_5_.1) | copy-start | bytes 4718596
  38.5 22.6 %copy-start.6 = (bf16[512,512]{1,0:T(8,128)(2,1)S(1)}, bf16[512,512]{1,0:T(8,128)(2,1)}, u32[]{:S(2)}) copy-start(bf16[512,512]{1,0:T(8,128)(2,1)} %refs_6_.1) | copy-start | bytes 1572868
  38.5 22.5 %collective-permute-start.8 = (bf16[128,512]{1,0:T(8,128)(2,1)S(1)}, bf16[128,512]{1,0:T(8,128)(2,1)S(1)}, u32[]{:S(2)}, u32[]{:S(2)}) collective-permute-start(bf16[128,512]{1,0:T(8,128)(2,1)S(1)} %get-tuple-element.36), channel_id=1, source_target_pairs={{0,14},{2,12},{4,10},{6,8},{8,6},{10,4},{12,2},{14,0},{1,15},{3,13... | collective-permute-start | bytes 393224 | tf_op jit(solution)/shard_map/ppermute | solution.py:523
  46.6 14.4 %collective-permute-start.9 = (bf16[128,512]{1,0:T(8,128)(2,1)S(1)}, bf16[128,512]{1,0:T(8,128)(2,1)S(1)}, u32[]{:S(2)}, u32[]{:S(2)}) collective-permute-start(bf16[128,512]{1,0:T(8,128)(2,1)S(1)} %get-tuple-element.38), channel_id=1, source_target_pairs={{0,2},{2,0},{4,6},{6,4},{8,10},{10,8},{12,14},{14,12},{1,3},{3,1},... | collective-permute-start | bytes 393224 | tf_op jit(solution)/shard_map/ppermute | solution.py:523
  51.1 10.0 %collective-permute-start.10 = (bf16[128,512]{1,0:T(8,128)(2,1)S(1)}, bf16[128,512]{1,0:T(8,128)(2,1)S(1)}, u32[]{:S(2)}, u32[]{:S(2)}) collective-permute-start(bf16[128,512]{1,0:T(8,128)(2,1)S(1)} %get-tuple-element.39), channel_id=1, source_target_pairs={{0,4},{2,6},{4,0},{6,2},{8,12},{10,14},{12,8},{14,10},{1,5},{3,7},... | collective-permute-start | bytes 393224 | tf_op jit(solution)/shard_map/ppermute | solution.py:523
  53.9 7.2 %collective-permute-start.11 = (bf16[128,512]{1,0:T(8,128)(2,1)S(1)}, bf16[128,512]{1,0:T(8,128)(2,1)S(1)}, u32[]{:S(2)}, u32[]{:S(2)}) collective-permute-start(bf16[128,512]{1,0:T(8,128)(2,1)S(1)} %get-tuple-element.40), channel_id=1, source_target_pairs={{0,6},{2,4},{4,2},{6,0},{8,14},{10,12},{12,10},{14,8},{1,7},{3,5},... | collective-permute-start | bytes 393224 | tf_op jit(solution)/shard_map/ppermute | solution.py:523
  73.3 5.9 %collective-permute-start.17 = (bf16[128,512]{1,0:T(8,128)(2,1)S(1)}, bf16[128,512]{1,0:T(8,128)(2,1)S(1)}, u32[]{:S(2)}, u32[]{:S(2)}) collective-permute-start(bf16[128,512]{1,0:T(8,128)(2,1)S(1)} %get-tuple-element.50), channel_id=1, source_target_pairs={{0,2},{2,0},{4,6},{6,4},{8,10},{10,8},{12,14},{14,12},{1,3},{3,1},... | collective-permute-start | bytes 393224 | tf_op jit(solution)/shard_map/ppermute | solution.py:523
  73.7 8.1 %collective-permute-start.18 = (bf16[128,512]{1,0:T(8,128)(2,1)S(1)}, bf16[128,512]{1,0:T(8,128)(2,1)S(1)}, u32[]{:S(2)}, u32[]{:S(2)}) collective-permute-start(bf16[128,512]{1,0:T(8,128)(2,1)S(1)} %get-tuple-element.51), channel_id=1, source_target_pairs={{0,4},{2,6},{4,0},{6,2},{8,12},{10,14},{12,8},{14,10},{1,5},{3,7},... | collective-permute-start | bytes 393224 | tf_op jit(solution)/shard_map/ppermute | solution.py:523
  73.7 8.4 %collective-permute-start.19 = (bf16[128,512]{1,0:T(8,128)(2,1)S(1)}, bf16[128,512]{1,0:T(8,128)(2,1)S(1)}, u32[]{:S(2)}, u32[]{:S(2)}) collective-permute-start(bf16[128,512]{1,0:T(8,128)(2,1)S(1)} %get-tuple-element.52), channel_id=1, source_target_pairs={{0,6},{2,4},{4,2},{6,0},{8,14},{10,12},{12,10},{14,8},{1,7},{3,5},... | collective-permute-start | bytes 393224 | tf_op jit(solution)/shard_map/ppermute | solution.py:523
  76.0 10.3 %collective-permute-start.12 = (bf16[128,512]{1,0:T(8,128)(2,1)S(1)}, bf16[128,512]{1,0:T(8,128)(2,1)S(1)}, u32[]{:S(2)}, u32[]{:S(2)}) collective-permute-start(bf16[128,512]{1,0:T(8,128)(2,1)S(1)} %get-tuple-element.41), channel_id=1, source_target_pairs={{0,8},{2,10},{4,12},{6,14},{8,0},{10,2},{12,4},{14,6},{1,9},{3,11}... | collective-permute-start | bytes 393224 | tf_op jit(solution)/shard_map/ppermute | solution.py:523
  78.3 16.0 %collective-permute-start.13 = (bf16[128,512]{1,0:T(8,128)(2,1)S(1)}, bf16[128,512]{1,0:T(8,128)(2,1)S(1)}, u32[]{:S(2)}, u32[]{:S(2)}) collective-permute-start(bf16[128,512]{1,0:T(8,128)(2,1)S(1)} %get-tuple-element.42), channel_id=1, source_target_pairs={{0,10},{2,8},{4,14},{6,12},{8,2},{10,0},{12,6},{14,4},{1,11},{3,9}... | collective-permute-start | bytes 393224 | tf_op jit(solution)/shard_map/ppermute | solution.py:523
  79.2 19.0 %collective-permute-start.14 = (bf16[128,512]{1,0:T(8,128)(2,1)S(1)}, bf16[128,512]{1,0:T(8,128)(2,1)S(1)}, u32[]{:S(2)}, u32[]{:S(2)}) collective-permute-start(bf16[128,512]{1,0:T(8,128)(2,1)S(1)} %get-tuple-element.43), channel_id=1, source_target_pairs={{0,12},{2,14},{4,8},{6,10},{8,4},{10,6},{12,0},{14,2},{1,13},{3,15... | collective-permute-start | bytes 393224 | tf_op jit(solution)/shard_map/ppermute | solution.py:523
  81.8 20.7 %collective-permute-start.15 = (bf16[128,512]{1,0:T(8,128)(2,1)S(1)}, bf16[128,512]{1,0:T(8,128)(2,1)S(1)}, u32[]{:S(2)}, u32[]{:S(2)}) collective-permute-start(bf16[128,512]{1,0:T(8,128)(2,1)S(1)} %get-tuple-element.44), channel_id=1, source_target_pairs={{0,14},{2,12},{4,10},{6,8},{8,6},{10,4},{12,2},{14,0},{1,15},{3,13... | collective-permute-start | bytes 393224 | tf_op jit(solution)/shard_map/ppermute | solution.py:523
  82.9 21.9 %collective-permute-start.20 = (bf16[256,512]{1,0:T(8,128)(2,1)S(1)}, bf16[256,512]{1,0:T(8,128)(2,1)S(1)}, u32[]{:S(2)}, u32[]{:S(2)}) collective-permute-start(bf16[256,512]{1,0:T(8,128)(2,1)S(1)} %get-tuple-element.54), channel_id=1, source_target_pairs={{0,1},{1,0},{2,3},{3,2},{4,5},{5,4},{6,7},{7,6},{8,9},{9,8},{10,11... | collective-permute-start | bytes 786440 | tf_op jit(solution)/shard_map/ppermute | solution.py:543
  103.2 3.1 %collective-permute-start.16 = (bf16[256,512]{1,0:T(8,128)(2,1)S(1)}, bf16[256,512]{1,0:T(8,128)(2,1)S(1)}, u32[]{:S(2)}, u32[]{:S(2)}) collective-permute-start(bf16[256,512]{1,0:T(8,128)(2,1)S(1)} %get-tuple-element.46), channel_id=1, source_target_pairs={{0,1},{1,0},{2,3},{3,2},{4,5},{5,4},{6,7},{7,6},{8,9},{9,8},{10,11... | collective-permute-start | bytes 786440 | tf_op jit(solution)/shard_map/ppermute | solution.py:543
  (4 other events, 16.9 us)

commit v4 on v3

--- a/solution.py
+++ b/solution.py
@@ -89,22 +89,26 @@
     return result.reshape(count, members, channels)
 
 
-def arrange_kernel(place_ref, *refs, stride_cols, share):
-    count = len(refs) // 3
-    cols, _ = refs[0].shape[1:]
-    size = refs[-1].shape[1]
+def arrange_kernel(
+    place_ref, own_ref, other_ref, ordered_ref, far_ref, near_ref, *, stride_cols, share, owners
+):
+    rows, cols, _ = own_ref.shape
+    size = ordered_ref.shape[1]
     col = place_ref[0]
     at = lax.broadcasted_iota(jnp.int32, (size, cols), 0)
     want = (at % GRID) * stride_cols + at // GRID + (col * share - 1)
     index = lax.broadcasted_iota(jnp.int32, (size, cols), 1)
     select_own = (index + col * cols == want).astype(jnp.bfloat16)
     select_other = (index + (1 - col) * cols == want).astype(jnp.bfloat16)
-    for own_ref, other_ref, ordered_ref in zip(refs[:count], refs[count : 2 * count], refs[2 * count :]):
-        for row in range(own_ref.shape[0]):
-            picked = jnp.dot(select_own, own_ref[row], preferred_element_type=jnp.float32) + jnp.dot(
-                select_other, other_ref[row], preferred_element_type=jnp.float32
-            )
-            ordered_ref[row] = picked.astype(jnp.bfloat16)
+    for row in range(rows):
+        picked = jnp.dot(select_own, own_ref[row], preferred_element_type=jnp.float32) + jnp.dot(
+            select_other, other_ref[row], preferred_element_type=jnp.float32
+        )
+        ordered_ref[row] = picked.astype(jnp.bfloat16)
+    is_low = place_ref[1] < owners
+    first, last = ordered_ref[0], ordered_ref[rows - 1]
+    far_ref[...] = jnp.where(is_low, first, last)
+    near_ref[...] = jnp.where(is_low, last, first)
 
 
 VMEM = pl.BlockSpec(memory_space=pltpu.VMEM)
@@ -124,15 +128,15 @@
     )(place, *operands)
 
 
-def arrange(place, owns, others, stride_cols, share):
-    cols, channels = owns[0].shape[1:]
+def arrange(place, own, other, stride_cols, share, owners):
+    rows, cols, channels = own.shape
     size = (share + 2) * GRID
     return call(
-        functools.partial(arrange_kernel, stride_cols=stride_cols, share=share),
+        functools.partial(arrange_kernel, stride_cols=stride_cols, share=share, owners=owners),
         place,
-        [*owns, *others],
-        [(own.shape[0], size, channels) for own in owns],
-        sum(4 * own.shape[0] * size * cols * channels for own in owns),
+        [own, other],
+        [(rows, size, channels), (size, channels), (size, channels)],
+        4 * rows * size * cols * channels,
         8 * MIB,
     )
 
@@ -167,35 +171,31 @@
     )[0]
 
 
-def mbconv_kernel(
-    place_ref, up_ref, down_ref, ordered_ref, own_ref,
-    expand_ref, taps_ref, project_ref, gain_ref,
-    mbconv_ref, *rest,
-    far, span, stride_rows,
-):
-    *normed_refs, edge_rows, depth_a, depth_b, acc = rest
+def mbconv_kernel(place_ref, *refs, far, share, stride_rows, halos, owners):
+    halo_refs = refs[:halos]
+    ordered_ref, own_ref, expand_ref, taps_ref, project_ref, gain_ref, mbconv_ref = refs[halos : halos + 7]
+    normed_refs = refs[halos + 7 : halos + 7 + owners]
+    edge_rows, depth_a, depth_b, acc = refs[halos + 7 + owners :]
     hidden = expand_ref.shape[1]
     rows = ordered_ref.shape[0]
     row_blocks = rows // stride_rows
-    owners = len(normed_refs)
     spot_half = place_ref[1] // owners
     half_at = 1 - spot_half if far else spot_half
-    begin = pl.multiple_of(half_at * (span * GRID), GRID)
-    part = (span + 2) * GRID
-
     depth_b[...] = jnp.zeros_like(depth_b)
     acc[...] = jnp.zeros_like(acc)
-
-    def step(index, carry):
+    halo = halo_refs[0][...]
+    for ref in halo_refs[1:]:
+        halo = halo + ref[...]
+
+    def step(hm, index, carry):
         for half, depth in ((0, depth_a), (1, depth_b)):
             block = 2 * index + half
-            for side, ref in enumerate((up_ref, down_ref)):
-                product = jnp.dot(
-                    ref[0, pl.ds(begin, part), :],
-                    expand_ref[:, pl.ds(block * BLOCK, BLOCK)],
-                    preferred_element_type=jnp.float32,
-                )
-                edge_rows[half, side] = gelu_twice(product)
+            product = jnp.dot(
+                halo,
+                expand_ref[:, pl.ds(block * BLOCK, BLOCK)],
+                preferred_element_type=jnp.float32,
+            )
+            edge_rows[half] = gelu_twice(product)
             if half == 0:
                 acc[...] = acc[...] + jnp.dot(
                     depth_b[...],
@@ -206,40 +206,39 @@
                 lanes = slice(lane, lane + LANES)
                 taps = [
                     [
-                        taps_ref[dr, dc : dc + 1, pl.ds(block * BLOCK + lane, LANES)]
-                        * TAP_SCALE
+                        taps_ref[dr, dc : dc + 1, pl.ds(block * BLOCK + lane, LANES)] * TAP_SCALE
                         for dc in range(3)
                     ]
                     for dr in range(3)
                 ]
-                for pair in range(0, span, 2):
+                for pair in range(0, share, 2):
                     parts = {}
                     for low in range(0, GRID, SUBLANES):
                         source = []
-                        for row in range(rows + 2):
+                        for row in range(hm, rows + hm + 1):
                             tiles = []
                             for k in range(4):
                                 at = (pair + k) * GRID
                                 if row == 0 or row == rows + 1:
                                     at += low
-                                    tiles.append(edge_rows[half, min(row, 1), at : at + SUBLANES, lanes])
+                                    tiles.append(edge_rows[half, at : at + SUBLANES, lanes])
                                 else:
-                                    tile = own_ref[block, row - 1, pl.ds(begin + at, GRID), lanes]
+                                    tile = own_ref[block, row - 1, at : at + GRID, lanes]
                                     tiles.append(tile.astype(jnp.float32)[low : low + SUBLANES])
                             source.append(tiles)
                         for b in (0, 1):
-                            for row in range(rows):
+                            for rb in range(row_blocks):
                                 total = None
                                 for dr in range(3):
                                     for dc in range(3):
-                                        term = source[row + dr][b + dc] * taps[dr][dc]
+                                        term = source[rb * stride_rows + dr][b + dc] * taps[dr][dc]
                                         total = term if total is None else total + term
-                                parts.setdefault((row, b), []).append(gelu_scaled(total))
-                    for (row, b), tiles in parts.items():
-                        spot = ((row % stride_rows) * span + pair + b) * row_blocks + row // stride_rows
-                        depth[spot * GRID : (spot + 1) * GRID, lanes] = jnp.concatenate(
-                            tiles, axis=0
-                        ).astype(jnp.bfloat16)
+                                parts.setdefault((rb, b), []).append(gelu_scaled(total))
+                    for (rb, b), tiles in parts.items():
+                        spot = ((pair + b) * row_blocks + rb) * GRID
+                        depth[spot : spot + GRID, lanes] = jnp.concatenate(tiles, axis=0).astype(
+                            jnp.bfloat16
+                        )
             if half == 0:
                 acc[...] = acc[...] + jnp.dot(
                     depth_a[...],
@@ -248,7 +247,11 @@
                 )
         return carry
 
-    lax.fori_loop(0, hidden // (2 * BLOCK), step, 0)
+    for hm in range(stride_rows):
+
+        @pl.when(half_at == hm)
+        def _():
+            lax.fori_loop(0, hidden // (2 * BLOCK), functools.partial(step, hm), 0)
 
     gain = gain_ref[...]
     acc[...] = acc[...] + jnp.dot(
@@ -257,16 +260,14 @@
         preferred_element_type=jnp.float32,
     )
     members = row_blocks * GRID
-    per_row = stride_rows * span // owners
+    items = share // owners
     for k, normed_ref in enumerate(normed_refs):
         owner = (place_ref[1] % owners) ^ k
-        hm = owner // (owners // stride_rows)
-        first = (owner % (owners // stride_rows)) * per_row
-        for item in range(per_row):
+        for item in range(items):
             for rb in range(row_blocks):
-                spot = pl.multiple_of((owner * per_row + item) * members + rb * GRID, GRID)
-                column = pl.multiple_of(begin + (first + item + 1) * GRID, GRID)
-                tokens = ordered_ref[rb * stride_rows + hm, pl.ds(column, GRID), :]
+                spot = pl.multiple_of((owner * items + item) * members + rb * GRID, GRID)
+                column = pl.multiple_of((owner * items + item + 1) * GRID, GRID)
+                tokens = ordered_ref[rb * stride_rows + half_at, pl.ds(column, GRID), :]
                 mixed = tokens.astype(jnp.float32) + acc[pl.ds(spot, GRID), :] * BRANCH_SCALE
                 mixed = mixed.astype(jnp.bfloat16)
                 mbconv_ref[pl.ds(spot, GRID), :] = mixed
@@ -280,20 +281,22 @@
                 ).astype(jnp.bfloat16)
 
 
-def mbconv_half(far, span, stride_rows, owners, place, up, down, ordered, own, weights):
-    rows, _, channels = ordered.shape
+def mbconv_half(far, share, stride_rows, owners, place, halos, ordered, own, weights):
+    rows, size, channels = ordered.shape
     hidden = weights[0].shape[1]
-    count = rows * span * GRID
-    part = (span + 2) * GRID
+    count = rows // stride_rows * share * GRID
     mbconv, *normed = call(
-        functools.partial(mbconv_kernel, far=far, span=span, stride_rows=stride_rows),
+        functools.partial(
+            mbconv_kernel, far=far, share=share, stride_rows=stride_rows, halos=len(halos),
+            owners=owners,
+        ),
         place,
-        [up, down, ordered, own, *weights],
+        [*halos, ordered, own, *weights],
         [(count, channels)] + [(count // owners, channels)] * owners,
         4 * count * channels * hidden,
         8 * MIB,
         [
-            pltpu.VMEM((2, 2, part, BLOCK), jnp.float32),
+            pltpu.VMEM((2, size, BLOCK), jnp.float32),
             pltpu.VMEM((count, BLOCK), jnp.bfloat16),
             pltpu.VMEM((count, BLOCK), jnp.bfloat16),
             pltpu.VMEM((count, channels), jnp.float32),
@@ -385,63 +388,65 @@
     )
 
 
-def add_kernel(place_ref, mbconv_ref, *refs):
-    *back_refs, keep_ref, send_ref = refs
-    owners = len(back_refs)
-    channels = mbconv_ref.shape[1]
+def add_kernel(place_ref, *refs, owners):
+    halves = len(refs) // (1 + owners)
+    keep_ref, send_ref = refs[-2:]
     is_left = place_ref[0] == 0
-    for k, back_ref in enumerate(back_refs):
-        size = back_ref.shape[0]
-        base = ((place_ref[1] % owners) ^ k) * size
-        for at in range(0, size, 2 * GRID):
-            spot = pl.multiple_of(base + at, 2 * GRID)
-            total = (
-                back_ref[at : at + 2 * GRID, :].astype(jnp.float32)
-                + mbconv_ref[pl.ds(spot, 2 * GRID), :].astype(jnp.float32)
-            ).reshape(2, 2, SUBLANES, channels)
-            left = total[:, 0].reshape(GRID, channels)
-            right = total[:, 1].reshape(GRID, channels)
-            to = pl.ds(pl.multiple_of(spot // 2, GRID), GRID)
-            keep_ref[to, :] = jnp.where(is_left, left, right).astype(jnp.bfloat16)
-            send_ref[to, :] = jnp.where(is_left, right, left).astype(jnp.bfloat16)
-
-
-def add_half(place, mbconv, backs):
-    count, channels = mbconv.shape
+    for half in range(halves):
+        mbconv_ref = refs[half]
+        channels = mbconv_ref.shape[1]
+        for k in range(owners):
+            back_ref = refs[halves + half * owners + k]
+            size = back_ref.shape[0]
+            base = ((place_ref[1] % owners) ^ k) * size
+            for at in range(0, size, 2 * GRID):
+                spot = pl.multiple_of(base + at, 2 * GRID)
+                total = (
+                    back_ref[at : at + 2 * GRID, :].astype(jnp.float32)
+                    + mbconv_ref[pl.ds(spot, 2 * GRID), :].astype(jnp.float32)
+                ).reshape(2, 2, SUBLANES, channels)
+                left = total[:, 0].reshape(GRID, channels)
+                right = total[:, 1].reshape(GRID, channels)
+                to = pl.ds(pl.multiple_of(spot // 2, GRID), GRID)
+                keep_ref[half, to, :] = jnp.where(is_left, left, right).astype(jnp.bfloat16)
+                send_ref[half, to, :] = jnp.where(is_left, right, left).astype(jnp.bfloat16)
+
+
+def add_halves(place, mbconvs, backs):
+    count, channels = mbconvs[0].shape
     return call(
-        add_kernel, place, [mbconv, *backs], [(count // 2, channels)] * 2,
-        count * channels * 64, 4 * MIB,
-    )
-
-
-def finish_kernel(place_ref, keep_ref, got_ref, *rest, far, owners, span, stride_rows):
-    spot_half = place_ref[1] // owners
-    half_at = 1 - spot_half if far else spot_half
+        functools.partial(add_kernel, owners=len(backs[0])),
+        place,
+        [*mbconvs, *backs[0], *backs[1]],
+        [(len(mbconvs), count // 2, channels)] * 2,
+        count * channels * 64,
+        6 * MIB,
+    )
+
+
+def finish_kernel(place_ref, ready_ref, *rest, mine, owners):
     out_ref, placed_ref, sems = rest[-3:]
-    count, channels = keep_ref.shape
-    length = count // stride_rows
-    row_blocks = length // (span * SUBLANES)
+    halves, length, _ = ready_ref.shape
+    row_blocks, _, blocks, _, share, channels = out_ref.shape
+    which = place_ref[0] if mine else 1 - place_ref[0]
     at = lax.broadcasted_iota(jnp.int32, (length, length), 0)
-    b = at % span
-    a = (at // span) % SUBLANES
-    rb = at // (span * SUBLANES)
-    source = (b * row_blocks + rb) * SUBLANES + a
+    b = at % share
+    a = (at // share) % blocks
+    rb = at // (share * blocks)
+    source = (b * row_blocks + rb) * blocks + a
     select = lax.broadcasted_iota(jnp.int32, (length, length), 1) == source
     select = select.astype(jnp.bfloat16)
     copies = []
-    for hm in range(stride_rows):
-        for ref, which in ((keep_ref, place_ref[0]), (got_ref, 1 - place_ref[0])):
-            placed = jnp.dot(
-                select, ref[hm * length : (hm + 1) * length, :], preferred_element_type=jnp.float32
-            ).astype(jnp.bfloat16)
-            placed = placed.reshape(row_blocks, SUBLANES, span, channels)
-            for rb_at in range(row_blocks):
-                placed_ref[rb_at * stride_rows + hm, :, which] = placed[rb_at]
+    for half in range(halves):
+        hm = place_ref[1] // owners if half == 0 else 1 - place_ref[1] // owners
+        placed = jnp.dot(select, ready_ref[half], preferred_element_type=jnp.float32)
+        placed_ref[half] = placed.astype(jnp.bfloat16).reshape(row_blocks, blocks, share, channels)
         for rb_at in range(row_blocks):
-            row = rb_at * stride_rows + hm
             copies.append(
                 pltpu.make_async_copy(
-                    placed_ref.at[row], out_ref.at[row, :, :, half_at], sems.at[row]
+                    placed_ref.at[half, rb_at],
+                    out_ref.at[rb_at, hm, :, which],
+                    sems.at[half, rb_at],
                 )
             )
             copies[-1].start()
@@ -449,28 +454,25 @@
         copy.wait()
 
 
-def finish_half(place, keep, got, previous, far, owners, rows, stride_rows, span):
-    channels = keep.shape[1]
+def finish(place, ready, previous, mine, owners, shape):
     anywhere = pl.BlockSpec(memory_space=pl.ANY)
-    operands = [keep, got]
+    row_blocks, stride_rows, blocks, _, share, channels = shape
     previous = [] if previous is None else [previous]
     return pl.pallas_call(
-        functools.partial(
-            finish_kernel, far=far, owners=owners, span=span, stride_rows=stride_rows
+        functools.partial(finish_kernel, mine=mine, owners=owners),
+        in_specs=[SMEM, VMEM] + [anywhere] * len(previous),
+        out_specs=anywhere,
+        out_shape=jax.ShapeDtypeStruct(shape, jnp.bfloat16),
+        scratch_shapes=[
+            pltpu.VMEM((stride_rows, row_blocks, blocks, share, channels), jnp.bfloat16),
+            pltpu.SemaphoreType.DMA((stride_rows, row_blocks)),
+        ],
+        input_output_aliases={2: 0} if previous else {},
+        compiler_params=pltpu.CompilerParams(vmem_limit_bytes=6 * MIB),
+        cost_estimate=pl.CostEstimate(
+            flops=4 * ready.size * 256, bytes_accessed=1 << 20, transcendentals=0
         ),
-        in_specs=[SMEM, VMEM, VMEM] + [anywhere] * len(previous),
-        out_specs=anywhere,
-        out_shape=jax.ShapeDtypeStruct((rows, SUBLANES, 2, HALVES, span, channels), jnp.bfloat16),
-        scratch_shapes=[
-            pltpu.VMEM((rows, SUBLANES, 2, span, channels), jnp.bfloat16),
-            pltpu.SemaphoreType.DMA((rows,)),
-        ],
-        input_output_aliases={3: 0} if previous else {},
-        compiler_params=pltpu.CompilerParams(vmem_limit_bytes=4 * MIB),
-        cost_estimate=pl.CostEstimate(
-            flops=2 * keep.shape[0] * channels * 256, bytes_accessed=2 << 20, transcendentals=0
-        ),
-    )(place, *operands, *previous)
+    )(place, ready, *previous)
 
 
 def fits(tokens_shape, hidden, row_count, col_count):
@@ -481,12 +483,10 @@
     return (
         col_count == 2
         and row_count & (row_count - 1) == 0
-        and stride_rows > 0
+        and stride_rows == HALVES
         and rows == 2 * stride_rows
         and cols == SUBLANES * stride_cols
-        and stride_cols % (2 * col_count * HALVES) == 0
-        and owners % stride_rows == 0
-        and stride_cols // (col_count * HALVES) % (owners // stride_rows) == 0
+        and stride_cols % (2 * col_count * owners) == 0
         and channels % BLOCK == 0
         and hidden % (2 * BLOCK) == 0
     )
@@ -501,19 +501,21 @@
     stride_rows = rows * row_count // GRID
     stride_cols = cols * col_count // GRID
     share = stride_cols // col_count
-    span = share // HALVES
     owners = row_count // HALVES
     per = rows // stride_rows * GRID
     swap = [(0, 1), (1, 0)]
     place = jnp.stack([lax.axis_index("col"), lax.axis_index("row")]).astype(jnp.int32)
 
-    up = lax.ppermute(tokens[rows - 1 :], "row", [(r, r + 1) for r in range(row_count - 1)])
-    down = lax.ppermute(tokens[:1], "row", [(r + 1, r) for r in range(row_count - 1)])
     other = lax.ppermute(tokens, "col", swap)
-    (ordered,) = arrange(place, [tokens], [other], stride_cols, share)
+    ordered, to_ends, to_middle = arrange(place, tokens, other, stride_cols, share, owners)
+    outward = [(r, r - 1) for r in range(1, owners)]
+    outward += [(r, r + 1) for r in range(owners, row_count - 1)]
+    far_halos = [
+        lax.ppermute(to_middle, "row", [(owners - 1, owners), (owners, owners - 1)]),
+        lax.ppermute(to_ends, "row", outward),
+    ]
     own = expand_rows(place, ordered, expand_weight)
-    halos = [lax.ppermute(row, "col", swap) for row in (up, down)]
-    up, down = arrange(place, [up, down], halos, stride_cols, share)
+    near_halos = [lax.ppermute(to_middle, "row", [(t, f) for f, t in outward])]
     weights = (expand_weight, depth_kernel, project_weight, norm_gain.reshape(1, -1))
 
     def exchange(arrays, far):
@@ -529,7 +531,8 @@
     keeps, pieces = {}, {}
     for far in (1, 0):
         keeps[far], normed = mbconv_half(
-            far, span, stride_rows, owners, place, up, down, ordered, own, weights
+            far, share, stride_rows, owners, place,
+            far_halos if far else near_halos, ordered, own, weights,
         )
         pieces[far] = exchange(normed, far)
     backs, others = {}, pieces[0]
@@ -537,11 +540,11 @@
         result = attend_half(place, pieces[far], others, far, per, attend_weight, output_weight)
         others = result[owners:]
         backs[far] = exchange(result[:owners], far)
-    out = None
-    for far in (0, 1):
-        keep, send = add_half(place, keeps[far], backs[far])
-        got = lax.ppermute(send, "col", swap)
-        out = finish_half(place, keep, got, out, far, owners, rows, stride_rows, span)
+    keep, send = add_halves(place, (keeps[0], keeps[1]), (backs[0], backs[1]))
+    got = lax.ppermute(send, "col", swap)
+    shape = (rows // stride_rows, stride_rows, cols // stride_cols, col_count, share, channels)
+    out = finish(place, keep, None, True, owners, shape)
+    out = finish(place, got, out, False, owners, shape)
     return out.reshape(rows, cols, channels)
 
 

time: 108 us -> 101 us (0.935)
  the two profiles are of different devices: /device:TPU:9 before, /device:TPU:0 now
where the time goes in v4:
time: 101 us; the launch traced here: 99.2 us
  Pallas kernels  37 us (37%)
  starting transfers between devices  34.7 us (34%)
  waiting for transfers between devices  25.9 us (26%)
  local copies, waits for them, and re-layouts  1.25 us (1%)
    pallas_call x7, Pallas kernels, call(): pl.pallas_call(kernel, in_specs=[SMEM] + [VMEM] * len(operands), out_spec...  33.8 us
    ppermute x14, starting transfers between devices, exchange(): lax.ppermute(array, 'row', [(r, r ^ k + far * owners) for r in range(row_...  26.7 us
    ppermute x14, waiting for transfers between devices, exchange(): lax.ppermute(array, 'row', [(r, r ^ k + far * owners) for r in range(row_...  23 us
    ppermute x1, starting transfers between devices, chunked(): near_halos = [lax.ppermute(to_middle, 'row', [(t, f) for f, t in outward])]  5.43 us
    pallas_call x2, Pallas kernels, finish(): pl.pallas_call(functools.partial(finish_kernel, mine=mine, owners=owners)...  3.19 us
    ppermute x1, waiting for transfers between devices, chunked(): other = lax.ppermute(tokens, 'col', swap)  2.42 us
  transfers between devices with their start and end apart: 19, of which 12 were waited for; matrix products, arithmetic and copies ran while one was open for 0% of the time, Pallas kernels for 21%

profile of v4, /device:TPU:0, one launch (start us, length us, event | category | flops | bytes accessed | tf_op | source)
XLA Modules:
  0.0 99.2 jit_solution(15659532283731136833)
XLA Ops:
  0.6 2.4 %collective-permute-done.other_ref = bf16[4,256,512]{2,1,0:T(8,128)(2,1)S(1)} collective-permute-done((bf16[4,256,512]{2,1,0:T(8,128)(2,1)}, bf16[4,256,512]{2,1,0:T(8,128)(2,1)S(1)}, u32[]{:S(2)}, u32[]{:S(2)}) %collective-permute-start) | collective-permute-done | bytes 1048608 | tf_op jit(solution)/shard_map/ppermute | solution.py:509
  4.2 1.3 %shard_map.73 = (bf16[4,288,512]{2,1,0:T(8,128)(2,1)S(1)}, bf16[288,512]{1,0:T(8,128)(2,1)S(1)}, bf16[288,512]{1,0:T(8,128)(2,1)S(1)}) custom-call(s32[2]{0:T(128)S(1)} %pad_add_fusion.place_ref, bf16[4,256,512]{2,1,0:T(8,128)(2,1)S(1)} %copy-done.5, bf16[4,256,512]{2,1,0:T(8,128)(2,1)S(1)} %collective-permute-done.other_ref), custom_call_target="tpu_custom_call" | custom-call | flops 603979776 | bytes 1048576 | tf_op jit(solution)/shard_map/pallas_call | solution.py:120
  7.5 5.4 %collective-permute-start.1 = (bf16[288,512]{1,0:T(8,128)(2,1)S(1)}, bf16[288,512]{1,0:T(8,128)(2,1)S(1)}, u32[]{:S(2)}, u32[]{:S(2)}) collective-permute-start(bf16[288,512]{1,0:T(8,128)(2,1)S(1)} %get-tuple-element.29), channel_id=1, source_target_pairs={{0,2},{2,4},{4,6},{10,8},{12,10},{14,12},{1,3},{3,5},{5,7},{11,9},... | collective-permute-start | bytes 884744 | tf_op jit(solution)/shard_map/ppermute | solution.py:518
  13.0 4.4 %shard_map.74.refs_2_.refs_3_ = bf16[8,4,288,256]{3,2,1,0:T(8,128)(2,1)S(1)} custom-call(s32[2]{0:T(128)S(1)} %pad_add_fusion.place_ref, bf16[4,288,512]{2,1,0:T(8,128)(2,1)S(1)} %get-tuple-element.30.ordered_ref.refs_1_.refs_2_, bf16[512,2048]{1,0:T(8,128)(2,1)S(1)} %copy-done), custom_call_target="tpu_custom_call" | custom-call | flops 2415919104 | bytes 1048576 | tf_op jit(solution)/shard_map/pallas_call | solution.py:120
  17.7 7.2 %shard_map.76 = (bf16[512,512]{1,0:T(8,128)(2,1)S(1)}, bf16[128,512]{1,0:T(8,128)(2,1)S(1)}, bf16[128,512]{1,0:T(8,128)(2,1)S(1)}, bf16[128,512]{1,0:T(8,128)(2,1)S(1)}, bf16[128,512]{1,0:T(8,128)(2,1)S(1)}) custom-call(s32[2]{0:T(128)S(1)} %pad_add_fusion.place_ref, bf16[288,512]{1,0:T(8,128)(2,1)S(1)} %collective-permute-done.2.refs_0_, ...), custom_call_target="tpu_custom_call" | custom-call | flops 2147483648 | bytes 1048576 | tf_op jit(solution)/shard_map/pallas_call | solution.py:120
  24.9 8.6 %collective-permute-start.7 = (bf16[128,512]{1,0:T(8,128)(2,1)S(1)}, bf16[128,512]{1,0:T(8,128)(2,1)S(1)}, u32[]{:S(2)}, u32[]{:S(2)}) collective-permute-start(bf16[128,512]{1,0:T(8,128)(2,1)S(1)} %get-tuple-element.38), channel_id=1, source_target_pairs={{0,8},{2,10},{4,12},{6,14},{8,0},{10,2},{12,4},{14,6},{1,9},{3,11}... | collective-permute-start | bytes 393224 | tf_op jit(solution)/shard_map/ppermute | solution.py:525
  33.5 2.0 %collective-permute-start.8 = (bf16[128,512]{1,0:T(8,128)(2,1)S(1)}, bf16[128,512]{1,0:T(8,128)(2,1)S(1)}, u32[]{:S(2)}, u32[]{:S(2)}) collective-permute-start(bf16[128,512]{1,0:T(8,128)(2,1)S(1)} %get-tuple-element.39), channel_id=1, source_target_pairs={{0,10},{2,8},{4,14},{6,12},{8,2},{10,0},{12,6},{14,4},{1,11},{3,9}... | collective-permute-start | bytes 393224 | tf_op jit(solution)/shard_map/ppermute | solution.py:525
  35.5 3.7 %collective-permute-start.10 = (bf16[128,512]{1,0:T(8,128)(2,1)S(1)}, bf16[128,512]{1,0:T(8,128)(2,1)S(1)}, u32[]{:S(2)}, u32[]{:S(2)}) collective-permute-start(bf16[128,512]{1,0:T(8,128)(2,1)S(1)} %get-tuple-element.41), channel_id=1, source_target_pairs={{0,14},{2,12},{4,10},{6,8},{8,6},{10,4},{12,2},{14,0},{1,15},{3,13... | collective-permute-start | bytes 393224 | tf_op jit(solution)/shard_map/ppermute | solution.py:525
  39.2 7.8 %shard_map.75 = (bf16[512,512]{1,0:T(8,128)(2,1)S(1)}, bf16[128,512]{1,0:T(8,128)(2,1)S(1)}, bf16[128,512]{1,0:T(8,128)(2,1)S(1)}, bf16[128,512]{1,0:T(8,128)(2,1)S(1)}, bf16[128,512]{1,0:T(8,128)(2,1)S(1)}) custom-call(s32[2]{0:T(128)S(1)} %pad_add_fusion.place_ref, bf16[288,512]{1,0:T(8,128)(2,1)S(1)} %collective-permute-done.1.refs_0_, ...), custom_call_target="tpu_custom_call" | custom-call | flops 2147483648 | bytes 1048576 | tf_op jit(solution)/shard_map/pallas_call | solution.py:120
  47.0 1.6 %collective-permute-start.4 = (bf16[128,512]{1,0:T(8,128)(2,1)S(1)}, bf16[128,512]{1,0:T(8,128)(2,1)S(1)}, u32[]{:S(2)}, u32[]{:S(2)}) collective-permute-start(bf16[128,512]{1,0:T(8,128)(2,1)S(1)} %get-tuple-element.35), channel_id=1, source_target_pairs={{0,2},{2,0},{4,6},{6,4},{8,10},{10,8},{12,14},{14,12},{1,3},{3,1},... | collective-permute-start | bytes 393224 | tf_op jit(solution)/shard_map/ppermute | solution.py:525
  48.7 2.7 %collective-permute-done.8.refs_1_ = bf16[128,512]{1,0:T(8,128)(2,1)S(1)} collective-permute-done((bf16[128,512]{1,0:T(8,128)(2,1)S(1)}, bf16[128,512]{1,0:T(8,128)(2,1)S(1)}, u32[]{:S(2)}, u32[]{:S(2)}) %collective-permute-start.8) | collective-permute-done | bytes 131104 | tf_op jit(solution)/shard_map/ppermute | solution.py:525
  51.5 2.1 %collective-permute-done.4.refs_5_.refs_1_ = bf16[128,512]{1,0:T(8,128)(2,1)S(1)} collective-permute-done((bf16[128,512]{1,0:T(8,128)(2,1)S(1)}, bf16[128,512]{1,0:T(8,128)(2,1)S(1)}, u32[]{:S(2)}, u32[]{:S(2)}) %collective-permute-start.4) | collective-permute-done | bytes 131104 | tf_op jit(solution)/shard_map/ppermute | solution.py:525
  54.3 3.0 %collective-permute-done.6.refs_7_.refs_3_ = bf16[128,512]{1,0:T(8,128)(2,1)S(1)} collective-permute-done((bf16[128,512]{1,0:T(8,128)(2,1)S(1)}, bf16[128,512]{1,0:T(8,128)(2,1)S(1)}, u32[]{:S(2)}, u32[]{:S(2)}) %collective-permute-start.6) | collective-permute-done | bytes 131104 | tf_op jit(solution)/shard_map/ppermute | solution.py:525
  57.3 6.7 %shard_map.77 = (bf16[128,512]{1,0:T(8,128)(2,1)S(1)}, bf16[128,512]{1,0:T(8,128)(2,1)S(1)}, bf16[128,512]{1,0:T(8,128)(2,1)S(1)}, bf16[128,512]{1,0:T(8,128)(2,1)S(1)}, bf16[4,256,1024]{2,1,0:T(8,128)(2,1)S(1)}) custom-call(s32[2]{0:T(128)S(1)} %pad_add_fusion.place_ref, bf16[128,512]{1,0:T(8,128)(2,1)S(1)} %collective-permute-done.7.refs_0_, ...), custom_call_target="tpu_custom_call" | custom-call | flops 1610612736 | bytes 1048576 | tf_op jit(solution)/shard_map/pallas_call | solution.py:120
  64.1 5.5 %shard_map.78 = (bf16[128,512]{1,0:T(8,128)(2,1)S(1)}, bf16[128,512]{1,0:T(8,128)(2,1)S(1)}, bf16[128,512]{1,0:T(8,128)(2,1)S(1)}, bf16[128,512]{1,0:T(8,128)(2,1)S(1)}) custom-call(s32[2]{0:T(128)S(1)} %pad_add_fusion.place_ref, bf16[128,512]{1,0:T(8,128)(2,1)S(1)} %get-tuple-element.34.refs_4_.refs_0_, ...), custom_call_target="tpu_custom_call" | custom-call | flops 1610612736 | bytes 1048576 | tf_op jit(solution)/shard_map/pallas_call | solution.py:120
  69.5 1.6 %collective-permute-start.11 = (bf16[128,512]{1,0:T(8,128)(2,1)S(1)}, bf16[128,512]{1,0:T(8,128)(2,1)S(1)}, u32[]{:S(2)}, u32[]{:S(2)}) collective-permute-start(bf16[128,512]{1,0:T(8,128)(2,1)S(1)} %get-tuple-element.44), channel_id=1, source_target_pairs={{0,2},{2,0},{4,6},{6,4},{8,10},{10,8},{12,14},{14,12},{1,3},{3,1},... | collective-permute-start | bytes 393224 | tf_op jit(solution)/shard_map/ppermute | solution.py:525
  71.1 1.4 %collective-permute-start.12 = (bf16[128,512]{1,0:T(8,128)(2,1)S(1)}, bf16[128,512]{1,0:T(8,128)(2,1)S(1)}, u32[]{:S(2)}, u32[]{:S(2)}) collective-permute-start(bf16[128,512]{1,0:T(8,128)(2,1)S(1)} %get-tuple-element.45), channel_id=1, source_target_pairs={{0,4},{2,6},{4,0},{6,2},{8,12},{10,14},{12,8},{14,10},{1,5},{3,7},... | collective-permute-start | bytes 393224 | tf_op jit(solution)/shard_map/ppermute | solution.py:525
  73.1 2.0 %collective-permute-start.14 = (bf16[128,512]{1,0:T(8,128)(2,1)S(1)}, bf16[128,512]{1,0:T(8,128)(2,1)S(1)}, u32[]{:S(2)}, u32[]{:S(2)}) collective-permute-start(bf16[128,512]{1,0:T(8,128)(2,1)S(1)} %get-tuple-element.47), channel_id=1, source_target_pairs={{0,8},{2,10},{4,12},{6,14},{8,0},{10,2},{12,4},{14,6},{1,9},{3,11}... | collective-permute-start | bytes 393224 | tf_op jit(solution)/shard_map/ppermute | solution.py:525
  75.1 1.8 %collective-permute-start.15 = (bf16[128,512]{1,0:T(8,128)(2,1)S(1)}, bf16[128,512]{1,0:T(8,128)(2,1)S(1)}, u32[]{:S(2)}, u32[]{:S(2)}) collective-permute-start(bf16[128,512]{1,0:T(8,128)(2,1)S(1)} %get-tuple-element.48), channel_id=1, source_target_pairs={{0,10},{2,8},{4,14},{6,12},{8,2},{10,0},{12,6},{14,4},{1,11},{3,9}... | collective-permute-start | bytes 393224 | tf_op jit(solution)/shard_map/ppermute | solution.py:525
  77.0 2.3 %collective-permute-start.16 = (bf16[128,512]{1,0:T(8,128)(2,1)S(1)}, bf16[128,512]{1,0:T(8,128)(2,1)S(1)}, u32[]{:S(2)}, u32[]{:S(2)}) collective-permute-start(bf16[128,512]{1,0:T(8,128)(2,1)S(1)} %get-tuple-element.49), channel_id=1, source_target_pairs={{0,12},{2,14},{4,8},{6,10},{8,4},{10,6},{12,0},{14,2},{1,13},{3,15... | collective-permute-start | bytes 393224 | tf_op jit(solution)/shard_map/ppermute | solution.py:525
  81.8 9.1 %collective-permute-done.14.refs_6_ = bf16[128,512]{1,0:T(8,128)(2,1)S(1)} collective-permute-done((bf16[128,512]{1,0:T(8,128)(2,1)S(1)}, bf16[128,512]{1,0:T(8,128)(2,1)S(1)}, u32[]{:S(2)}, u32[]{:S(2)}) %collective-permute-start.14) | collective-permute-done | bytes 131104 | tf_op jit(solution)/shard_map/ppermute | solution.py:525
  90.9 3.7 %collective-permute-done.15.refs_7_ = bf16[128,512]{1,0:T(8,128)(2,1)S(1)} collective-permute-done((bf16[128,512]{1,0:T(8,128)(2,1)S(1)}, bf16[128,512]{1,0:T(8,128)(2,1)S(1)}, u32[]{:S(2)}, u32[]{:S(2)}) %collective-permute-start.15) | collective-permute-done | bytes 131104 | tf_op jit(solution)/shard_map/ppermute | solution.py:525
  95.5 1.6 %shard_map.80.rest_0_ = bf16[2,2,8,2,16,512]{5,4,3,2,1,0:T(8,128)(2,1)} custom-call(s32[2]{0:T(128)S(1)} %pad_add_fusion.place_ref, bf16[2,256,512]{2,1,0:T(8,128)(2,1)S(1)} %get-tuple-element.52.ready_ref), custom_call_target="tpu_custom_call" | custom-call | flops 268435456 | bytes 1048576 | tf_op jit(solution)/shard_map/pallas_call | solution.py:461
  97.4 1.6 %shard_map.81 = bf16[2,2,8,2,16,512]{5,4,3,2,1,0:T(8,128)(2,1)} custom-call(s32[2]{0:T(128)S(1)} %pad_add_fusion.place_ref, bf16[2,256,512]{2,1,0:T(8,128)(2,1)S(1)} %collective-permute-done.18.ready_ref, bf16[2,2,8,2,16,512]{5,4,3,2,1,0:T(8,128)(2,1)} %shard_map.80.rest_0_), custom_call_target="tpu_custom_call", output_to_operand_aliasing={{}: (2, {})} | custom-call | flops 268435456 | bytes 1048576 | tf_op jit(solution)/shard_map/pallas_call | solution.py:461
  (38 shorter events, 9.2 us)
Async XLA Ops:
  0.0 13.0 %copy-start = (bf16[512,2048]{1,0:T(8,128)(2,1)S(1)}, bf16[512,2048]{1,0:T(8,128)(2,1)}, u32[]{:S(2)}) copy-start(bf16[512,2048]{1,0:T(8,128)(2,1)} %refs_4_.3) | copy-start | bytes 6291460
  0.0 3.0 %collective-permute-start = (bf16[4,256,512]{2,1,0:T(8,128)(2,1)}, bf16[4,256,512]{2,1,0:T(8,128)(2,1)S(1)}, u32[]{:S(2)}, u32[]{:S(2)}) collective-permute-start(bf16[4,256,512]{2,1,0:T(8,128)(2,1)} %own_ref.1), channel_id=1, source_target_pairs={{0,1},{1,0},{2,3},{3,2},{4,5},{5,4},{6,7},{7,6},{8,9},{9,8},{10,11... | collective-permute-start | bytes 3145736 | tf_op jit(solution)/shard_map/ppermute | solution.py:509
  5.5 12.1 %collective-permute-start.3 = (bf16[288,512]{1,0:T(8,128)(2,1)S(1)}, bf16[288,512]{1,0:T(8,128)(2,1)S(1)}, u32[]{:S(2)}, u32[]{:S(2)}) collective-permute-start(bf16[288,512]{1,0:T(8,128)(2,1)S(1)} %get-tuple-element.32), channel_id=1, source_target_pairs={{2,0},{4,2},{6,4},{8,10},{10,12},{12,14},{3,1},{5,3},{7,5},{9,11},... | collective-permute-start | bytes 884744 | tf_op jit(solution)/shard_map/ppermute | solution.py:515
  6.8 10.8 %collective-permute-start.2 = (bf16[288,512]{1,0:T(8,128)(2,1)S(1)}, bf16[288,512]{1,0:T(8,128)(2,1)S(1)}, u32[]{:S(2)}, u32[]{:S(2)}) collective-permute-start(bf16[288,512]{1,0:T(8,128)(2,1)S(1)} %get-tuple-element.29), channel_id=1, source_target_pairs={{6,8},{8,6},{7,9},{9,7},{22,24},{24,22},{23,25},{25,23}} | collective-permute-start | bytes 884744 | tf_op jit(solution)/shard_map/ppermute | solution.py:514
  7.5 31.7 %collective-permute-start.1 = (bf16[288,512]{1,0:T(8,128)(2,1)S(1)}, bf16[288,512]{1,0:T(8,128)(2,1)S(1)}, u32[]{:S(2)}, u32[]{:S(2)}) collective-permute-start(bf16[288,512]{1,0:T(8,128)(2,1)S(1)} %get-tuple-element.29), channel_id=1, source_target_pairs={{0,2},{2,4},{4,6},{10,8},{12,10},{14,12},{1,3},{3,5},{5,7},{11,9},... | collective-permute-start | bytes 884744 | tf_op jit(solution)/shard_map/ppermute | solution.py:518
  13.0 4.7 %copy-start.1 = (bf16[2048,512]{1,0:T(8,128)(2,1)S(1)}, bf16[2048,512]{1,0:T(8,128)(2,1)}, u32[]{:S(2)}) copy-start(bf16[2048,512]{1,0:T(8,128)(2,1)} %refs_6_.2) | copy-start | bytes 6291460
  13.0 4.7 %copy-start.2 = (f32[3,3,2048]{2,1,0:T(4,128)S(1)}, f32[3,3,2048]{2,1,0:T(4,128)}, u32[]{:S(2)}) copy-start(f32[3,3,2048]{2,1,0:T(4,128)} %refs_5_.4) | copy-start | bytes 221188
  24.9 23.9 %collective-permute-start.7 = (bf16[128,512]{1,0:T(8,128)(2,1)S(1)}, bf16[128,512]{1,0:T(8,128)(2,1)S(1)}, u32[]{:S(2)}, u32[]{:S(2)}) collective-permute-start(bf16[128,512]{1,0:T(8,128)(2,1)S(1)} %get-tuple-element.38), channel_id=1, source_target_pairs={{0,8},{2,10},{4,12},{6,14},{8,0},{10,2},{12,4},{14,6},{1,9},{3,11}... | collective-permute-start | bytes 393224 | tf_op jit(solution)/shard_map/ppermute | solution.py:525
  33.5 18.0 %collective-permute-start.8 = (bf16[128,512]{1,0:T(8,128)(2,1)S(1)}, bf16[128,512]{1,0:T(8,128)(2,1)S(1)}, u32[]{:S(2)}, u32[]{:S(2)}) collective-permute-start(bf16[128,512]{1,0:T(8,128)(2,1)S(1)} %get-tuple-element.39), channel_id=1, source_target_pairs={{0,10},{2,8},{4,14},{6,12},{8,2},{10,0},{12,6},{14,4},{1,11},{3,9}... | collective-permute-start | bytes 393224 | tf_op jit(solution)/shard_map/ppermute | solution.py:525
  35.5 16.0 %collective-permute-start.9 = (bf16[128,512]{1,0:T(8,128)(2,1)S(1)}, bf16[128,512]{1,0:T(8,128)(2,1)S(1)}, u32[]{:S(2)}, u32[]{:S(2)}) collective-permute-start(bf16[128,512]{1,0:T(8,128)(2,1)S(1)} %get-tuple-element.40), channel_id=1, source_target_pairs={{0,12},{2,14},{4,8},{6,10},{8,4},{10,6},{12,0},{14,2},{1,13},{3,15... | collective-permute-start | bytes 393224 | tf_op jit(solution)/shard_map/ppermute | solution.py:525
  35.5 21.9 %copy-start.4 = (bf16[512,1536]{1,0:T(8,128)(2,1)S(1)}, bf16[512,1536]{1,0:T(8,128)(2,1)}, u32[]{:S(2)}) copy-start(bf16[512,1536]{1,0:T(8,128)(2,1)} %refs_5_.5) | copy-start | bytes 4718596
  35.5 21.9 %copy-start.6 = (bf16[512,512]{1,0:T(8,128)(2,1)S(1)}, bf16[512,512]{1,0:T(8,128)(2,1)}, u32[]{:S(2)}) copy-start(bf16[512,512]{1,0:T(8,128)(2,1)} %refs_6_.3) | copy-start | bytes 1572868
  35.5 16.0 %collective-permute-start.10 = (bf16[128,512]{1,0:T(8,128)(2,1)S(1)}, bf16[128,512]{1,0:T(8,128)(2,1)S(1)}, u32[]{:S(2)}, u32[]{:S(2)}) collective-permute-start(bf16[128,512]{1,0:T(8,128)(2,1)S(1)} %get-tuple-element.41), channel_id=1, source_target_pairs={{0,14},{2,12},{4,10},{6,8},{8,6},{10,4},{12,2},{14,0},{1,15},{3,13... | collective-permute-start | bytes 393224 | tf_op jit(solution)/shard_map/ppermute | solution.py:525
  47.0 6.5 %collective-permute-start.4 = (bf16[128,512]{1,0:T(8,128)(2,1)S(1)}, bf16[128,512]{1,0:T(8,128)(2,1)S(1)}, u32[]{:S(2)}, u32[]{:S(2)}) collective-permute-start(bf16[128,512]{1,0:T(8,128)(2,1)S(1)} %get-tuple-element.35), channel_id=1, source_target_pairs={{0,2},{2,0},{4,6},{6,4},{8,10},{10,8},{12,14},{14,12},{1,3},{3,1},... | collective-permute-start | bytes 393224 | tf_op jit(solution)/shard_map/ppermute | solution.py:525
  48.7 5.6 %collective-permute-start.5 = (bf16[128,512]{1,0:T(8,128)(2,1)S(1)}, bf16[128,512]{1,0:T(8,128)(2,1)S(1)}, u32[]{:S(2)}, u32[]{:S(2)}) collective-permute-start(bf16[128,512]{1,0:T(8,128)(2,1)S(1)} %get-tuple-element.36), channel_id=1, source_target_pairs={{0,4},{2,6},{4,0},{6,2},{8,12},{10,14},{12,8},{14,10},{1,5},{3,7},... | collective-permute-start | bytes 393224 | tf_op jit(solution)/shard_map/ppermute | solution.py:525
  51.5 5.9 %collective-permute-start.6 = (bf16[128,512]{1,0:T(8,128)(2,1)S(1)}, bf16[128,512]{1,0:T(8,128)(2,1)S(1)}, u32[]{:S(2)}, u32[]{:S(2)}) collective-permute-start(bf16[128,512]{1,0:T(8,128)(2,1)S(1)} %get-tuple-element.37), channel_id=1, source_target_pairs={{0,6},{2,4},{4,2},{6,0},{8,14},{10,12},{12,10},{14,8},{1,7},{3,5},... | collective-permute-start | bytes 393224 | tf_op jit(solution)/shard_map/ppermute | solution.py:525
  69.5 7.4 %collective-permute-start.11 = (bf16[128,512]{1,0:T(8,128)(2,1)S(1)}, bf16[128,512]{1,0:T(8,128)(2,1)S(1)}, u32[]{:S(2)}, u32[]{:S(2)}) collective-permute-start(bf16[128,512]{1,0:T(8,128)(2,1)S(1)} %get-tuple-element.44), channel_id=1, source_target_pairs={{0,2},{2,0},{4,6},{6,4},{8,10},{10,8},{12,14},{14,12},{1,3},{3,1},... | collective-permute-start | bytes 393224 | tf_op jit(solution)/shard_map/ppermute | solution.py:525
  71.1 8.6 %collective-permute-start.12 = (bf16[128,512]{1,0:T(8,128)(2,1)S(1)}, bf16[128,512]{1,0:T(8,128)(2,1)S(1)}, u32[]{:S(2)}, u32[]{:S(2)}) collective-permute-start(bf16[128,512]{1,0:T(8,128)(2,1)S(1)} %get-tuple-element.45), channel_id=1, source_target_pairs={{0,4},{2,6},{4,0},{6,2},{8,12},{10,14},{12,8},{14,10},{1,5},{3,7},... | collective-permute-start | bytes 393224 | tf_op jit(solution)/shard_map/ppermute | solution.py:525
  72.5 9.3 %collective-permute-start.13 = (bf16[128,512]{1,0:T(8,128)(2,1)S(1)}, bf16[128,512]{1,0:T(8,128)(2,1)S(1)}, u32[]{:S(2)}, u32[]{:S(2)}) collective-permute-start(bf16[128,512]{1,0:T(8,128)(2,1)S(1)} %get-tuple-element.46), channel_id=1, source_target_pairs={{0,6},{2,4},{4,2},{6,0},{8,14},{10,12},{12,10},{14,8},{1,7},{3,5},... | collective-permute-start | bytes 393224 | tf_op jit(solution)/shard_map/ppermute | solution.py:525
  73.1 17.8 %collective-permute-start.14 = (bf16[128,512]{1,0:T(8,128)(2,1)S(1)}, bf16[128,512]{1,0:T(8,128)(2,1)S(1)}, u32[]{:S(2)}, u32[]{:S(2)}) collective-permute-start(bf16[128,512]{1,0:T(8,128)(2,1)S(1)} %get-tuple-element.47), channel_id=1, source_target_pairs={{0,8},{2,10},{4,12},{6,14},{8,0},{10,2},{12,4},{14,6},{1,9},{3,11}... | collective-permute-start | bytes 393224 | tf_op jit(solution)/shard_map/ppermute | solution.py:525
  75.1 19.4 %collective-permute-start.15 = (bf16[128,512]{1,0:T(8,128)(2,1)S(1)}, bf16[128,512]{1,0:T(8,128)(2,1)S(1)}, u32[]{:S(2)}, u32[]{:S(2)}) collective-permute-start(bf16[128,512]{1,0:T(8,128)(2,1)S(1)} %get-tuple-element.48), channel_id=1, source_target_pairs={{0,10},{2,8},{4,14},{6,12},{8,2},{10,0},{12,6},{14,4},{1,11},{3,9}... | collective-permute-start | bytes 393224 | tf_op jit(solution)/shard_map/ppermute | solution.py:525
  77.0 17.6 %collective-permute-start.16 = (bf16[128,512]{1,0:T(8,128)(2,1)S(1)}, bf16[128,512]{1,0:T(8,128)(2,1)S(1)}, u32[]{:S(2)}, u32[]{:S(2)}) collective-permute-start(bf16[128,512]{1,0:T(8,128)(2,1)S(1)} %get-tuple-element.49), channel_id=1, source_target_pairs={{0,12},{2,14},{4,8},{6,10},{8,4},{10,6},{12,0},{14,2},{1,13},{3,15... | collective-permute-start | bytes 393224 | tf_op jit(solution)/shard_map/ppermute | solution.py:525
  79.8 14.8 %collective-permute-start.17 = (bf16[128,512]{1,0:T(8,128)(2,1)S(1)}, bf16[128,512]{1,0:T(8,128)(2,1)S(1)}, u32[]{:S(2)}, u32[]{:S(2)}) collective-permute-start(bf16[128,512]{1,0:T(8,128)(2,1)S(1)} %get-tuple-element.50), channel_id=1, source_target_pairs={{0,14},{2,12},{4,10},{6,8},{8,6},{10,4},{12,2},{14,0},{1,15},{3,13... | collective-permute-start | bytes 393224 | tf_op jit(solution)/shard_map/ppermute | solution.py:525
  95.5 2.0 %collective-permute-start.18 = (bf16[2,256,512]{2,1,0:T(8,128)(2,1)S(1)}, bf16[2,256,512]{2,1,0:T(8,128)(2,1)S(1)}, u32[]{:S(2)}, u32[]{:S(2)}) collective-permute-start(bf16[2,256,512]{2,1,0:T(8,128)(2,1)S(1)} %get-tuple-element.51), channel_id=1, source_target_pairs={{0,1},{1,0},{2,3},{3,2},{4,5},{5,4},{6,7},{7,6},{8,9},{9,8},{10,11... | collective-permute-start | bytes 1572872 | tf_op jit(solution)/shard_map/ppermute | solution.py:544
  (2 other events, 5.9 us)

commit v5 on v4

--- a/solution.py
+++ b/solution.py
@@ -89,22 +89,29 @@
     return result.reshape(count, members, channels)
 
 
+def pick(place_ref, source_ref, row, size, mine, stride_cols, share):
+    cols = source_ref.shape[1]
+    col = place_ref[0] if mine else 1 - place_ref[0]
+    at = lax.broadcasted_iota(jnp.int32, (size, cols), 0)
+    want = (at % GRID) * stride_cols + at // GRID + (place_ref[0] * share - 1 - col * cols)
+    select = (lax.broadcasted_iota(jnp.int32, (size, cols), 1) == want).astype(jnp.bfloat16)
+    return jnp.dot(select, source_ref[row], preferred_element_type=jnp.float32)
+
+
+def arrange_mine_kernel(place_ref, own_ref, ordered_ref, *, stride_cols, share):
+    for row in range(own_ref.shape[0]):
+        ordered_ref[row] = pick(
+            place_ref, own_ref, row, ordered_ref.shape[1], True, stride_cols, share
+        ).astype(jnp.bfloat16)
+
+
 def arrange_kernel(
-    place_ref, own_ref, other_ref, ordered_ref, far_ref, near_ref, *, stride_cols, share, owners
+    place_ref, mine_ref, other_ref, ordered_ref, far_ref, near_ref, *, stride_cols, share, owners
 ):
-    rows, cols, _ = own_ref.shape
-    size = ordered_ref.shape[1]
-    col = place_ref[0]
-    at = lax.broadcasted_iota(jnp.int32, (size, cols), 0)
-    want = (at % GRID) * stride_cols + at // GRID + (col * share - 1)
-    index = lax.broadcasted_iota(jnp.int32, (size, cols), 1)
-    select_own = (index + col * cols == want).astype(jnp.bfloat16)
-    select_other = (index + (1 - col) * cols == want).astype(jnp.bfloat16)
+    rows, size, _ = ordered_ref.shape
     for row in range(rows):
-        picked = jnp.dot(select_own, own_ref[row], preferred_element_type=jnp.float32) + jnp.dot(
-            select_other, other_ref[row], preferred_element_type=jnp.float32
-        )
-        ordered_ref[row] = picked.astype(jnp.bfloat16)
+        picked = pick(place_ref, other_ref, row, size, False, stride_cols, share)
+        ordered_ref[row] = (picked + mine_ref[row].astype(jnp.float32)).astype(jnp.bfloat16)
     is_low = place_ref[1] < owners
     first, last = ordered_ref[0], ordered_ref[rows - 1]
     far_ref[...] = jnp.where(is_low, first, last)
@@ -128,15 +135,27 @@
     )(place, *operands)
 
 
-def arrange(place, own, other, stride_cols, share, owners):
+def arrange_mine(place, own, stride_cols, share):
     rows, cols, channels = own.shape
     size = (share + 2) * GRID
     return call(
+        functools.partial(arrange_mine_kernel, stride_cols=stride_cols, share=share),
+        place,
+        [own],
+        [(rows, size, channels)],
+        2 * rows * size * cols * channels,
+        8 * MIB,
+    )[0]
+
+
+def arrange(place, mine, other, stride_cols, share, owners):
+    rows, size, channels = mine.shape
+    return call(
         functools.partial(arrange_kernel, stride_cols=stride_cols, share=share, owners=owners),
         place,
-        [own, other],
+        [mine, other],
         [(rows, size, channels), (size, channels), (size, channels)],
-        4 * rows * size * cols * channels,
+        2 * rows * size * other.shape[1] * channels,
         8 * MIB,
     )
 
@@ -171,11 +190,11 @@
     )[0]
 
 
-def mbconv_kernel(place_ref, *refs, far, share, stride_rows, halos, owners):
+def mbconv_kernel(place_ref, *refs, far, part, span, stride_rows, halos, owners):
     halo_refs = refs[:halos]
     ordered_ref, own_ref, expand_ref, taps_ref, project_ref, gain_ref, mbconv_ref = refs[halos : halos + 7]
-    normed_refs = refs[halos + 7 : halos + 7 + owners]
-    edge_rows, depth_a, depth_b, acc = refs[halos + 7 + owners :]
+    normed_refs = refs[halos + 7 : halos + 7 + len(part)]
+    edge_rows, depth_a, depth_b, acc = refs[halos + 7 + len(part) :]
     hidden = expand_ref.shape[1]
     rows = ordered_ref.shape[0]
     row_blocks = rows // stride_rows
@@ -183,9 +202,12 @@
     half_at = 1 - spot_half if far else spot_half
     depth_b[...] = jnp.zeros_like(depth_b)
     acc[...] = jnp.zeros_like(acc)
-    halo = halo_refs[0][...]
+    nearest = (place_ref[1] % owners) ^ part[0]
+    begin = pl.multiple_of(nearest // len(part) * (span * GRID), GRID)
+    size = edge_rows.shape[1]
+    halo = halo_refs[0][pl.ds(begin, size), :]
     for ref in halo_refs[1:]:
-        halo = halo + ref[...]
+        halo = halo + ref[pl.ds(begin, size), :]
 
     def step(hm, index, carry):
         for half, depth in ((0, depth_a), (1, depth_b)):
@@ -211,7 +233,7 @@
                     ]
                     for dr in range(3)
                 ]
-                for pair in range(0, share, 2):
+                for pair in range(0, span, 2):
                     parts = {}
                     for low in range(0, GRID, SUBLANES):
                         source = []
@@ -223,7 +245,7 @@
                                     at += low
                                     tiles.append(edge_rows[half, at : at + SUBLANES, lanes])
                                 else:
-                                    tile = own_ref[block, row - 1, at : at + GRID, lanes]
+                                    tile = own_ref[block, row - 1, pl.ds(begin + at, GRID), lanes]
                                     tiles.append(tile.astype(jnp.float32)[low : low + SUBLANES])
                             source.append(tiles)
                         for b in (0, 1):
@@ -260,13 +282,13 @@
         preferred_element_type=jnp.float32,
     )
     members = row_blocks * GRID
-    items = share // owners
-    for k, normed_ref in enumerate(normed_refs):
-        owner = (place_ref[1] % owners) ^ k
+    items = span // len(part)
+    for k, normed_ref in zip(part, normed_refs):
+        owner = ((place_ref[1] % owners) ^ k) % len(part)
         for item in range(items):
             for rb in range(row_blocks):
                 spot = pl.multiple_of((owner * items + item) * members + rb * GRID, GRID)
-                column = pl.multiple_of((owner * items + item + 1) * GRID, GRID)
+                column = pl.multiple_of(begin + (owner * items + item + 1) * GRID, GRID)
                 tokens = ordered_ref[rb * stride_rows + half_at, pl.ds(column, GRID), :]
                 mixed = tokens.astype(jnp.float32) + acc[pl.ds(spot, GRID), :] * BRANCH_SCALE
                 mixed = mixed.astype(jnp.bfloat16)
@@ -281,22 +303,22 @@
                 ).astype(jnp.bfloat16)
 
 
-def mbconv_half(far, share, stride_rows, owners, place, halos, ordered, own, weights):
-    rows, size, channels = ordered.shape
+def mbconv_part(far, part, span, stride_rows, owners, place, halos, ordered, own, weights):
+    rows, _, channels = ordered.shape
     hidden = weights[0].shape[1]
-    count = rows // stride_rows * share * GRID
+    count = rows // stride_rows * span * GRID
     mbconv, *normed = call(
         functools.partial(
-            mbconv_kernel, far=far, share=share, stride_rows=stride_rows, halos=len(halos),
-            owners=owners,
+            mbconv_kernel, far=far, part=part, span=span, stride_rows=stride_rows,
+            halos=len(halos), owners=owners,
         ),
         place,
         [*halos, ordered, own, *weights],
-        [(count, channels)] + [(count // owners, channels)] * owners,
+        [(count, channels)] + [(count // len(part), channels)] * len(part),
         4 * count * channels * hidden,
         8 * MIB,
         [
-            pltpu.VMEM((2, size, BLOCK), jnp.float32),
+            pltpu.VMEM((2, (span + 2) * GRID, BLOCK), jnp.float32),
             pltpu.VMEM((count, BLOCK), jnp.bfloat16),
             pltpu.VMEM((count, BLOCK), jnp.bfloat16),
             pltpu.VMEM((count, channels), jnp.float32),
@@ -305,25 +327,24 @@
     return mbconv, normed
 
 
-def attend_kernel(place_ref, *refs, per, far, count):
+def attend_kernel(place_ref, *refs, per, first, count):
     x_refs = refs[:count]
-    attend_ref, output_ref = refs[-2 - count - far], refs[-1 - count - far]
-    out_refs = refs[-count - far :][:count]
+    attend_ref, output_ref = refs[-2 - count - first], refs[-1 - count - first]
+    out_refs = refs[-count - first :][:count]
     channels = x_refs[0].shape[1]
     scale = LOG2E / math.sqrt(HEAD_DIM)
     fold = LANES // HEAD_DIM
-    kv_ref = refs[-1] if far else refs[count]
+    kv_ref = refs[-1] if first else refs[count]
     members = kv_ref.shape[1]
     key_lane = lax.broadcasted_iota(jnp.int32, (members, LANES), 1) // HEAD_DIM
     query_lane = lax.broadcasted_iota(jnp.int32, (count * per, LANES), 1) // HEAD_DIM
-    ones = jnp.ones((members, LANES), jnp.bfloat16)
 
     def step(item, carry):
         spot = pl.ds(pl.multiple_of(item * per, per), per)
         x = jnp.concatenate([ref[spot, :] for ref in x_refs], axis=0)
-        if far:
+        if first:
             everything = jnp.concatenate(
-                [x] + [ref[spot, :] for ref in refs[count : -2 - count - far]], axis=0
+                [x] + [ref[spot, :] for ref in refs[count : -2 - count - first]], axis=0
             )
             for begin in range(0, 2 * channels, BLOCK):
                 kv_ref[item, :, begin : begin + BLOCK] = jnp.dot(
@@ -341,25 +362,32 @@
             query = (query * scale).astype(jnp.bfloat16)
             key = kv_ref[item, :, begin : begin + LANES]
             value = kv_ref[item, :, channels + begin : channels + begin + LANES]
-            upper = None
+            stacked = jnp.concatenate(
+                [jnp.where(query_lane == head, query, jnp.zeros_like(query)) for head in range(fold)],
+                axis=0,
+            )
+            scores = lax.dot_general(
+                stacked, key, (((1,), (1,)), ((), ())), preferred_element_type=jnp.float32
+            )
+            weight = jnp.exp2(scores - jnp.max(scores, axis=-1, keepdims=True)).astype(jnp.bfloat16)
+            upper = lower = None
             for head in range(fold):
-                key_head = jnp.where(key_lane == head, key, jnp.zeros_like(key))
-                value_head = jnp.where(key_lane == head, value, jnp.zeros_like(value))
-                scores = lax.dot_general(
-                    query, key_head, (((1,), (1,)), ((), ())), preferred_element_type=jnp.float32
+                value_head = jnp.where(
+                    key_lane == head,
+                    value,
+                    (key_lane == (head + 1) % fold).astype(jnp.bfloat16),
                 )
-                top = jnp.max(scores, axis=-1, keepdims=True)
-                weight = jnp.exp2(scores - top).astype(jnp.bfloat16)
                 mixed = jnp.dot(
-                    weight,
-                    jnp.concatenate([value_head, ones], axis=1),
+                    weight[head * count * per : (head + 1) * count * per],
+                    value_head,
                     preferred_element_type=jnp.float32,
                 )
                 if upper is None:
-                    upper, lower = mixed[:, :LANES], mixed[:, LANES:]
+                    upper = lower = mixed
                 else:
-                    upper = upper + mixed[:, :LANES]
-                    lower = jnp.where(query_lane == head, mixed[:, LANES:], lower)
+                    upper = jnp.where(query_lane == head, mixed, upper)
+                    lower = jnp.where(query_lane == (head + 1) % fold, mixed, lower)
+            lower = pltpu.roll(lower, LANES - HEAD_DIM, 1)
             tiles.append((upper / lower).astype(jnp.bfloat16))
         heads_out = jnp.concatenate(tiles, axis=1)
         result = jnp.dot(heads_out, output_ref[...], preferred_element_type=jnp.float32)
@@ -371,55 +399,54 @@
     lax.fori_loop(0, x_refs[0].shape[0] // per, step, 0)
 
 
-def attend_half(place, pieces, others, far, per, attend_weight, output_weight):
+def attend_part(place, pieces, others, first, per, attend_weight, output_weight):
     size, channels = pieces[0].shape
     items = size // per
-    members = 2 * len(pieces) * per
+    members = (len(pieces) + len(others)) * per if first else others[0].shape[1]
     shapes = [p.shape for p in pieces]
-    if far:
+    if first:
         shapes.append((items, members, 2 * channels))
     return call(
-        functools.partial(attend_kernel, per=per, far=far, count=len(pieces)),
+        functools.partial(attend_kernel, per=per, first=first, count=len(pieces)),
         place,
         [*pieces, *others, attend_weight, output_weight],
         shapes,
-        items * members * channels * (4 * channels + 4 * members),
+        items * len(pieces) * per * channels * (8 * channels + 4 * members),
         8 * MIB,
     )
 
 
-def add_kernel(place_ref, *refs, owners):
-    halves = len(refs) // (1 + owners)
+def add_kernel(place_ref, *refs, parts, owners):
     keep_ref, send_ref = refs[-2:]
+    back_refs = list(refs[len(parts) : -2])
     is_left = place_ref[0] == 0
-    for half in range(halves):
-        mbconv_ref = refs[half]
+    for (far, part), mbconv_ref in zip(parts, refs):
         channels = mbconv_ref.shape[1]
-        for k in range(owners):
-            back_ref = refs[halves + half * owners + k]
+        for k in part:
+            back_ref = back_refs.pop(0)
             size = back_ref.shape[0]
-            base = ((place_ref[1] % owners) ^ k) * size
+            owner = (place_ref[1] % owners) ^ k
             for at in range(0, size, 2 * GRID):
-                spot = pl.multiple_of(base + at, 2 * GRID)
+                spot = pl.multiple_of(owner % len(part) * size + at, 2 * GRID)
                 total = (
                     back_ref[at : at + 2 * GRID, :].astype(jnp.float32)
                     + mbconv_ref[pl.ds(spot, 2 * GRID), :].astype(jnp.float32)
                 ).reshape(2, 2, SUBLANES, channels)
                 left = total[:, 0].reshape(GRID, channels)
                 right = total[:, 1].reshape(GRID, channels)
-                to = pl.ds(pl.multiple_of(spot // 2, GRID), GRID)
-                keep_ref[half, to, :] = jnp.where(is_left, left, right).astype(jnp.bfloat16)
-                send_ref[half, to, :] = jnp.where(is_left, right, left).astype(jnp.bfloat16)
-
-
-def add_halves(place, mbconvs, backs):
-    count, channels = mbconvs[0].shape
+                to = pl.ds(pl.multiple_of((owner * size + at) // 2, GRID), GRID)
+                keep_ref[far, to, :] = jnp.where(is_left, left, right).astype(jnp.bfloat16)
+                send_ref[far, to, :] = jnp.where(is_left, right, left).astype(jnp.bfloat16)
+
+
+def add_parts(place, parts, owners, mbconvs, backs):
+    size, channels = backs[0][0].shape
     return call(
-        functools.partial(add_kernel, owners=len(backs[0])),
+        functools.partial(add_kernel, parts=parts, owners=owners),
         place,
-        [*mbconvs, *backs[0], *backs[1]],
-        [(len(mbconvs), count // 2, channels)] * 2,
-        count * channels * 64,
+        [*mbconvs, *[b for back in backs for b in back]],
+        [(HALVES, owners * size // 2, channels)] * 2,
+        2 * owners * size * channels * 64,
         6 * MIB,
     )
 
@@ -486,6 +513,7 @@
         and stride_rows == HALVES
         and rows == 2 * stride_rows
         and cols == SUBLANES * stride_cols
+        and owners % 2 == 0
         and stride_cols % (2 * col_count * owners) == 0
         and channels % BLOCK == 0
         and hidden % (2 * BLOCK) == 0
@@ -507,7 +535,8 @@
     place = jnp.stack([lax.axis_index("col"), lax.axis_index("row")]).astype(jnp.int32)
 
     other = lax.ppermute(tokens, "col", swap)
-    ordered, to_ends, to_middle = arrange(place, tokens, other, stride_cols, share, owners)
+    mine = arrange_mine(place, tokens, stride_cols, share)
+    ordered, to_ends, to_middle = arrange(place, mine, other, stride_cols, share, owners)
     outward = [(r, r - 1) for r in range(1, owners)]
     outward += [(r, r + 1) for r in range(owners, row_count - 1)]
     far_halos = [
@@ -518,29 +547,38 @@
     near_halos = [lax.ppermute(to_middle, "row", [(t, f) for f, t in outward])]
     weights = (expand_weight, depth_kernel, project_weight, norm_gain.reshape(1, -1))
 
-    def exchange(arrays, far):
+    def exchange(arrays, far, part):
         return [
             array
             if k + far * owners == 0
             else lax.ppermute(
                 array, "row", [(r, r ^ (k + far * owners)) for r in range(row_count)]
             )
-            for k, array in enumerate(arrays)
+            for k, array in zip(part, arrays)
         ]
 
-    keeps, pieces = {}, {}
-    for far in (1, 0):
-        keeps[far], normed = mbconv_half(
-            far, share, stride_rows, owners, place,
+    every = tuple(range(owners))
+    pair = len(every) // 2
+    parts = ((1, every[:pair]), (1, every[pair:]), (0, every))
+    keeps, pieces = [], []
+    for far, part in parts:
+        mbconv, normed = mbconv_part(
+            far, part, share * len(part) // owners, stride_rows, owners, place,
             far_halos if far else near_halos, ordered, own, weights,
         )
-        pieces[far] = exchange(normed, far)
-    backs, others = {}, pieces[0]
-    for far in (1, 0):
-        result = attend_half(place, pieces[far], others, far, per, attend_weight, output_weight)
-        others = result[owners:]
-        backs[far] = exchange(result[:owners], far)
-    keep, send = add_halves(place, (keeps[0], keeps[1]), (backs[0], backs[1]))
+        keeps.append(mbconv)
+        pieces.append(exchange(normed, far, part))
+    backs, others = [], [p for piece in pieces[1:] for p in piece]
+    for index, (far, part) in enumerate(parts):
+        result = attend_part(
+            place, pieces[index], others, index == 0, per, attend_weight,
+            output_weight,
+        )
+        if index == 0:
+            *result, keys_values = result
+            others = [keys_values]
+        backs.append(exchange(result, far, part))
+    keep, send = add_parts(place, parts, owners, keeps, backs)
     got = lax.ppermute(send, "col", swap)
     shape = (rows // stride_rows, stride_rows, cols // stride_cols, col_count, share, channels)
     out = finish(place, keep, None, True, owners, shape)

time: 101 us -> 104 us (1.030); the launches traced: 99.2 us -> 104 us
  Pallas kernels: 37 us -> 43.4 us
  waiting for transfers between devices: 25.9 us -> 23.7 us
    pallas_call x7 -> x10, Pallas kernels: 33.8 us -> 40.2 us  [call(): pl.pallas_call(kernel, in_specs=[SMEM] + [VMEM] * len(operands), out_spec...]
    ppermute x1, waiting for transfers between devices: 2.42 us -> 0.18 us  [chunked(): other = lax.ppermute(tokens, 'col', swap)]
  transfers between devices with their start and end apart: 19 -> 19, of which waited for: 12 -> 10; matrix products, arithmetic and copies ran while one was open for 0% -> 0% of each run, Pallas kernels for 21% -> 27%
where the time goes in v5:
time: 104 us
  Pallas kernels  43.4 us (42%)
  starting transfers between devices  35.3 us (34%)
  waiting for transfers between devices  23.7 us (23%)
  local copies, waits for them, and re-layouts  1.25 us (1%)
    pallas_call x10, Pallas kernels, call(): pl.pallas_call(kernel, in_specs=[SMEM] + [VMEM] * len(operands), out_spec...  40.2 us
    ppermute x14, starting transfers between devices, exchange(): lax.ppermute(array, 'row', [(r, r ^ k + far * owners) for r in range(row_...  27.3 us
    ppermute x14, waiting for transfers between devices, exchange(): lax.ppermute(array, 'row', [(r, r ^ k + far * owners) for r in range(row_...  23.1 us
    ppermute x1, starting transfers between devices, chunked(): near_halos = [lax.ppermute(to_middle, 'row', [(t, f) for f, t in outward])]  5.43 us
    pallas_call x2, Pallas kernels, finish(): pl.pallas_call(functools.partial(finish_kernel, mine=mine, owners=owners)...  3.19 us
  transfers between devices with their start and end apart: 19, of which 10 were waited for; matrix products, arithmetic and copies ran while one was open for 0% of the time, Pallas kernels for 27%

profile of v5, /device:TPU:0, one launch (start us, length us, event | category | flops | bytes accessed | tf_op | source)
XLA Modules:
  0.0 104.1 jit_solution(9870471000134394183)
XLA Ops:
  4.0 1.3 %collective-permute-start.2 = (bf16[288,512]{1,0:T(8,128)(2,1)S(1)}, bf16[288,512]{1,0:T(8,128)(2,1)S(1)}, u32[]{:S(2)}, u32[]{:S(2)}) collective-permute-start(bf16[288,512]{1,0:T(8,128)(2,1)S(1)} %get-tuple-element.31), channel_id=1, source_target_pairs={{2,0},{4,2},{6,4},{8,10},{10,12},{12,14},{3,1},{5,3},{7,5},{9,11},... | collective-permute-start | bytes 884744 | tf_op jit(solution)/shard_map/ppermute | solution.py:544
  6.0 5.4 %collective-permute-start.3 = (bf16[288,512]{1,0:T(8,128)(2,1)S(1)}, bf16[288,512]{1,0:T(8,128)(2,1)S(1)}, u32[]{:S(2)}, u32[]{:S(2)}) collective-permute-start(bf16[288,512]{1,0:T(8,128)(2,1)S(1)} %get-tuple-element.30), channel_id=1, source_target_pairs={{0,2},{2,4},{4,6},{10,8},{12,10},{14,12},{1,3},{3,5},{5,7},{11,9},... | collective-permute-start | bytes 884744 | tf_op jit(solution)/shard_map/ppermute | solution.py:547
  11.5 4.4 %shard_map.75.refs_3_.refs_2_ = bf16[8,4,288,256]{3,2,1,0:T(8,128)(2,1)S(1)} custom-call(s32[2]{0:T(128)S(1)} %pad_add_fusion.place_ref, bf16[4,288,512]{2,1,0:T(8,128)(2,1)S(1)} %get-tuple-element.32.ordered_ref.refs_2_.refs_1_, bf16[512,2048]{1,0:T(8,128)(2,1)S(1)} %copy-done), custom_call_target="tpu_custom_call" | custom-call | flops 2415919104 | bytes 1048576 | tf_op jit(solution)/shard_map/pallas_call | solution.py:127
  16.1 4.5 %shard_map.77 = (bf16[256,512]{1,0:T(8,128)(2,1)S(1)}, bf16[128,512]{1,0:T(8,128)(2,1)S(1)}, bf16[128,512]{1,0:T(8,128)(2,1)S(1)}) custom-call(s32[2]{0:T(128)S(1)} %pad_add_fusion.place_ref, bf16[288,512]{1,0:T(8,128)(2,1)S(1)} %collective-permute-done.1.refs_0_, bf16[288,512]{1,0:T(8,128)(2,1)S(1)} %collective-permute-done.2.refs_1_, ...), custom_call_target="tpu_custom_call" | custom-call | flops 1073741824 | bytes 1048576 | tf_op jit(solution)/shard_map/pallas_call | solution.py:127
  20.6 5.0 %collective-permute-start.6 = (bf16[128,512]{1,0:T(8,128)(2,1)S(1)}, bf16[128,512]{1,0:T(8,128)(2,1)S(1)}, u32[]{:S(2)}, u32[]{:S(2)}) collective-permute-start(bf16[128,512]{1,0:T(8,128)(2,1)S(1)} %get-tuple-element.38), channel_id=1, source_target_pairs={{0,12},{2,14},{4,8},{6,10},{8,4},{10,6},{12,0},{14,2},{1,13},{3,15... | collective-permute-start | bytes 393224 | tf_op jit(solution)/shard_map/ppermute | solution.py:554
  26.7 4.5 %shard_map.76 = (bf16[256,512]{1,0:T(8,128)(2,1)S(1)}, bf16[128,512]{1,0:T(8,128)(2,1)S(1)}, bf16[128,512]{1,0:T(8,128)(2,1)S(1)}) custom-call(s32[2]{0:T(128)S(1)} %pad_add_fusion.place_ref, bf16[288,512]{1,0:T(8,128)(2,1)S(1)} %collective-permute-done.1.refs_0_, bf16[288,512]{1,0:T(8,128)(2,1)S(1)} %collective-permute-done.2.refs_1_, ...), custom_call_target="tpu_custom_call" | custom-call | flops 1073741824 | bytes 1048576 | tf_op jit(solution)/shard_map/pallas_call | solution.py:127
  31.2 6.4 %collective-permute-start.4 = (bf16[128,512]{1,0:T(8,128)(2,1)S(1)}, bf16[128,512]{1,0:T(8,128)(2,1)S(1)}, u32[]{:S(2)}, u32[]{:S(2)}) collective-permute-start(bf16[128,512]{1,0:T(8,128)(2,1)S(1)} %get-tuple-element.36), channel_id=1, source_target_pairs={{0,8},{2,10},{4,12},{6,14},{8,0},{10,2},{12,4},{14,6},{1,9},{3,11}... | collective-permute-start | bytes 393224 | tf_op jit(solution)/shard_map/ppermute | solution.py:554
  37.7 7.7 %shard_map.78 = (bf16[512,512]{1,0:T(8,128)(2,1)S(1)}, bf16[128,512]{1,0:T(8,128)(2,1)S(1)}, bf16[128,512]{1,0:T(8,128)(2,1)S(1)}, bf16[128,512]{1,0:T(8,128)(2,1)S(1)}, bf16[128,512]{1,0:T(8,128)(2,1)S(1)}) custom-call(s32[2]{0:T(128)S(1)} %pad_add_fusion.place_ref, bf16[288,512]{1,0:T(8,128)(2,1)S(1)} %collective-permute-done.3.refs_0_, ...), custom_call_target="tpu_custom_call" | custom-call | flops 2147483648 | bytes 1048576 | tf_op jit(solution)/shard_map/pallas_call | solution.py:127
  45.4 1.6 %collective-permute-start.8 = (bf16[128,512]{1,0:T(8,128)(2,1)S(1)}, bf16[128,512]{1,0:T(8,128)(2,1)S(1)}, u32[]{:S(2)}, u32[]{:S(2)}) collective-permute-start(bf16[128,512]{1,0:T(8,128)(2,1)S(1)} %get-tuple-element.41), channel_id=1, source_target_pairs={{0,2},{2,0},{4,6},{6,4},{8,10},{10,8},{12,14},{14,12},{1,3},{3,1},... | collective-permute-start | bytes 393224 | tf_op jit(solution)/shard_map/ppermute | solution.py:554
  47.0 1.3 %collective-permute-start.9 = (bf16[128,512]{1,0:T(8,128)(2,1)S(1)}, bf16[128,512]{1,0:T(8,128)(2,1)S(1)}, u32[]{:S(2)}, u32[]{:S(2)}) collective-permute-start(bf16[128,512]{1,0:T(8,128)(2,1)S(1)} %get-tuple-element.42), channel_id=1, source_target_pairs={{0,4},{2,6},{4,0},{6,2},{8,12},{10,14},{12,8},{14,10},{1,5},{3,7},... | collective-permute-start | bytes 393224 | tf_op jit(solution)/shard_map/ppermute | solution.py:554
  50.0 2.1 %collective-permute-done.8.refs_5_.refs_1_ = bf16[128,512]{1,0:T(8,128)(2,1)S(1)} collective-permute-done((bf16[128,512]{1,0:T(8,128)(2,1)S(1)}, bf16[128,512]{1,0:T(8,128)(2,1)S(1)}, u32[]{:S(2)}, u32[]{:S(2)}) %collective-permute-start.8) | collective-permute-done | bytes 131104 | tf_op jit(solution)/shard_map/ppermute | solution.py:554
  53.4 2.2 %collective-permute-done.10.refs_7_.refs_3_ = bf16[128,512]{1,0:T(8,128)(2,1)S(1)} collective-permute-done((bf16[128,512]{1,0:T(8,128)(2,1)S(1)}, bf16[128,512]{1,0:T(8,128)(2,1)S(1)}, u32[]{:S(2)}, u32[]{:S(2)}) %collective-permute-start.10) | collective-permute-done | bytes 131104 | tf_op jit(solution)/shard_map/ppermute | solution.py:554
  55.6 5.8 %shard_map.79 = (bf16[128,512]{1,0:T(8,128)(2,1)S(1)}, bf16[128,512]{1,0:T(8,128)(2,1)S(1)}, bf16[4,256,1024]{2,1,0:T(8,128)(2,1)S(1)}) custom-call(s32[2]{0:T(128)S(1)} %pad_add_fusion.place_ref, bf16[128,512]{1,0:T(8,128)(2,1)S(1)} %collective-permute-done.4.refs_0_, bf16[128,512]{1,0:T(8,128)(2,1)S(1)} %collective-permute-done.5.refs_1_, ...), custom_call_target="tpu_custom_call" | custom-call | flops 671088640 | bytes 1048576 | tf_op jit(solution)/shard_map/pallas_call | solution.py:127
  61.4 5.8 %shard_map.81 = (bf16[128,512]{1,0:T(8,128)(2,1)S(1)}, bf16[128,512]{1,0:T(8,128)(2,1)S(1)}, bf16[128,512]{1,0:T(8,128)(2,1)S(1)}, bf16[128,512]{1,0:T(8,128)(2,1)S(1)}) custom-call(s32[2]{0:T(128)S(1)} %pad_add_fusion.place_ref, bf16[128,512]{1,0:T(8,128)(2,1)S(1)} %get-tuple-element.40.refs_4_.refs_0_, ...), custom_call_target="tpu_custom_call" | custom-call | flops 1342177280 | bytes 1048576 | tf_op jit(solution)/shard_map/pallas_call | solution.py:127
  67.9 2.8 %collective-permute-start.17 = (bf16[128,512]{1,0:T(8,128)(2,1)S(1)}, bf16[128,512]{1,0:T(8,128)(2,1)S(1)}, u32[]{:S(2)}, u32[]{:S(2)}) collective-permute-start(bf16[128,512]{1,0:T(8,128)(2,1)S(1)} %get-tuple-element.52), channel_id=1, source_target_pairs={{0,6},{2,4},{4,2},{6,0},{8,14},{10,12},{12,10},{14,8},{1,7},{3,5},... | collective-permute-start | bytes 393224 | tf_op jit(solution)/shard_map/ppermute | solution.py:554
  70.7 4.6 %shard_map.80 = (bf16[128,512]{1,0:T(8,128)(2,1)S(1)}, bf16[128,512]{1,0:T(8,128)(2,1)S(1)}) custom-call(s32[2]{0:T(128)S(1)} %pad_add_fusion.place_ref, bf16[128,512]{1,0:T(8,128)(2,1)S(1)} %collective-permute-done.6.refs_2_.refs_0_, bf16[128,512]{1,0:T(8,128)(2,1)S(1)} %collective-permute-done.7.refs_3_.refs_1_, ...), custom_call_target="tpu_custom_call" | custom-call | flops 671088640 | bytes 1048576 | tf_op jit(solution)/shard_map/pallas_call | solution.py:127
  75.3 2.3 %collective-permute-start.13 = (bf16[128,512]{1,0:T(8,128)(2,1)S(1)}, bf16[128,512]{1,0:T(8,128)(2,1)S(1)}, u32[]{:S(2)}, u32[]{:S(2)}) collective-permute-start(bf16[128,512]{1,0:T(8,128)(2,1)S(1)} %get-tuple-element.47), channel_id=1, source_target_pairs={{0,12},{2,14},{4,8},{6,10},{8,4},{10,6},{12,0},{14,2},{1,13},{3,15... | collective-permute-start | bytes 393224 | tf_op jit(solution)/shard_map/ppermute | solution.py:554
  77.6 1.7 %collective-permute-start.14 = (bf16[128,512]{1,0:T(8,128)(2,1)S(1)}, bf16[128,512]{1,0:T(8,128)(2,1)S(1)}, u32[]{:S(2)}, u32[]{:S(2)}) collective-permute-start(bf16[128,512]{1,0:T(8,128)(2,1)S(1)} %get-tuple-element.48), channel_id=1, source_target_pairs={{0,14},{2,12},{4,10},{6,8},{8,6},{10,4},{12,2},{14,0},{1,15},{3,13... | collective-permute-start | bytes 393224 | tf_op jit(solution)/shard_map/ppermute | solution.py:554
  79.3 3.7 %collective-permute-start.12 = (bf16[128,512]{1,0:T(8,128)(2,1)S(1)}, bf16[128,512]{1,0:T(8,128)(2,1)S(1)}, u32[]{:S(2)}, u32[]{:S(2)}) collective-permute-start(bf16[128,512]{1,0:T(8,128)(2,1)S(1)} %get-tuple-element.45), channel_id=1, source_target_pairs={{0,10},{2,8},{4,14},{6,12},{8,2},{10,0},{12,6},{14,4},{1,11},{3,9}... | collective-permute-start | bytes 393224 | tf_op jit(solution)/shard_map/ppermute | solution.py:554
  83.0 3.7 %collective-permute-done.14.refs_6_ = bf16[128,512]{1,0:T(8,128)(2,1)S(1)} collective-permute-done((bf16[128,512]{1,0:T(8,128)(2,1)S(1)}, bf16[128,512]{1,0:T(8,128)(2,1)S(1)}, u32[]{:S(2)}, u32[]{:S(2)}) %collective-permute-start.14) | collective-permute-done | bytes 131104 | tf_op jit(solution)/shard_map/ppermute | solution.py:554
  86.7 11.2 %collective-permute-done.11.refs_3_ = bf16[128,512]{1,0:T(8,128)(2,1)S(1)} collective-permute-done((bf16[128,512]{1,0:T(8,128)(2,1)S(1)}, bf16[128,512]{1,0:T(8,128)(2,1)S(1)}, u32[]{:S(2)}, u32[]{:S(2)}) %collective-permute-start.11) | collective-permute-done | bytes 131104 | tf_op jit(solution)/shard_map/ppermute | solution.py:554
  97.9 1.6 %collective-permute-done.12.refs_4_ = bf16[128,512]{1,0:T(8,128)(2,1)S(1)} collective-permute-done((bf16[128,512]{1,0:T(8,128)(2,1)S(1)}, bf16[128,512]{1,0:T(8,128)(2,1)S(1)}, u32[]{:S(2)}, u32[]{:S(2)}) %collective-permute-start.12) | collective-permute-done | bytes 131104 | tf_op jit(solution)/shard_map/ppermute | solution.py:554
  100.4 1.6 %shard_map.83.rest_0_ = bf16[2,2,8,2,16,512]{5,4,3,2,1,0:T(8,128)(2,1)} custom-call(s32[2]{0:T(128)S(1)} %pad_add_fusion.place_ref, bf16[2,256,512]{2,1,0:T(8,128)(2,1)S(1)} %get-tuple-element.54.ready_ref), custom_call_target="tpu_custom_call" | custom-call | flops 268435456 | bytes 1048576 | tf_op jit(solution)/shard_map/pallas_call | solution.py:488
  102.3 1.6 %shard_map.84 = bf16[2,2,8,2,16,512]{5,4,3,2,1,0:T(8,128)(2,1)} custom-call(s32[2]{0:T(128)S(1)} %pad_add_fusion.place_ref, bf16[2,256,512]{2,1,0:T(8,128)(2,1)S(1)} %collective-permute-done.18.ready_ref, bf16[2,2,8,2,16,512]{5,4,3,2,1,0:T(8,128)(2,1)} %shard_map.83.rest_0_), custom_call_target="tpu_custom_call", output_to_operand_aliasing={{}: (2, {})} | custom-call | flops 268435456 | bytes 1048576 | tf_op jit(solution)/shard_map/pallas_call | solution.py:488
  (41 shorter events, 10.9 us)
Async XLA Ops:
  0.0 3.0 %collective-permute-start = (bf16[4,256,512]{2,1,0:T(8,128)(2,1)}, bf16[4,256,512]{2,1,0:T(8,128)(2,1)S(1)}, u32[]{:S(2)}, u32[]{:S(2)}) collective-permute-start(bf16[4,256,512]{2,1,0:T(8,128)(2,1)} %own_ref.1), channel_id=1, source_target_pairs={{0,1},{1,0},{2,3},{3,2},{4,5},{5,4},{6,7},{7,6},{8,9},{9,8},{10,11... | collective-permute-start | bytes 3145736 | tf_op jit(solution)/shard_map/ppermute | solution.py:537
  1.8 9.7 %copy-start = (bf16[512,2048]{1,0:T(8,128)(2,1)S(1)}, bf16[512,2048]{1,0:T(8,128)(2,1)}, u32[]{:S(2)}) copy-start(bf16[512,2048]{1,0:T(8,128)(2,1)} %refs_3_.2) | copy-start | bytes 6291460
  4.0 12.1 %collective-permute-start.2 = (bf16[288,512]{1,0:T(8,128)(2,1)S(1)}, bf16[288,512]{1,0:T(8,128)(2,1)S(1)}, u32[]{:S(2)}, u32[]{:S(2)}) collective-permute-start(bf16[288,512]{1,0:T(8,128)(2,1)S(1)} %get-tuple-element.31), channel_id=1, source_target_pairs={{2,0},{4,2},{6,4},{8,10},{10,12},{12,14},{3,1},{5,3},{7,5},{9,11},... | collective-permute-start | bytes 884744 | tf_op jit(solution)/shard_map/ppermute | solution.py:544
  5.3 10.8 %collective-permute-start.1 = (bf16[288,512]{1,0:T(8,128)(2,1)S(1)}, bf16[288,512]{1,0:T(8,128)(2,1)S(1)}, u32[]{:S(2)}, u32[]{:S(2)}) collective-permute-start(bf16[288,512]{1,0:T(8,128)(2,1)S(1)} %get-tuple-element.30), channel_id=1, source_target_pairs={{6,8},{8,6},{7,9},{9,7},{22,24},{24,22},{23,25},{25,23}} | collective-permute-start | bytes 884744 | tf_op jit(solution)/shard_map/ppermute | solution.py:543
  6.0 31.7 %collective-permute-start.3 = (bf16[288,512]{1,0:T(8,128)(2,1)S(1)}, bf16[288,512]{1,0:T(8,128)(2,1)S(1)}, u32[]{:S(2)}, u32[]{:S(2)}) collective-permute-start(bf16[288,512]{1,0:T(8,128)(2,1)S(1)} %get-tuple-element.30), channel_id=1, source_target_pairs={{0,2},{2,4},{4,6},{10,8},{12,10},{14,12},{1,3},{3,5},{5,7},{11,9},... | collective-permute-start | bytes 884744 | tf_op jit(solution)/shard_map/ppermute | solution.py:547
  11.5 4.7 %copy-start.1 = (bf16[2048,512]{1,0:T(8,128)(2,1)S(1)}, bf16[2048,512]{1,0:T(8,128)(2,1)}, u32[]{:S(2)}) copy-start(bf16[2048,512]{1,0:T(8,128)(2,1)} %refs_5_.6) | copy-start | bytes 6291460
  11.5 4.6 %copy-start.5 = (f32[3,3,2048]{2,1,0:T(4,128)S(1)}, f32[3,3,2048]{2,1,0:T(4,128)}, u32[]{:S(2)}) copy-start(f32[3,3,2048]{2,1,0:T(4,128)} %refs_4_.6) | copy-start | bytes 221188
  20.6 26.4 %collective-permute-start.6 = (bf16[128,512]{1,0:T(8,128)(2,1)S(1)}, bf16[128,512]{1,0:T(8,128)(2,1)S(1)}, u32[]{:S(2)}, u32[]{:S(2)}) collective-permute-start(bf16[128,512]{1,0:T(8,128)(2,1)S(1)} %get-tuple-element.38), channel_id=1, source_target_pairs={{0,12},{2,14},{4,8},{6,10},{8,4},{10,6},{12,0},{14,2},{1,13},{3,15... | collective-permute-start | bytes 393224 | tf_op jit(solution)/shard_map/ppermute | solution.py:554
  25.7 22.7 %collective-permute-start.7 = (bf16[128,512]{1,0:T(8,128)(2,1)S(1)}, bf16[128,512]{1,0:T(8,128)(2,1)S(1)}, u32[]{:S(2)}, u32[]{:S(2)}) collective-permute-start(bf16[128,512]{1,0:T(8,128)(2,1)S(1)} %get-tuple-element.39), channel_id=1, source_target_pairs={{0,14},{2,12},{4,10},{6,8},{8,6},{10,4},{12,2},{14,0},{1,15},{3,13... | collective-permute-start | bytes 393224 | tf_op jit(solution)/shard_map/ppermute | solution.py:554
  31.2 17.7 %collective-permute-start.4 = (bf16[128,512]{1,0:T(8,128)(2,1)S(1)}, bf16[128,512]{1,0:T(8,128)(2,1)S(1)}, u32[]{:S(2)}, u32[]{:S(2)}) collective-permute-start(bf16[128,512]{1,0:T(8,128)(2,1)S(1)} %get-tuple-element.36), channel_id=1, source_target_pairs={{0,8},{2,10},{4,12},{6,14},{8,0},{10,2},{12,4},{14,6},{1,9},{3,11}... | collective-permute-start | bytes 393224 | tf_op jit(solution)/shard_map/ppermute | solution.py:554
  37.6 17.9 %copy-start.2 = (bf16[512,1536]{1,0:T(8,128)(2,1)S(1)}, bf16[512,1536]{1,0:T(8,128)(2,1)}, u32[]{:S(2)}) copy-start(bf16[512,1536]{1,0:T(8,128)(2,1)} %refs_5_.7) | copy-start | bytes 4718596
  37.6 17.9 %copy-start.3 = (bf16[512,512]{1,0:T(8,128)(2,1)S(1)}, bf16[512,512]{1,0:T(8,128)(2,1)}, u32[]{:S(2)}) copy-start(bf16[512,512]{1,0:T(8,128)(2,1)} %refs_6_.5) | copy-start | bytes 1572868
  37.6 12.4 %collective-permute-start.5 = (bf16[128,512]{1,0:T(8,128)(2,1)S(1)}, bf16[128,512]{1,0:T(8,128)(2,1)S(1)}, u32[]{:S(2)}, u32[]{:S(2)}) collective-permute-start(bf16[128,512]{1,0:T(8,128)(2,1)S(1)} %get-tuple-element.37), channel_id=1, source_target_pairs={{0,10},{2,8},{4,14},{6,12},{8,2},{10,0},{12,6},{14,4},{1,11},{3,9}... | collective-permute-start | bytes 393224 | tf_op jit(solution)/shard_map/ppermute | solution.py:554
  45.4 6.7 %collective-permute-start.8 = (bf16[128,512]{1,0:T(8,128)(2,1)S(1)}, bf16[128,512]{1,0:T(8,128)(2,1)S(1)}, u32[]{:S(2)}, u32[]{:S(2)}) collective-permute-start(bf16[128,512]{1,0:T(8,128)(2,1)S(1)} %get-tuple-element.41), channel_id=1, source_target_pairs={{0,2},{2,0},{4,6},{6,4},{8,10},{10,8},{12,14},{14,12},{1,3},{3,1},... | collective-permute-start | bytes 393224 | tf_op jit(solution)/shard_map/ppermute | solution.py:554
  47.0 6.4 %collective-permute-start.9 = (bf16[128,512]{1,0:T(8,128)(2,1)S(1)}, bf16[128,512]{1,0:T(8,128)(2,1)S(1)}, u32[]{:S(2)}, u32[]{:S(2)}) collective-permute-start(bf16[128,512]{1,0:T(8,128)(2,1)S(1)} %get-tuple-element.42), channel_id=1, source_target_pairs={{0,4},{2,6},{4,0},{6,2},{8,12},{10,14},{12,8},{14,10},{1,5},{3,7},... | collective-permute-start | bytes 393224 | tf_op jit(solution)/shard_map/ppermute | solution.py:554
  48.3 7.2 %collective-permute-start.10 = (bf16[128,512]{1,0:T(8,128)(2,1)S(1)}, bf16[128,512]{1,0:T(8,128)(2,1)S(1)}, u32[]{:S(2)}, u32[]{:S(2)}) collective-permute-start(bf16[128,512]{1,0:T(8,128)(2,1)S(1)} %get-tuple-element.43), channel_id=1, source_target_pairs={{0,6},{2,4},{4,2},{6,0},{8,14},{10,12},{12,10},{14,8},{1,7},{3,5},... | collective-permute-start | bytes 393224 | tf_op jit(solution)/shard_map/ppermute | solution.py:554
  67.1 12.2 %collective-permute-start.15 = (bf16[128,512]{1,0:T(8,128)(2,1)S(1)}, bf16[128,512]{1,0:T(8,128)(2,1)S(1)}, u32[]{:S(2)}, u32[]{:S(2)}) collective-permute-start(bf16[128,512]{1,0:T(8,128)(2,1)S(1)} %get-tuple-element.50), channel_id=1, source_target_pairs={{0,2},{2,0},{4,6},{6,4},{8,10},{10,8},{12,14},{14,12},{1,3},{3,1},... | collective-permute-start | bytes 393224 | tf_op jit(solution)/shard_map/ppermute | solution.py:554
  67.9 11.4 %collective-permute-start.16 = (bf16[128,512]{1,0:T(8,128)(2,1)S(1)}, bf16[128,512]{1,0:T(8,128)(2,1)S(1)}, u32[]{:S(2)}, u32[]{:S(2)}) collective-permute-start(bf16[128,512]{1,0:T(8,128)(2,1)S(1)} %get-tuple-element.51), channel_id=1, source_target_pairs={{0,4},{2,6},{4,0},{6,2},{8,12},{10,14},{12,8},{14,10},{1,5},{3,7},... | collective-permute-start | bytes 393224 | tf_op jit(solution)/shard_map/ppermute | solution.py:554
  67.9 15.2 %collective-permute-start.17 = (bf16[128,512]{1,0:T(8,128)(2,1)S(1)}, bf16[128,512]{1,0:T(8,128)(2,1)S(1)}, u32[]{:S(2)}, u32[]{:S(2)}) collective-permute-start(bf16[128,512]{1,0:T(8,128)(2,1)S(1)} %get-tuple-element.52), channel_id=1, source_target_pairs={{0,6},{2,4},{4,2},{6,0},{8,14},{10,12},{12,10},{14,8},{1,7},{3,5},... | collective-permute-start | bytes 393224 | tf_op jit(solution)/shard_map/ppermute | solution.py:554
  75.3 7.7 %collective-permute-start.13 = (bf16[128,512]{1,0:T(8,128)(2,1)S(1)}, bf16[128,512]{1,0:T(8,128)(2,1)S(1)}, u32[]{:S(2)}, u32[]{:S(2)}) collective-permute-start(bf16[128,512]{1,0:T(8,128)(2,1)S(1)} %get-tuple-element.47), channel_id=1, source_target_pairs={{0,12},{2,14},{4,8},{6,10},{8,4},{10,6},{12,0},{14,2},{1,13},{3,15... | collective-permute-start | bytes 393224 | tf_op jit(solution)/shard_map/ppermute | solution.py:554
  77.6 9.1 %collective-permute-start.14 = (bf16[128,512]{1,0:T(8,128)(2,1)S(1)}, bf16[128,512]{1,0:T(8,128)(2,1)S(1)}, u32[]{:S(2)}, u32[]{:S(2)}) collective-permute-start(bf16[128,512]{1,0:T(8,128)(2,1)S(1)} %get-tuple-element.48), channel_id=1, source_target_pairs={{0,14},{2,12},{4,10},{6,8},{8,6},{10,4},{12,2},{14,0},{1,15},{3,13... | collective-permute-start | bytes 393224 | tf_op jit(solution)/shard_map/ppermute | solution.py:554
  79.3 18.6 %collective-permute-start.11 = (bf16[128,512]{1,0:T(8,128)(2,1)S(1)}, bf16[128,512]{1,0:T(8,128)(2,1)S(1)}, u32[]{:S(2)}, u32[]{:S(2)}) collective-permute-start(bf16[128,512]{1,0:T(8,128)(2,1)S(1)} %get-tuple-element.44), channel_id=1, source_target_pairs={{0,8},{2,10},{4,12},{6,14},{8,0},{10,2},{12,4},{14,6},{1,9},{3,11}... | collective-permute-start | bytes 393224 | tf_op jit(solution)/shard_map/ppermute | solution.py:554
  79.3 20.2 %collective-permute-start.12 = (bf16[128,512]{1,0:T(8,128)(2,1)S(1)}, bf16[128,512]{1,0:T(8,128)(2,1)S(1)}, u32[]{:S(2)}, u32[]{:S(2)}) collective-permute-start(bf16[128,512]{1,0:T(8,128)(2,1)S(1)} %get-tuple-element.45), channel_id=1, source_target_pairs={{0,10},{2,8},{4,14},{6,12},{8,2},{10,0},{12,6},{14,4},{1,11},{3,9}... | collective-permute-start | bytes 393224 | tf_op jit(solution)/shard_map/ppermute | solution.py:554
  100.4 2.0 %collective-permute-start.18 = (bf16[2,256,512]{2,1,0:T(8,128)(2,1)S(1)}, bf16[2,256,512]{2,1,0:T(8,128)(2,1)S(1)}, u32[]{:S(2)}, u32[]{:S(2)}) collective-permute-start(bf16[2,256,512]{2,1,0:T(8,128)(2,1)S(1)} %get-tuple-element.53), channel_id=1, source_target_pairs={{0,1},{1,0},{2,3},{3,2},{4,5},{5,4},{6,7},{7,6},{8,9},{9,8},{10,11... | collective-permute-start | bytes 1572872 | tf_op jit(solution)/shard_map/ppermute | solution.py:582
  (2 other events, 5.9 us)

commit v6 on v5

--- a/solution.py
+++ b/solution.py
@@ -123,12 +123,12 @@
 MIB = 1 << 20
 
 
-def call(kernel, place, operands, shapes, flops, limit, scratch=(), **options):
+def call(kernel, place, operands, shapes, flops, limit, scratch=(), kind=jnp.bfloat16):
     return pl.pallas_call(
         kernel,
         in_specs=[SMEM] + [VMEM] * len(operands),
         out_specs=[VMEM] * len(shapes),
-        out_shape=[jax.ShapeDtypeStruct(shape, jnp.bfloat16) for shape in shapes],
+        out_shape=[jax.ShapeDtypeStruct(shape, kind) for shape in shapes],
         scratch_shapes=list(scratch),
         compiler_params=pltpu.CompilerParams(vmem_limit_bytes=limit),
         cost_estimate=pl.CostEstimate(flops=flops, bytes_accessed=1 << 20, transcendentals=0),
@@ -171,7 +171,7 @@
                 product = jnp.dot(
                     ordered_ref[row], expand_ref[:, lanes], preferred_element_type=jnp.float32
                 )
-                expanded_ref[2 * index + half, row] = gelu_twice(product).astype(jnp.bfloat16)
+                expanded_ref[2 * index + half, row] = gelu_twice(product)
         return carry
 
     lax.fori_loop(0, hidden // (2 * BLOCK), step, 0)
@@ -187,6 +187,7 @@
         [(hidden // BLOCK, rows, size, BLOCK)],
         2 * rows * size * channels * hidden,
         8 * MIB,
+        kind=jnp.float32,
     )[0]
 
 
@@ -245,8 +246,10 @@
                                     at += low
                                     tiles.append(edge_rows[half, at : at + SUBLANES, lanes])
                                 else:
-                                    tile = own_ref[block, row - 1, pl.ds(begin + at, GRID), lanes]
-                                    tiles.append(tile.astype(jnp.float32)[low : low + SUBLANES])
+                                    at = pl.multiple_of(begin + at + low, SUBLANES)
+                                    tiles.append(
+                                        own_ref[block, row - 1, pl.ds(at, SUBLANES), lanes]
+                                    )
                             source.append(tiles)
                         for b in (0, 1):
                             for rb in range(row_blocks):
@@ -339,7 +342,7 @@
     key_lane = lax.broadcasted_iota(jnp.int32, (members, LANES), 1) // HEAD_DIM
     query_lane = lax.broadcasted_iota(jnp.int32, (count * per, LANES), 1) // HEAD_DIM
 
-    def step(item, carry):
+    def attend(item):
         spot = pl.ds(pl.multiple_of(item * per, per), per)
         x = jnp.concatenate([ref[spot, :] for ref in x_refs], axis=0)
         if first:
@@ -394,9 +397,13 @@
         result = result.astype(jnp.bfloat16)
         for index, ref in enumerate(out_refs):
             ref[spot, :] = result[index * per : (index + 1) * per]
+
+    def step(index, carry):
+        for item in range(2):
+            attend(2 * index + item)
         return carry
 
-    lax.fori_loop(0, x_refs[0].shape[0] // per, step, 0)
+    lax.fori_loop(0, x_refs[0].shape[0] // per // 2, step, 0)
 
 
 def attend_part(place, pieces, others, first, per, attend_weight, output_weight):
@@ -420,7 +427,7 @@
     keep_ref, send_ref = refs[-2:]
     back_refs = list(refs[len(parts) : -2])
     is_left = place_ref[0] == 0
-    for (far, part), mbconv_ref in zip(parts, refs):
+    for part, mbconv_ref in zip(parts, refs):
         channels = mbconv_ref.shape[1]
         for k in part:
             back_ref = back_refs.pop(0)
@@ -435,8 +442,8 @@
                 left = total[:, 0].reshape(GRID, channels)
                 right = total[:, 1].reshape(GRID, channels)
                 to = pl.ds(pl.multiple_of((owner * size + at) // 2, GRID), GRID)
-                keep_ref[far, to, :] = jnp.where(is_left, left, right).astype(jnp.bfloat16)
-                send_ref[far, to, :] = jnp.where(is_left, right, left).astype(jnp.bfloat16)
+                keep_ref[to, :] = jnp.where(is_left, left, right).astype(jnp.bfloat16)
+                send_ref[to, :] = jnp.where(is_left, right, left).astype(jnp.bfloat16)
 
 
 def add_parts(place, parts, owners, mbconvs, backs):
@@ -445,54 +452,53 @@
         functools.partial(add_kernel, parts=parts, owners=owners),
         place,
         [*mbconvs, *[b for back in backs for b in back]],
-        [(HALVES, owners * size // 2, channels)] * 2,
-        2 * owners * size * channels * 64,
+        [(owners * size // 2, channels)] * 2,
+        owners * size * channels * 64,
         6 * MIB,
     )
 
 
-def finish_kernel(place_ref, ready_ref, *rest, mine, owners):
+def finish_kernel(place_ref, ready_ref, *rest, mine, far, owners):
     out_ref, placed_ref, sems = rest[-3:]
-    halves, length, _ = ready_ref.shape
+    length, _ = ready_ref.shape
     row_blocks, _, blocks, _, share, channels = out_ref.shape
     which = place_ref[0] if mine else 1 - place_ref[0]
+    hm = 1 - place_ref[1] // owners if far else place_ref[1] // owners
     at = lax.broadcasted_iota(jnp.int32, (length, length), 0)
     b = at % share
     a = (at // share) % blocks
     rb = at // (share * blocks)
     source = (b * row_blocks + rb) * blocks + a
     select = lax.broadcasted_iota(jnp.int32, (length, length), 1) == source
-    select = select.astype(jnp.bfloat16)
+    placed = jnp.dot(
+        select.astype(jnp.bfloat16), ready_ref[...], preferred_element_type=jnp.float32
+    )
+    placed = placed.astype(jnp.bfloat16).reshape(row_blocks, blocks, share, channels)
     copies = []
-    for half in range(halves):
-        hm = place_ref[1] // owners if half == 0 else 1 - place_ref[1] // owners
-        placed = jnp.dot(select, ready_ref[half], preferred_element_type=jnp.float32)
-        placed_ref[half] = placed.astype(jnp.bfloat16).reshape(row_blocks, blocks, share, channels)
-        for rb_at in range(row_blocks):
-            copies.append(
-                pltpu.make_async_copy(
-                    placed_ref.at[half, rb_at],
-                    out_ref.at[rb_at, hm, :, which],
-                    sems.at[half, rb_at],
-                )
+    for rb_at in range(row_blocks):
+        placed_ref[rb_at] = placed[rb_at]
+        copies.append(
+            pltpu.make_async_copy(
+                placed_ref.at[rb_at], out_ref.at[rb_at, hm, :, which], sems.at[rb_at]
             )
-            copies[-1].start()
+        )
+        copies[-1].start()
     for copy in copies:
         copy.wait()
 
 
-def finish(place, ready, previous, mine, owners, shape):
+def finish(place, ready, previous, mine, far, owners, shape):
     anywhere = pl.BlockSpec(memory_space=pl.ANY)
-    row_blocks, stride_rows, blocks, _, share, channels = shape
+    row_blocks, _, blocks, _, share, channels = shape
     previous = [] if previous is None else [previous]
     return pl.pallas_call(
-        functools.partial(finish_kernel, mine=mine, owners=owners),
+        functools.partial(finish_kernel, mine=mine, far=far, owners=owners),
         in_specs=[SMEM, VMEM] + [anywhere] * len(previous),
         out_specs=anywhere,
         out_shape=jax.ShapeDtypeStruct(shape, jnp.bfloat16),
         scratch_shapes=[
-            pltpu.VMEM((stride_rows, row_blocks, blocks, share, channels), jnp.bfloat16),
-            pltpu.SemaphoreType.DMA((stride_rows, row_blocks)),
+            pltpu.VMEM((row_blocks, blocks, share, channels), jnp.bfloat16),
+            pltpu.SemaphoreType.DMA((row_blocks,)),
         ],
         input_output_aliases={2: 0} if previous else {},
         compiler_params=pltpu.CompilerParams(vmem_limit_bytes=6 * MIB),
@@ -578,11 +584,17 @@
             *result, keys_values = result
             others = [keys_values]
         backs.append(exchange(result, far, part))
-    keep, send = add_parts(place, parts, owners, keeps, backs)
-    got = lax.ppermute(send, "col", swap)
     shape = (rows // stride_rows, stride_rows, cols // stride_cols, col_count, share, channels)
-    out = finish(place, keep, None, True, owners, shape)
-    out = finish(place, got, out, False, owners, shape)
+    out = None
+    for far in (1, 0):
+        chosen = [i for i, (is_far, _) in enumerate(parts) if is_far == far]
+        keep, send = add_parts(
+            place, [parts[i][1] for i in chosen], owners,
+            [keeps[i] for i in chosen], [backs[i] for i in chosen],
+        )
+        got = lax.ppermute(send, "col", swap)
+        out = finish(place, keep, out, True, far, owners, shape)
+        out = finish(place, got, out, False, far, owners, shape)
     return out.reshape(rows, cols, channels)
 
 

time: 104 us -> 100 us (0.962)
  waiting for transfers between devices: 23.7 us -> 14.1 us
  starting transfers between devices: 35.3 us -> 38.9 us
  Pallas kernels: 43.4 us -> 45.1 us
    ppermute x14, waiting for transfers between devices: 23.1 us -> 13.6 us  [exchange(): lax.ppermute(array, 'row', [(r, r ^ k + far * owners) for r in range(row_...]
    ppermute x14, starting transfers between devices: 27.3 us -> 30.8 us  [exchange(): lax.ppermute(array, 'row', [(r, r ^ k + far * owners) for r in range(row_...]
    pallas_call x2 -> x4, Pallas kernels: 3.19 us -> 5.8 us  [finish(): pl.pallas_call(functools.partial(finish_kernel, mine=mine, far=far, owner...]
    pallas_call x10 -> x11, Pallas kernels: 40.2 us -> 39.3 us  [call(): pl.pallas_call(kernel, in_specs=[SMEM] + [VMEM] * len(operands), out_spec...]
  transfers between devices with their start and end apart: 19 -> 20, of which waited for: 10 -> 10; matrix products, arithmetic and copies ran while one was open for 0% -> 0% of each run, Pallas kernels for 27% -> 33%
where the time goes in v6:
time: 100 us; the launch traced here: 99.9 us
  Pallas kernels  45.1 us (45%)
  starting transfers between devices  38.9 us (39%)
  waiting for transfers between devices  14.1 us (14%)
  local copies, waits for them, and re-layouts  1.25 us (1%)
    pallas_call x11, Pallas kernels, call(): pl.pallas_call(kernel, in_specs=[SMEM] + [VMEM] * len(operands), out_spec...  39.3 us
    ppermute x14, starting transfers between devices, exchange(): lax.ppermute(array, 'row', [(r, r ^ k + far * owners) for r in range(row_...  30.8 us
    ppermute x14, waiting for transfers between devices, exchange(): lax.ppermute(array, 'row', [(r, r ^ k + far * owners) for r in range(row_...  13.6 us
    pallas_call x4, Pallas kernels, finish(): pl.pallas_call(functools.partial(finish_kernel, mine=mine, far=far, owner...  5.8 us
    ppermute x1, starting transfers between devices, chunked(): near_halos = [lax.ppermute(to_middle, 'row', [(t, f) for f, t in outward])]  5.43 us
  transfers between devices with their start and end apart: 20, of which 10 were waited for; matrix products, arithmetic and copies ran while one was open for 0% of the time, Pallas kernels for 33%

profile of v6, /device:TPU:0, one launch (start us, length us, event | category | flops | bytes accessed | tf_op | source)
XLA Modules:
  0.0 99.9 jit_solution(3923695682176579763)
XLA Ops:
  6.0 5.4 %collective-permute-start.1 = (bf16[288,512]{1,0:T(8,128)(2,1)S(1)}, bf16[288,512]{1,0:T(8,128)(2,1)S(1)}, u32[]{:S(2)}, u32[]{:S(2)}) collective-permute-start(bf16[288,512]{1,0:T(8,128)(2,1)S(1)} %get-tuple-element.32), channel_id=1, source_target_pairs={{0,2},{2,4},{4,6},{10,8},{12,10},{14,12},{1,3},{3,5},{5,7},{11,9},... | collective-permute-start | bytes 884744 | tf_op jit(solution)/shard_map/ppermute | solution.py:553
  11.5 4.3 %shard_map.75.refs_2_.refs_3_ = f32[8,4,288,256]{3,2,1,0:T(8,128)S(1)} custom-call(s32[2]{0:T(128)S(1)} %pad_add_fusion.place_ref, bf16[4,288,512]{2,1,0:T(8,128)(2,1)S(1)} %get-tuple-element.33.ordered_ref.refs_1_.refs_2_, bf16[512,2048]{1,0:T(8,128)(2,1)S(1)} %copy-done), custom_call_target="tpu_custom_call" | custom-call | flops 2415919104 | bytes 1048576 | tf_op jit(solution)/shard_map/pallas_call | solution.py:127
  16.1 4.4 %shard_map.78 = (bf16[256,512]{1,0:T(8,128)(2,1)S(1)}, bf16[128,512]{1,0:T(8,128)(2,1)S(1)}, bf16[128,512]{1,0:T(8,128)(2,1)S(1)}) custom-call(s32[2]{0:T(128)S(1)} %pad_add_fusion.place_ref, bf16[288,512]{1,0:T(8,128)(2,1)S(1)} %collective-permute-done.5.refs_0_, bf16[288,512]{1,0:T(8,128)(2,1)S(1)} %collective-permute-done.6.refs_1_, ...), custom_call_target="tpu_custom_call" | custom-call | flops 1073741824 | bytes 1048576 | tf_op jit(solution)/shard_map/pallas_call | solution.py:127
  20.5 4.9 %collective-permute-start.9 = (bf16[128,512]{1,0:T(8,128)(2,1)S(1)}, bf16[128,512]{1,0:T(8,128)(2,1)S(1)}, u32[]{:S(2)}, u32[]{:S(2)}) collective-permute-start(bf16[128,512]{1,0:T(8,128)(2,1)S(1)} %get-tuple-element.42), channel_id=1, source_target_pairs={{0,12},{2,14},{4,8},{6,10},{8,4},{10,6},{12,0},{14,2},{1,13},{3,15... | collective-permute-start | bytes 393224 | tf_op jit(solution)/shard_map/ppermute | solution.py:560
  26.6 4.4 %shard_map.77 = (bf16[256,512]{1,0:T(8,128)(2,1)S(1)}, bf16[128,512]{1,0:T(8,128)(2,1)S(1)}, bf16[128,512]{1,0:T(8,128)(2,1)S(1)}) custom-call(s32[2]{0:T(128)S(1)} %pad_add_fusion.place_ref, bf16[288,512]{1,0:T(8,128)(2,1)S(1)} %collective-permute-done.5.refs_0_, bf16[288,512]{1,0:T(8,128)(2,1)S(1)} %collective-permute-done.6.refs_1_, ...), custom_call_target="tpu_custom_call" | custom-call | flops 1073741824 | bytes 1048576 | tf_op jit(solution)/shard_map/pallas_call | solution.py:127
  31.0 6.2 %collective-permute-start.7 = (bf16[128,512]{1,0:T(8,128)(2,1)S(1)}, bf16[128,512]{1,0:T(8,128)(2,1)S(1)}, u32[]{:S(2)}, u32[]{:S(2)}) collective-permute-start(bf16[128,512]{1,0:T(8,128)(2,1)S(1)} %get-tuple-element.40), channel_id=1, source_target_pairs={{0,8},{2,10},{4,12},{6,14},{8,0},{10,2},{12,4},{14,6},{1,9},{3,11}... | collective-permute-start | bytes 393224 | tf_op jit(solution)/shard_map/ppermute | solution.py:560
  37.2 7.4 %shard_map.76 = (bf16[512,512]{1,0:T(8,128)(2,1)S(1)}, bf16[128,512]{1,0:T(8,128)(2,1)S(1)}, bf16[128,512]{1,0:T(8,128)(2,1)S(1)}, bf16[128,512]{1,0:T(8,128)(2,1)S(1)}, bf16[128,512]{1,0:T(8,128)(2,1)S(1)}) custom-call(s32[2]{0:T(128)S(1)} %pad_add_fusion.place_ref, bf16[288,512]{1,0:T(8,128)(2,1)S(1)} %collective-permute-done.1.refs_0_, ...), custom_call_target="tpu_custom_call" | custom-call | flops 2147483648 | bytes 1048576 | tf_op jit(solution)/shard_map/pallas_call | solution.py:127
  44.6 1.6 %collective-permute-start.2 = (bf16[128,512]{1,0:T(8,128)(2,1)S(1)}, bf16[128,512]{1,0:T(8,128)(2,1)S(1)}, u32[]{:S(2)}, u32[]{:S(2)}) collective-permute-start(bf16[128,512]{1,0:T(8,128)(2,1)S(1)} %get-tuple-element.36), channel_id=1, source_target_pairs={{0,2},{2,0},{4,6},{6,4},{8,10},{10,8},{12,14},{14,12},{1,3},{3,1},... | collective-permute-start | bytes 393224 | tf_op jit(solution)/shard_map/ppermute | solution.py:560
  48.2 1.5 %collective-permute-done.8.refs_1_ = bf16[128,512]{1,0:T(8,128)(2,1)S(1)} collective-permute-done((bf16[128,512]{1,0:T(8,128)(2,1)S(1)}, bf16[128,512]{1,0:T(8,128)(2,1)S(1)}, u32[]{:S(2)}, u32[]{:S(2)}) %collective-permute-start.8) | collective-permute-done | bytes 131104 | tf_op jit(solution)/shard_map/ppermute | solution.py:560
  49.7 1.6 %collective-permute-done.2.refs_5_.refs_1_ = bf16[128,512]{1,0:T(8,128)(2,1)S(1)} collective-permute-done((bf16[128,512]{1,0:T(8,128)(2,1)S(1)}, bf16[128,512]{1,0:T(8,128)(2,1)S(1)}, u32[]{:S(2)}, u32[]{:S(2)}) %collective-permute-start.2) | collective-permute-done | bytes 131104 | tf_op jit(solution)/shard_map/ppermute | solution.py:560
  52.6 2.6 %collective-permute-done.4.refs_7_.refs_3_ = bf16[128,512]{1,0:T(8,128)(2,1)S(1)} collective-permute-done((bf16[128,512]{1,0:T(8,128)(2,1)S(1)}, bf16[128,512]{1,0:T(8,128)(2,1)S(1)}, u32[]{:S(2)}, u32[]{:S(2)}) %collective-permute-start.4) | collective-permute-done | bytes 131104 | tf_op jit(solution)/shard_map/ppermute | solution.py:560
  55.2 5.6 %shard_map.79 = (bf16[128,512]{1,0:T(8,128)(2,1)S(1)}, bf16[128,512]{1,0:T(8,128)(2,1)S(1)}, bf16[4,256,1024]{2,1,0:T(8,128)(2,1)S(1)}) custom-call(s32[2]{0:T(128)S(1)} %pad_add_fusion.place_ref, bf16[128,512]{1,0:T(8,128)(2,1)S(1)} %collective-permute-done.7.refs_0_, bf16[128,512]{1,0:T(8,128)(2,1)S(1)} %collective-permute-done.8.refs_1_, ...), custom_call_target="tpu_custom_call" | custom-call | flops 671088640 | bytes 1048576 | tf_op jit(solution)/shard_map/pallas_call | solution.py:127
  60.7 4.4 %shard_map.82 = (bf16[128,512]{1,0:T(8,128)(2,1)S(1)}, bf16[128,512]{1,0:T(8,128)(2,1)S(1)}) custom-call(s32[2]{0:T(128)S(1)} %pad_add_fusion.place_ref, bf16[128,512]{1,0:T(8,128)(2,1)S(1)} %collective-permute-done.9.refs_2_.refs_0_, bf16[128,512]{1,0:T(8,128)(2,1)S(1)} %collective-permute-done.10.refs_3_.refs_1_, ...), custom_call_target="tpu_custom_call" | custom-call | flops 671088640 | bytes 1048576 | tf_op jit(solution)/shard_map/pallas_call | solution.py:127
  65.1 2.3 %collective-permute-start.17 = (bf16[128,512]{1,0:T(8,128)(2,1)S(1)}, bf16[128,512]{1,0:T(8,128)(2,1)S(1)}, u32[]{:S(2)}, u32[]{:S(2)}) collective-permute-start(bf16[128,512]{1,0:T(8,128)(2,1)S(1)} %get-tuple-element.55), channel_id=1, source_target_pairs={{0,12},{2,14},{4,8},{6,10},{8,4},{10,6},{12,0},{14,2},{1,13},{3,15... | collective-permute-start | bytes 393224 | tf_op jit(solution)/shard_map/ppermute | solution.py:560
  67.4 1.6 %collective-permute-start.18 = (bf16[128,512]{1,0:T(8,128)(2,1)S(1)}, bf16[128,512]{1,0:T(8,128)(2,1)S(1)}, u32[]{:S(2)}, u32[]{:S(2)}) collective-permute-start(bf16[128,512]{1,0:T(8,128)(2,1)S(1)} %get-tuple-element.56), channel_id=1, source_target_pairs={{0,14},{2,12},{4,10},{6,8},{8,6},{10,4},{12,2},{14,0},{1,15},{3,13... | collective-permute-start | bytes 393224 | tf_op jit(solution)/shard_map/ppermute | solution.py:560
  69.1 3.8 %collective-permute-start.16 = (bf16[128,512]{1,0:T(8,128)(2,1)S(1)}, bf16[128,512]{1,0:T(8,128)(2,1)S(1)}, u32[]{:S(2)}, u32[]{:S(2)}) collective-permute-start(bf16[128,512]{1,0:T(8,128)(2,1)S(1)} %get-tuple-element.54), channel_id=1, source_target_pairs={{0,10},{2,8},{4,14},{6,12},{8,2},{10,0},{12,6},{14,4},{1,11},{3,9}... | collective-permute-start | bytes 393224 | tf_op jit(solution)/shard_map/ppermute | solution.py:560
  72.8 5.5 %shard_map.80 = (bf16[128,512]{1,0:T(8,128)(2,1)S(1)}, bf16[128,512]{1,0:T(8,128)(2,1)S(1)}, bf16[128,512]{1,0:T(8,128)(2,1)S(1)}, bf16[128,512]{1,0:T(8,128)(2,1)S(1)}) custom-call(s32[2]{0:T(128)S(1)} %pad_add_fusion.place_ref, bf16[128,512]{1,0:T(8,128)(2,1)S(1)} %get-tuple-element.35.refs_4_.refs_0_, ...), custom_call_target="tpu_custom_call" | custom-call | flops 1342177280 | bytes 1048576 | tf_op jit(solution)/shard_map/pallas_call | solution.py:127
  79.0 2.9 %collective-permute-start.12 = (bf16[128,512]{1,0:T(8,128)(2,1)S(1)}, bf16[128,512]{1,0:T(8,128)(2,1)S(1)}, u32[]{:S(2)}, u32[]{:S(2)}) collective-permute-start(bf16[128,512]{1,0:T(8,128)(2,1)S(1)} %get-tuple-element.47), channel_id=1, source_target_pairs={{0,4},{2,6},{4,0},{6,2},{8,12},{10,14},{12,8},{14,10},{1,5},{3,7},... | collective-permute-start | bytes 393224 | tf_op jit(solution)/shard_map/ppermute | solution.py:560
  81.9 3.7 %collective-permute-start.13 = (bf16[128,512]{1,0:T(8,128)(2,1)S(1)}, bf16[128,512]{1,0:T(8,128)(2,1)S(1)}, u32[]{:S(2)}, u32[]{:S(2)}) collective-permute-start(bf16[128,512]{1,0:T(8,128)(2,1)S(1)} %get-tuple-element.48), channel_id=1, source_target_pairs={{0,6},{2,4},{4,2},{6,0},{8,14},{10,12},{12,10},{14,8},{1,7},{3,5},... | collective-permute-start | bytes 393224 | tf_op jit(solution)/shard_map/ppermute | solution.py:560
  87.1 2.2 %collective-permute-done.16.refs_3_ = bf16[128,512]{1,0:T(8,128)(2,1)S(1)} collective-permute-done((bf16[128,512]{1,0:T(8,128)(2,1)S(1)}, bf16[128,512]{1,0:T(8,128)(2,1)S(1)}, u32[]{:S(2)}, u32[]{:S(2)}) %collective-permute-start.16) | collective-permute-done | bytes 131104 | tf_op jit(solution)/shard_map/ppermute | solution.py:560
  90.8 2.2 %collective-permute-done.13.refs_4_ = bf16[128,512]{1,0:T(8,128)(2,1)S(1)} collective-permute-done((bf16[128,512]{1,0:T(8,128)(2,1)S(1)}, bf16[128,512]{1,0:T(8,128)(2,1)S(1)}, u32[]{:S(2)}, u32[]{:S(2)}) %collective-permute-start.13) | collective-permute-done | bytes 131104 | tf_op jit(solution)/shard_map/ppermute | solution.py:560
  95.3 1.5 %shard_map.85.rest_0_ = bf16[2,2,8,2,16,512]{5,4,3,2,1,0:T(8,128)(2,1)} custom-call(s32[2]{0:T(128)S(1)} %pad_add_fusion.place_ref, bf16[256,512]{1,0:T(8,128)(2,1)S(1)} %collective-permute-done.19.ready_ref, bf16[2,2,8,2,16,512]{5,4,3,2,1,0:T(8,128)(2,1)} %shard_map.84.rest_0_), custom_call_target="tpu_custom_call", output_to_operand_aliasing={{}: (2, {})} | custom-call | flops 134217728 | bytes 1048576 | tf_op jit(solution)/shard_map/pallas_call | solution.py:494
  96.8 1.5 %shard_map.86.rest_0_ = bf16[2,2,8,2,16,512]{5,4,3,2,1,0:T(8,128)(2,1)} custom-call(s32[2]{0:T(128)S(1)} %pad_add_fusion.place_ref, bf16[256,512]{1,0:T(8,128)(2,1)S(1)} %get-tuple-element.50.ready_ref, bf16[2,2,8,2,16,512]{5,4,3,2,1,0:T(8,128)(2,1)} %shard_map.85.rest_0_), custom_call_target="tpu_custom_call", output_to_operand_aliasing={{}: (2, {})} | custom-call | flops 134217728 | bytes 1048576 | tf_op jit(solution)/shard_map/pallas_call | solution.py:494
  98.2 1.5 %shard_map.87 = bf16[2,2,8,2,16,512]{5,4,3,2,1,0:T(8,128)(2,1)} custom-call(s32[2]{0:T(128)S(1)} %pad_add_fusion.place_ref, bf16[256,512]{1,0:T(8,128)(2,1)S(1)} %collective-permute-done.14.ready_ref, bf16[2,2,8,2,16,512]{5,4,3,2,1,0:T(8,128)(2,1)} %shard_map.86.rest_0_), custom_call_target="tpu_custom_call", output_to_operand_aliasing={{}: (2, {})} | custom-call | flops 134217728 | bytes 1048576 | tf_op jit(solution)/shard_map/pallas_call | solution.py:494
  (46 shorter events, 16.6 us)
Async XLA Ops:
  0.0 3.0 %collective-permute-start = (bf16[4,256,512]{2,1,0:T(8,128)(2,1)}, bf16[4,256,512]{2,1,0:T(8,128)(2,1)S(1)}, u32[]{:S(2)}, u32[]{:S(2)}) collective-permute-start(bf16[4,256,512]{2,1,0:T(8,128)(2,1)} %own_ref.1), channel_id=1, source_target_pairs={{0,1},{1,0},{2,3},{3,2},{4,5},{5,4},{6,7},{7,6},{8,9},{9,8},{10,11... | collective-permute-start | bytes 3145736 | tf_op jit(solution)/shard_map/ppermute | solution.py:543
  1.8 9.7 %copy-start = (bf16[512,2048]{1,0:T(8,128)(2,1)S(1)}, bf16[512,2048]{1,0:T(8,128)(2,1)}, u32[]{:S(2)}) copy-start(bf16[512,2048]{1,0:T(8,128)(2,1)} %refs_4_.6) | copy-start | bytes 6291460
  4.0 12.1 %collective-permute-start.6 = (bf16[288,512]{1,0:T(8,128)(2,1)S(1)}, bf16[288,512]{1,0:T(8,128)(2,1)S(1)}, u32[]{:S(2)}, u32[]{:S(2)}) collective-permute-start(bf16[288,512]{1,0:T(8,128)(2,1)S(1)} %get-tuple-element.39), channel_id=1, source_target_pairs={{2,0},{4,2},{6,4},{8,10},{10,12},{12,14},{3,1},{5,3},{7,5},{9,11},... | collective-permute-start | bytes 884744 | tf_op jit(solution)/shard_map/ppermute | solution.py:550
  5.3 10.8 %collective-permute-start.5 = (bf16[288,512]{1,0:T(8,128)(2,1)S(1)}, bf16[288,512]{1,0:T(8,128)(2,1)S(1)}, u32[]{:S(2)}, u32[]{:S(2)}) collective-permute-start(bf16[288,512]{1,0:T(8,128)(2,1)S(1)} %get-tuple-element.32), channel_id=1, source_target_pairs={{6,8},{8,6},{7,9},{9,7},{22,24},{24,22},{23,25},{25,23}} | collective-permute-start | bytes 884744 | tf_op jit(solution)/shard_map/ppermute | solution.py:549
  6.0 31.2 %collective-permute-start.1 = (bf16[288,512]{1,0:T(8,128)(2,1)S(1)}, bf16[288,512]{1,0:T(8,128)(2,1)S(1)}, u32[]{:S(2)}, u32[]{:S(2)}) collective-permute-start(bf16[288,512]{1,0:T(8,128)(2,1)S(1)} %get-tuple-element.32), channel_id=1, source_target_pairs={{0,2},{2,4},{4,6},{10,8},{12,10},{14,12},{1,3},{3,5},{5,7},{11,9},... | collective-permute-start | bytes 884744 | tf_op jit(solution)/shard_map/ppermute | solution.py:553
  11.5 4.7 %copy-start.1 = (bf16[2048,512]{1,0:T(8,128)(2,1)S(1)}, bf16[2048,512]{1,0:T(8,128)(2,1)}, u32[]{:S(2)}) copy-start(bf16[2048,512]{1,0:T(8,128)(2,1)} %refs_6_.4) | copy-start | bytes 6291460
  20.5 25.7 %collective-permute-start.9 = (bf16[128,512]{1,0:T(8,128)(2,1)S(1)}, bf16[128,512]{1,0:T(8,128)(2,1)S(1)}, u32[]{:S(2)}, u32[]{:S(2)}) collective-permute-start(bf16[128,512]{1,0:T(8,128)(2,1)S(1)} %get-tuple-element.42), channel_id=1, source_target_pairs={{0,12},{2,14},{4,8},{6,10},{8,4},{10,6},{12,0},{14,2},{1,13},{3,15... | collective-permute-start | bytes 393224 | tf_op jit(solution)/shard_map/ppermute | solution.py:560
  25.4 22.2 %collective-permute-start.10 = (bf16[128,512]{1,0:T(8,128)(2,1)S(1)}, bf16[128,512]{1,0:T(8,128)(2,1)S(1)}, u32[]{:S(2)}, u32[]{:S(2)}) collective-permute-start(bf16[128,512]{1,0:T(8,128)(2,1)S(1)} %get-tuple-element.43), channel_id=1, source_target_pairs={{0,14},{2,12},{4,10},{6,8},{8,6},{10,4},{12,2},{14,0},{1,15},{3,13... | collective-permute-start | bytes 393224 | tf_op jit(solution)/shard_map/ppermute | solution.py:560
  31.0 17.2 %collective-permute-start.7 = (bf16[128,512]{1,0:T(8,128)(2,1)S(1)}, bf16[128,512]{1,0:T(8,128)(2,1)S(1)}, u32[]{:S(2)}, u32[]{:S(2)}) collective-permute-start(bf16[128,512]{1,0:T(8,128)(2,1)S(1)} %get-tuple-element.40), channel_id=1, source_target_pairs={{0,8},{2,10},{4,12},{6,14},{8,0},{10,2},{12,4},{14,6},{1,9},{3,11}... | collective-permute-start | bytes 393224 | tf_op jit(solution)/shard_map/ppermute | solution.py:560
  37.2 18.0 %copy-start.2 = (bf16[512,1536]{1,0:T(8,128)(2,1)S(1)}, bf16[512,1536]{1,0:T(8,128)(2,1)}, u32[]{:S(2)}) copy-start(bf16[512,1536]{1,0:T(8,128)(2,1)} %refs_3_.3) | copy-start | bytes 4718596
  37.2 18.0 %copy-start.3 = (bf16[512,512]{1,0:T(8,128)(2,1)S(1)}, bf16[512,512]{1,0:T(8,128)(2,1)}, u32[]{:S(2)}) copy-start(bf16[512,512]{1,0:T(8,128)(2,1)} %refs_4_.7) | copy-start | bytes 1572868
  37.2 12.5 %collective-permute-start.8 = (bf16[128,512]{1,0:T(8,128)(2,1)S(1)}, bf16[128,512]{1,0:T(8,128)(2,1)S(1)}, u32[]{:S(2)}, u32[]{:S(2)}) collective-permute-start(bf16[128,512]{1,0:T(8,128)(2,1)S(1)} %get-tuple-element.41), channel_id=1, source_target_pairs={{0,10},{2,8},{4,14},{6,12},{8,2},{10,0},{12,6},{14,4},{1,11},{3,9}... | collective-permute-start | bytes 393224 | tf_op jit(solution)/shard_map/ppermute | solution.py:560
  44.6 6.7 %collective-permute-start.2 = (bf16[128,512]{1,0:T(8,128)(2,1)S(1)}, bf16[128,512]{1,0:T(8,128)(2,1)S(1)}, u32[]{:S(2)}, u32[]{:S(2)}) collective-permute-start(bf16[128,512]{1,0:T(8,128)(2,1)S(1)} %get-tuple-element.36), channel_id=1, source_target_pairs={{0,2},{2,0},{4,6},{6,4},{8,10},{10,8},{12,14},{14,12},{1,3},{3,1},... | collective-permute-start | bytes 393224 | tf_op jit(solution)/shard_map/ppermute | solution.py:560
  46.2 6.4 %collective-permute-start.3 = (bf16[128,512]{1,0:T(8,128)(2,1)S(1)}, bf16[128,512]{1,0:T(8,128)(2,1)S(1)}, u32[]{:S(2)}, u32[]{:S(2)}) collective-permute-start(bf16[128,512]{1,0:T(8,128)(2,1)S(1)} %get-tuple-element.37), channel_id=1, source_target_pairs={{0,4},{2,6},{4,0},{6,2},{8,12},{10,14},{12,8},{14,10},{1,5},{3,7},... | collective-permute-start | bytes 393224 | tf_op jit(solution)/shard_map/ppermute | solution.py:560
  47.6 7.5 %collective-permute-start.4 = (bf16[128,512]{1,0:T(8,128)(2,1)S(1)}, bf16[128,512]{1,0:T(8,128)(2,1)S(1)}, u32[]{:S(2)}, u32[]{:S(2)}) collective-permute-start(bf16[128,512]{1,0:T(8,128)(2,1)S(1)} %get-tuple-element.38), channel_id=1, source_target_pairs={{0,6},{2,4},{4,2},{6,0},{8,14},{10,12},{12,10},{14,8},{1,7},{3,5},... | collective-permute-start | bytes 393224 | tf_op jit(solution)/shard_map/ppermute | solution.py:560
  65.1 13.9 %collective-permute-start.17 = (bf16[128,512]{1,0:T(8,128)(2,1)S(1)}, bf16[128,512]{1,0:T(8,128)(2,1)S(1)}, u32[]{:S(2)}, u32[]{:S(2)}) collective-permute-start(bf16[128,512]{1,0:T(8,128)(2,1)S(1)} %get-tuple-element.55), channel_id=1, source_target_pairs={{0,12},{2,14},{4,8},{6,10},{8,4},{10,6},{12,0},{14,2},{1,13},{3,15... | collective-permute-start | bytes 393224 | tf_op jit(solution)/shard_map/ppermute | solution.py:560
  67.4 14.5 %collective-permute-start.18 = (bf16[128,512]{1,0:T(8,128)(2,1)S(1)}, bf16[128,512]{1,0:T(8,128)(2,1)S(1)}, u32[]{:S(2)}, u32[]{:S(2)}) collective-permute-start(bf16[128,512]{1,0:T(8,128)(2,1)S(1)} %get-tuple-element.56), channel_id=1, source_target_pairs={{0,14},{2,12},{4,10},{6,8},{8,6},{10,4},{12,2},{14,0},{1,15},{3,13... | collective-permute-start | bytes 393224 | tf_op jit(solution)/shard_map/ppermute | solution.py:560
  69.1 18.0 %collective-permute-start.15 = (bf16[128,512]{1,0:T(8,128)(2,1)S(1)}, bf16[128,512]{1,0:T(8,128)(2,1)S(1)}, u32[]{:S(2)}, u32[]{:S(2)}) collective-permute-start(bf16[128,512]{1,0:T(8,128)(2,1)S(1)} %get-tuple-element.53), channel_id=1, source_target_pairs={{0,8},{2,10},{4,12},{6,14},{8,0},{10,2},{12,4},{14,6},{1,9},{3,11}... | collective-permute-start | bytes 393224 | tf_op jit(solution)/shard_map/ppermute | solution.py:560
  69.1 20.2 %collective-permute-start.16 = (bf16[128,512]{1,0:T(8,128)(2,1)S(1)}, bf16[128,512]{1,0:T(8,128)(2,1)S(1)}, u32[]{:S(2)}, u32[]{:S(2)}) collective-permute-start(bf16[128,512]{1,0:T(8,128)(2,1)S(1)} %get-tuple-element.54), channel_id=1, source_target_pairs={{0,10},{2,8},{4,14},{6,12},{8,2},{10,0},{12,6},{14,4},{1,11},{3,9}... | collective-permute-start | bytes 393224 | tf_op jit(solution)/shard_map/ppermute | solution.py:560
  78.3 11.8 %collective-permute-start.11 = (bf16[128,512]{1,0:T(8,128)(2,1)S(1)}, bf16[128,512]{1,0:T(8,128)(2,1)S(1)}, u32[]{:S(2)}, u32[]{:S(2)}) collective-permute-start(bf16[128,512]{1,0:T(8,128)(2,1)S(1)} %get-tuple-element.46), channel_id=1, source_target_pairs={{0,2},{2,0},{4,6},{6,4},{8,10},{10,8},{12,14},{14,12},{1,3},{3,1},... | collective-permute-start | bytes 393224 | tf_op jit(solution)/shard_map/ppermute | solution.py:560
  79.0 11.8 %collective-permute-start.12 = (bf16[128,512]{1,0:T(8,128)(2,1)S(1)}, bf16[128,512]{1,0:T(8,128)(2,1)S(1)}, u32[]{:S(2)}, u32[]{:S(2)}) collective-permute-start(bf16[128,512]{1,0:T(8,128)(2,1)S(1)} %get-tuple-element.47), channel_id=1, source_target_pairs={{0,4},{2,6},{4,0},{6,2},{8,12},{10,14},{12,8},{14,10},{1,5},{3,7},... | collective-permute-start | bytes 393224 | tf_op jit(solution)/shard_map/ppermute | solution.py:560
  81.9 11.1 %collective-permute-start.13 = (bf16[128,512]{1,0:T(8,128)(2,1)S(1)}, bf16[128,512]{1,0:T(8,128)(2,1)S(1)}, u32[]{:S(2)}, u32[]{:S(2)}) collective-permute-start(bf16[128,512]{1,0:T(8,128)(2,1)S(1)} %get-tuple-element.48), channel_id=1, source_target_pairs={{0,6},{2,4},{4,2},{6,0},{8,14},{10,12},{12,10},{14,8},{1,7},{3,5},... | collective-permute-start | bytes 393224 | tf_op jit(solution)/shard_map/ppermute | solution.py:560
  90.0 5.3 %collective-permute-start.19 = (bf16[256,512]{1,0:T(8,128)(2,1)S(1)}, bf16[256,512]{1,0:T(8,128)(2,1)S(1)}, u32[]{:S(2)}, u32[]{:S(2)}) collective-permute-start(bf16[256,512]{1,0:T(8,128)(2,1)S(1)} %get-tuple-element.57), channel_id=1, source_target_pairs={{0,1},{1,0},{2,3},{3,2},{4,5},{5,4},{6,7},{7,6},{8,9},{9,8},{10,11... | collective-permute-start | bytes 786440 | tf_op jit(solution)/shard_map/ppermute | solution.py:595
  93.8 4.5 %collective-permute-start.14 = (bf16[256,512]{1,0:T(8,128)(2,1)S(1)}, bf16[256,512]{1,0:T(8,128)(2,1)S(1)}, u32[]{:S(2)}, u32[]{:S(2)}) collective-permute-start(bf16[256,512]{1,0:T(8,128)(2,1)S(1)} %get-tuple-element.49), channel_id=1, source_target_pairs={{0,1},{1,0},{2,3},{3,2},{4,5},{5,4},{6,7},{7,6},{8,9},{9,8},{10,11... | collective-permute-start | bytes 786440 | tf_op jit(solution)/shard_map/ppermute | solution.py:595
  (3 other events, 10.5 us)
